TPU v7x, 256 devices: a whole 4x4x8 slice. The times are simulated.
256 devices in a mesh: gx: 16 (over z, y_lo), gy: 16 (over x, y_hi, core).
Axes of the slice: x: 4, y: 4 (y_hi: 2, y_lo: 2; y = y_hi * 2 + y_lo), z: 8, core: 2. Of those that a mesh axis runs over, the one named last changes fastest.
Arguments:
- preserved_vector: float32 [14, 128, 128, 128], P(None, 'gx', 'gy'), may hold values from -200 to 200, as said below
- nasa_table: float32 [32, 6], replicated, may hold values from -4 to 4.5, as said below
- gas_constant: float32 [32], replicated, may hold values from 0.3 to 3
- species_index: int32 [9], replicated, may hold values from 0 to 31, as said below
- face_kind: int32 [16, 16, 2], P('gx', 'gy'), may hold values from 0 to 1
Outputs:
- increment: float32 [14, 128, 128, 128], P(None, 'gx', 'gy')
Inputs may be any that keep to these rules, and one draw needn't show every extreme that they name: `preserved_vector`: every cell is a physical state: positive partial densities and an energy whose temperature lies between 0.5 and 2.5. `nasa_table`: each row's cp over R polynomial exceeds 1.5 for temperatures 0.3 to 3. `species_index`: 9 distinct rows.
All inputs are finite; a program needn't handle non-finite values.
Results may differ from a plain program's by a relative error of at most 0.0003.
Values sent between devices are 32-bit elements; how exact they have to be, the bound alone decides.
No kernel may reach another device: no remote copies, remote signals or barrier semaphores. Data moves between devices by JAX's collectives and lax.ppermute only.
A program may use at most 64 MiB of HBM per device.

v0:
```python
import jax
import jax.numpy as jnp
from jax import lax
from jax.sharding import Mesh
from jax.sharding import PartitionSpec as P

NS = 9
NVAR = 14
NEWTON = 2
GX_GY = ("gx_0", "gx_1", "gy_0", "gy_1", "gy_2")
GX = ("gx_0", "gx_1")
GY = ("gy_0", "gy_1", "gy_2")


EPSILON = 1e-06
COURANT = 0.8


def by_axis(shard, axes):
    for axis in axes:
        shard = lax.pmax(shard, axis)
    return shard


def padded_2(shard, sides, width):
    edges = {}
    for axis, dim in sides:
        size, length = (lax.axis_size(axis), shard.shape[dim])
        up = [(i, (i + 1) % size) for i in range(size)]
        last = lax.slice_in_dim(shard, length - width, length, axis=dim)
        leading = lax.slice_in_dim(shard, 0, width, axis=dim)
        edges[dim] = (
            lax.ppermute(last, axis, up),
            lax.ppermute(leading, axis, [(b, a) for a, b in up]),
        )
    done = []
    for _, dim in sides:
        low, high = edges[dim]
        around = [(width, width) if d in done else (0, 0) for d in range(shard.ndim)]
        shard = jnp.concatenate([jnp.pad(low, around), shard, jnp.pad(high, around)], axis=dim)
        done.append(dim)
    return shard


def column(vector, trailing_sizes):
    return vector.reshape((vector.shape[0],) + (1,) * trailing_sizes)


def caloric_fitted_curves_table(nasa_table_weights, kelvin_reading):
    trailing_sizes = kelvin_reading.ndim
    columns = [column(nasa_table_weights[:, degree], trailing_sizes) for degree in range(6)]
    replicated_layer = kelvin_reading[None]
    caloric_quotient = columns[0] + replicated_layer * (
        columns[1]
        + replicated_layer
        * (columns[2] + replicated_layer * (columns[3] + replicated_layer * columns[4]))
    )
    chemical_heat_content = columns[5] + replicated_layer * (
        columns[0]
        + replicated_layer
        * (
            columns[1] / 2.0
            + replicated_layer
            * (
                columns[2] / 3.0
                + replicated_layer * (columns[3] / 4.0 + replicated_layer * columns[4] / 5.0)
            )
        )
    )
    return (caloric_quotient, chemical_heat_content)


def solve_for_kelvin(preserved_vector_lines, nasa_table_weights, component_kind_r_factor):
    prefix_addition_result = preserved_vector_lines[:NS]
    bulk_compactness = jnp.sum(prefix_addition_result, axis=0)
    momentum = preserved_vector_lines[NS : NS + 3]
    caloric_content_inner = (
        preserved_vector_lines[NS + 3]
        - 0.5 * jnp.sum(momentum * momentum, axis=0) / bulk_compactness
    )
    blend_stack_lane = column(component_kind_r_factor, bulk_compactness.ndim)
    kelvin_reading = jnp.ones_like(bulk_compactness)
    for iteration in range(NEWTON):
        caloric_quotient, chemical_heat_content = caloric_fitted_curves_table(
            nasa_table_weights, kelvin_reading
        )
        solver_misfit = (
            jnp.sum(
                prefix_addition_result
                * blend_stack_lane
                * (chemical_heat_content - kelvin_reading[None]),
                axis=0,
            )
            - caloric_content_inner
        )
        tangent_steepness_fn = jnp.sum(
            prefix_addition_result * blend_stack_lane * (caloric_quotient - 1.0), axis=0
        )
        kelvin_reading = kelvin_reading - solver_misfit / tangent_steepness_fn
    return kelvin_reading


def nasa_fitted_monomials(
    preserved_vector_lines, kelvin_reading, nasa_table_weights, component_kind_r_factor
):
    prefix_addition_result = preserved_vector_lines[:NS]
    bulk_compactness = jnp.sum(prefix_addition_result, axis=0)
    momentum = preserved_vector_lines[NS : NS + 3]
    doubled_norm_motion = jnp.sum(momentum * momentum, axis=0) / (
        bulk_compactness * bulk_compactness
    )
    blend_stack_lane = column(component_kind_r_factor, bulk_compactness.ndim)
    caloric_quotient, chemical_heat_content = caloric_fitted_curves_table(
        nasa_table_weights, kelvin_reading
    )
    caloric_tiers = blend_stack_lane * (chemical_heat_content - kelvin_reading[None])
    averaged_mixing_law_r = jnp.sum(prefix_addition_result * blend_stack_lane, axis=0)
    thrust_load_quiet = averaged_mixing_law_r * kelvin_reading
    heat_quotient_decrement = averaged_mixing_law_r / jnp.sum(
        prefix_addition_result * blend_stack_lane * (caloric_quotient - 1.0), axis=0
    )
    sound_speed = jnp.sqrt((1.0 + heat_quotient_decrement) * thrust_load_quiet / bulk_compactness)
    force_spatial_jump = (
        blend_stack_lane * kelvin_reading[None]
        - heat_quotient_decrement[None] * caloric_tiers
        + 0.5 * heat_quotient_decrement[None] * doubled_norm_motion[None]
    )
    return jnp.concatenate(
        [
            thrust_load_quiet[None],
            heat_quotient_decrement[None],
            sound_speed[None],
            force_spatial_jump,
        ],
        axis=0,
    )


def reconstruct(values):
    value_zero, value_one, value_two, value_three, value_four = values
    candidate_zero = (2.0 * value_zero - 7.0 * value_one + 11.0 * value_two) / 6.0
    candidate_one = (-value_one + 5.0 * value_two + 2.0 * value_three) / 6.0
    candidate_two = (2.0 * value_two + 5.0 * value_three - value_four) / 6.0
    curve_zero = value_zero - 2.0 * value_one + value_two
    slope_zero = value_zero - 4.0 * value_one + 3.0 * value_two
    curve_one = value_one - 2.0 * value_two + value_three
    slope_one = value_one - value_three
    curve_two = value_two - 2.0 * value_three + value_four
    slope_two = 3.0 * value_two - 4.0 * value_three + value_four
    smooth_zero = 13.0 / 12.0 * curve_zero * curve_zero + 0.25 * slope_zero * slope_zero
    smooth_one = 13.0 / 12.0 * curve_one * curve_one + 0.25 * slope_one * slope_one
    smooth_two = 13.0 / 12.0 * curve_two * curve_two + 0.25 * slope_two * slope_two
    weight_zero = 0.1 / ((EPSILON + smooth_zero) * (EPSILON + smooth_zero))
    weight_one = 0.6 / ((EPSILON + smooth_one) * (EPSILON + smooth_one))
    weight_two = 0.3 / ((EPSILON + smooth_two) * (EPSILON + smooth_two))
    return (
        weight_zero * candidate_zero + weight_one * candidate_one + weight_two * candidate_two
    ) / (weight_zero + weight_one + weight_two)


def window(array, offset, count, array_axis):
    return lax.slice_in_dim(array, offset, offset + count, axis=array_axis)


def direction_rate(preserved_vector_lines, cell_coef, array_axis, normal, speed):
    cells = preserved_vector_lines.shape[array_axis] - 6
    faces = cells + 1
    bulk_compactness = jnp.sum(preserved_vector_lines[:NS], axis=0)
    fractions = preserved_vector_lines[:NS] / bulk_compactness[None]
    velocity = preserved_vector_lines[NS : NS + 3] / bulk_compactness[None]
    passive = preserved_vector_lines[NS + 4 : NS + 5] / bulk_compactness[None]
    thrust_load_quiet = cell_coef[0]
    normal_speed = velocity[normal]
    carried = preserved_vector_lines * normal_speed[None]
    flux_rows = [carried[:NS]]
    for component in range(3):
        if component == normal:
            flux_rows.append((carried[NS + component] + thrust_load_quiet)[None])
        else:
            flux_rows.append(carried[NS + component][None])
    flux_rows.append((carried[NS + 3] + thrust_load_quiet * normal_speed)[None])
    flux_rows.append(carried[NS + 4][None])
    physical = jnp.concatenate(flux_rows, axis=0)
    upwind = 0.5 * (physical + speed * preserved_vector_lines)
    downwind = 0.5 * (physical - speed * preserved_vector_lines)

    def average(array):
        return 0.5 * (window(array, 2, faces, array_axis) + window(array, 3, faces, array_axis))

    mean_frac = average(fractions)
    mean_vel = average(velocity)
    mean_passive = average(passive)[0]
    mean_gamma = average(cell_coef[1:2])[0]
    mean_sound = average(cell_coef[2:3])[0]
    mean_slopes = average(cell_coef[3:])
    mean_square = jnp.sum(mean_vel * mean_vel, axis=0)
    mean_enthalpy = (
        mean_sound * mean_sound - jnp.sum(mean_frac * mean_slopes, axis=0)
    ) / mean_gamma + mean_square
    inverse = 1.0 / (mean_sound * mean_sound)
    tangents = [component for component in range(3) if component != normal]

    def project(vector):
        total = jnp.sum(vector[:NS], axis=0)
        pressure_jump = (
            jnp.sum(mean_slopes * vector[:NS], axis=0)
            - mean_gamma * jnp.sum(mean_vel * vector[NS : NS + 3], axis=0)
            + mean_gamma * vector[NS + 3]
        )
        normal_jump = vector[NS + normal] - mean_vel[normal] * total
        scaled = pressure_jump * inverse
        slower = 0.5 * (pressure_jump - mean_sound * normal_jump) * inverse
        faster = 0.5 * (pressure_jump + mean_sound * normal_jump) * inverse
        species = vector[:NS] - mean_frac * scaled[None]
        first_shear = vector[NS + tangents[0]] - mean_vel[tangents[0]] * total
        second_shear = vector[NS + tangents[1]] - mean_vel[tangents[1]] * total
        scalar_wave = vector[NS + 4] - mean_passive * scaled
        return jnp.concatenate(
            [
                slower[None],
                species,
                first_shear[None],
                second_shear[None],
                faster[None],
                scalar_wave[None],
            ],
            axis=0,
        )

    rising = reconstruct(
        [project(window(upwind, offset, faces, array_axis)) for offset in (0, 1, 2, 3, 4)]
    )
    falling = reconstruct(
        [project(window(downwind, offset, faces, array_axis)) for offset in (5, 4, 3, 2, 1)]
    )
    amplitude = rising + falling
    slower = amplitude[0]
    species = amplitude[1 : NS + 1]
    first_shear = amplitude[NS + 1]
    second_shear = amplitude[NS + 2]
    faster = amplitude[NS + 3]
    scalar_wave = amplitude[NS + 4]
    species_total = jnp.sum(species, axis=0)
    acoustic = slower + faster
    normal_vel = mean_vel[normal]
    momentum_rows = []
    for component in range(3):
        if component == normal:
            momentum_rows.append(
                (normal_vel - mean_sound) * slower
                + (normal_vel + mean_sound) * faster
                + normal_vel * species_total
            )
        elif component == tangents[0]:
            momentum_rows.append(mean_vel[component] * (acoustic + species_total) + first_shear)
        else:
            momentum_rows.append(mean_vel[component] * (acoustic + species_total) + second_shear)
    energy_row = (
        (mean_enthalpy - normal_vel * mean_sound) * slower
        + (mean_enthalpy + normal_vel * mean_sound) * faster
        + jnp.sum((mean_square[None] - mean_slopes / mean_gamma[None]) * species, axis=0)
        + mean_vel[tangents[0]] * first_shear
        + mean_vel[tangents[1]] * second_shear
    )
    face_flux = jnp.concatenate(
        [
            mean_frac * acoustic[None] + species,
            jnp.stack(momentum_rows, axis=0),
            energy_row[None],
            (mean_passive * acoustic + scalar_wave)[None],
        ],
        axis=0,
    )
    return window(face_flux, 0, cells, array_axis) - window(face_flux, 1, cells, array_axis)


def wall_pad(payload, lower_kind, upper_kind):
    rows_count = payload.shape[0]
    sign_flips = (
        jnp.where(jnp.arange(rows_count) == NS + 2, -1.0, 1.0)
        .astype(payload.dtype)
        .reshape((rows_count, 1, 1, 1))
    )
    lower_copy = jnp.concatenate([payload[..., :1]] * 3, axis=3)
    upper_copy = jnp.concatenate([payload[..., -1:]] * 3, axis=3)
    lower_mirror = payload[..., 2::-1] * sign_flips
    upper_mirror = payload[..., :-4:-1] * sign_flips
    lower_ghost = jnp.where(lower_kind == 1, lower_mirror, lower_copy)
    upper_ghost = jnp.where(upper_kind == 1, upper_mirror, upper_copy)
    return jnp.concatenate([lower_ghost, payload, upper_ghost], axis=3)


def fill_rims(padded):
    preserved_vector_lines = padded[:NVAR]
    return (preserved_vector_lines, padded[NVAR:])


def shards(preserved_vector, nasa_table, gas_constant, species_index, face_kind):
    selector = (
        species_index[:, None] == jnp.arange(nasa_table.shape[0], dtype=jnp.int32)[None, :]
    ).astype(jnp.float32)
    nasa_table_weights = jnp.dot(selector, nasa_table, precision=lax.Precision.HIGHEST)
    component_kind_r_factor = jnp.dot(
        selector, gas_constant[:, None], precision=lax.Precision.HIGHEST
    )[:, 0]
    kelvin_reading = solve_for_kelvin(preserved_vector, nasa_table_weights, component_kind_r_factor)
    self_coefficient = nasa_fitted_monomials(
        preserved_vector, kelvin_reading, nasa_table_weights, component_kind_r_factor
    )
    bulk_compactness = jnp.sum(preserved_vector[:NS], axis=0)
    velocity = preserved_vector[NS : NS + 3] / bulk_compactness[None]
    local_speed = jnp.max(jnp.abs(velocity) + self_coefficient[2][None], axis=(1, 2, 3))
    speeds = by_axis(local_speed, GX_GY)
    joined = jnp.concatenate([preserved_vector, self_coefficient], axis=0)
    padded_both = padded_2(joined, ((GX, 1), (GY, 2)), 3)
    padded_x = padded_both[:, :, 3:-3]
    padded_y = padded_both[:, 3:-3, :]
    padded_z = wall_pad(joined, face_kind[0, 0, 0], face_kind[0, 0, 1])
    rate = direction_rate(padded_z[:NVAR], padded_z[NVAR:], 3, 2, speeds[2])
    state_x, coef_x = fill_rims(padded_x)
    rate = rate + direction_rate(state_x, coef_x, 1, 0, speeds[0])
    state_y, coef_y = fill_rims(padded_y)
    rate = rate + direction_rate(state_y, coef_y, 2, 1, speeds[1])
    return COURANT / jnp.sum(speeds) * rate


def solution(mesh):
    finer = Mesh(mesh.devices.reshape(8, 2, 4, 2, 2), ("gx_0", "gx_1", "gy_0", "gy_1", "gy_2"))
    placed = (P(None, GX, GY, None), P(), P(), P(), P(GX, GY, None))
    return jax.shard_map(
        shards, mesh=finer, in_specs=placed, out_specs=P(None, GX, GY, None), check_vma=False
    )
```

profile of v0, /device:TPU:1, one launch (start us, length us, event | category | flops | bytes accessed | tf_op | source)
XLA Modules:
  0.0 112.2 jit_solution(6320281386992279448)
XLA Ops:
  0.0 0.7 copy-done
  0.7 0.8 fusion.279
  1.6 0.9 multiply_reduce_fusion.41
  2.5 1.1 constant_dynamic-update-slice_fusion.4
  3.5 0.9 convolution_bitcast_fusion
  4.4 1.1 multiply_reduce_fusion.37
  5.5 0.8 fusion.283
  7.2 0.9 fusion.365
  8.1 2.1 %collective-permute-start = (f32[26,3,8,128]{3,2,1,0:T(8,128)}, f32[26,3,8,128]{3,2,1,0:T(8,128)}, u32[]{:S(2)}, u32[]{:S(2)}) collective-permute-start(f32[26,3,8,128]{3,2,1,0:T(8,128)} %get-tuple-element.534), channel_id=1, source_target_pairs={{0,16},{16,32},{32,48},{48,64},{64,80},{80,96},{96,112},{112,128},... | collective-permute-start | bytes 958472 | tf_op jit(solution)/shard_map/ppermute | solution.py:33
  10.2 5.3 %collective-permute-start.1 = (f32[26,3,8,128]{3,2,1,0:T(8,128)}, f32[26,3,8,128]{3,2,1,0:T(8,128)}, u32[]{:S(2)}, u32[]{:S(2)}) collective-permute-start(f32[26,3,8,128]{3,2,1,0:T(8,128)} %get-tuple-element.535), channel_id=1, source_target_pairs={{16,0},{32,16},{48,32},{64,48},{80,64},{96,80},{112,96},{128,112},... | collective-permute-start | bytes 958472 | tf_op jit(solution)/shard_map/ppermute | solution.py:34
  15.8 0.8 copy.1153
  16.5 1.0 collective-permute-start.3
  17.5 0.8 copy.1152
  18.2 2.5 %collective-permute-start.2 = (f32[26,8,3,128]{3,1,2,0:T(8,128)}, f32[26,8,3,128]{3,1,2,0:T(8,128)}, u32[]{:S(2)}, u32[]{:S(2)}) collective-permute-start(f32[26,8,3,128]{3,1,2,0:T(8,128)} %copy.1152), channel_id=1, source_target_pairs={{0,1},{1,2},{2,3},{3,4},{4,5},{5,6},{6,7},{7,8},{8,9},{9,10},{10,1... | collective-permute-start | bytes 958472 | tf_op jit(solution)/shard_map/ppermute | solution.py:33
  20.7 1.2 %fusion.363 = (f32[26,8,8,1]{3,2,1,0:T(8,128)}, f32[26,8,8,1]{3,2,1,0:T(8,128)S(1)}) fusion(f32[26,8,8,128]{3,2,1,0:T(8,128)S(1)} %constant_dynamic-update-slice_fusion), kind=kLoop, calls=%fused_computation.1072 | loop fusion | bytes 26624 | tf_op jit(solution)/shard_map/slice | solution.py:284
  23.2 13.0 %pmax.35 = f32[3]{0:T(128)S(1)} all-reduce(f32[3]{0:T(128)S(1)} %add_reduce_fusion), channel_id=1, replica_groups=mesh['gx_0'=8,'gx_1'=2,'gy_0'=4,'gy_1'=2,'gy_2'=2] {'gx_0'}, use_global_device_ids=true, to_apply=%region_9.0 | all-reduce | flops 3 | bytes 24 | tf_op jit(solution)/shard_map/pmax | solution.py:21
  36.2 4.1 %pmax.36 = f32[3]{0:T(128)S(1)} all-reduce(f32[3]{0:T(128)S(1)} %pmax.35), channel_id=1, replica_groups=mesh['gx_0'=8,'gx_1'=2,'gy_0'=4,'gy_1'=2,'gy_2'=2] {'gx_1'}, use_global_device_ids=true, to_apply=%region_10.0 | all-reduce | flops 3 | bytes 24 | tf_op jit(solution)/shard_map/pmax | solution.py:21
  41.6 8.2 %pmax.37 = f32[3]{0:T(128)S(1)} all-reduce(f32[3]{0:T(128)S(1)} %pmax.36), channel_id=1, replica_groups=mesh['gx_0'=8,'gx_1'=2,'gy_0'=4,'gy_1'=2,'gy_2'=2] {'gy_0'}, use_global_device_ids=true, to_apply=%region_11.0 | all-reduce | flops 3 | bytes 24 | tf_op jit(solution)/shard_map/pmax | solution.py:21
  49.7 2.4 %copy.1156 = f32[26,8,8,1]{2,1,0,3:T(8,128)S(1)} copy(f32[26,8,8,1]{3,2,1,0:T(8,128)} %get-tuple-element.530) | data formatting | bytes 13312 | tf_op jit(solution)/shard_map/slice | solution.py:284
  52.2 1.9 %copy.1157 = f32[26,8,8,1]{2,1,0,3:T(8,128)} copy(f32[26,8,8,1]{3,2,1,0:T(8,128)S(1)} %get-tuple-element.531) | data formatting | bytes 13312 | tf_op jit(solution)/shard_map/slice | solution.py:285
  54.1 1.2 %rev.6 = f32[26,8,8,3]{3,2,1,0:T(8,128)} reverse(f32[26,8,8,3]{3,2,1,0:T(8,128)S(1)} %get-tuple-element.532), dimensions={3} | reverse | bytes 39936 | tf_op jit(solution)/shard_map/rev | solution.py:286
  55.3 1.2 %rev.7 = f32[26,8,8,3]{3,2,1,0:T(8,128)} reverse(f32[26,8,8,3]{3,2,1,0:T(8,128)S(1)} %get-tuple-element.533), dimensions={3} | reverse | bytes 39936 | tf_op jit(solution)/shard_map/rev | solution.py:287
  56.5 2.0 %multiply_select_fusion.1 = (f32[26,8,8,3]{3,2,1,0:T(8,128)S(1)}, f32[26,8,8,3]{3,2,1,0:T(8,128)S(1)}) fusion(f32[26,8,8,3]{3,2,1,0:T(8,128)} %rev.6, f32[26,8,8]{2,1,0:T(8,128)S(1)} %bitcast.929, f32[26]{0:T(128)S(1)} %compare_select_fusion, pred[]{:T(512)} %bitcast.19, f32[26,8,8]{2,1,0:T(8,128)S(1)} %bitcast.930, f32[26,8,8,3]{3,2,1,0:T(8,128)} %rev.7, ...), kind=kLoop, calls=%fused_computation.55 | loop fusion | flops 19968 | bytes 93290 | tf_op jit(solution)/shard_map/jit(_where)/select_n | solution.py:288
  58.5 0.7 pad_maximum_fusion.1
  59.3 1.1 %copy-done.2 = f32[26,8,8,134]{3,2,1,0:T(8,128)} copy-done((f32[26,8,8,134]{3,2,1,0:T(8,128)}, f32[26,8,8,134]{3,2,1,0:T(8,128)S(1)}, u32[]{:S(2)}) %copy-start.2) | copy-done | bytes 891928
  60.7 6.4 %pmax.38 = f32[3]{0:T(128)S(1)} all-reduce(f32[3]{0:T(128)S(1)} %pmax.37), channel_id=1, replica_groups=mesh['gx_0'=8,'gx_1'=2,'gy_0'=4,'gy_1'=2,'gy_2'=2] {'gy_1'}, use_global_device_ids=true, to_apply=%region_12.0 | all-reduce | flops 3 | bytes 24 | tf_op jit(solution)/shard_map/pmax | solution.py:21
  67.0 1.2 %slice_multiply_fusion.1 = f32[14,8,8,134]{3,2,1,0:T(8,128)S(1)} fusion(f32[26,8,8,134]{3,2,1,0:T(8,128)} %copy-done.2, f32[8,8,134]{2,1,0:T(8,128)S(1)} %slice_bitcast_fusion), kind=kLoop, calls=%fused_computation.53 | loop fusion | flops 120064 | bytes 994816 | tf_op jit(solution)/shard_map/mul | solution.py:174
  68.3 0.9 slice_add_fusion.9
  69.2 0.9 slice.1845
  70.2 8.4 %pmax.39 = f32[3]{0:T(128)S(1)} all-reduce(f32[3]{0:T(128)S(1)} %pmax.38), channel_id=1, replica_groups=mesh['gx_0'=8,'gx_1'=2,'gy_0'=4,'gy_1'=2,'gy_2'=2] {'gy_2'}, use_global_device_ids=true, to_apply=%region_13.0 | all-reduce | flops 3 | bytes 24 | tf_op jit(solution)/shard_map/pmax | solution.py:21
  78.6 0.7 fusion.367
  79.3 0.9 slice_add_fusion.8
  80.2 2.3 %subtract_multiply_fusion = (f32[14,8,8,134]{3,2,1,0:T(8,128)S(1)}, f32[14,8,8,134]{3,2,1,0:T(8,128)S(1)}) fusion(f32[26,8,8,134]{3,2,1,0:T(8,128)} %copy-done.2, f32[1,8,8,134]{3,2,1,0:T(8,128)S(1)} %copy-done.6, f32[1,8,8,134]{3,2,1,0:T(8,128)S(1)} %slice_add_fusion.8, f32[1,8,8,134]{3,2,1,0:T(8,128)S(1)} %get-tuple-element.266, ...), kind=kLoop, calls=%fused_computation.50 | loop fusion | flops 960512 | bytes 1921028 | tf_op jit(solution)/shard_map/mul | solution.py:185
  82.4 0.9 slice_reduce_fusion.11
  84.8 1.4 %subtract_dynamic-update-slice_fusion.8 = (f32[14,8,8,129]{3,2,1,0:T(8,128)S(1)}, f32[14,8,8,129]{3,2,1,0:T(8,128)S(1)}, f32[14,8,8,129]{3,2,1,0:T(8,128)S(1)}, ...) fusion(f32[14,8,8,129]{3,2,1,0:T(8,128)S(1)} %get-tuple-element, ...), kind=kLoop, calls=%fused_computation.112 | loop fusion | flops 1841088 | bytes 9830400
  86.7 0.8 subtract_dynamic-update-slice_fusion.4
  88.8 4.4 %divide_add_fusion = f32[14,8,8,129]{3,2,1,0:T(8,128)S(1)} fusion(f32[14,8,8,129]{3,2,1,0:T(8,128)S(1)} %get-tuple-element.404, f32[14,8,8,129]{3,2,1,0:T(8,128)S(1)} %get-tuple-element.402, f32[14,8,8,129]{3,2,1,0:T(8,128)S(1)} %get-tuple-element.403, f32[14,8,8,129]{3,2,1,0:T(8,128)S(1)} %get-tuple-element.405, ...), kind=kLoop, calls=%fused_computation.49 | loop fusion | flops 14910336 | bytes 5085696 | tf_op jit(solution)/shard_map/add | solution.py:236
  93.5 0.7 reduce_sum.1271
  95.0 1.2 %pad_maximum_fusion.2 = f32[26,14,8,128]{3,2,1,0:T(8,128)S(1)} fusion(f32[26,3,8,128]{3,2,1,0:T(8,128)} %collective-permute-done.1, f32[26,8,8,128]{3,2,1,0:T(8,128)S(1)} %constant_dynamic-update-slice_fusion, f32[26,3,8,128]{3,2,1,0:T(8,128)} %collective-permute-done), kind=kLoop, calls=%fused_computation.10 | loop fusion | flops 745472 | bytes 2981888 | tf_op jit(solution)/shard_map/concatenate | solution.py:40
  96.5 1.0 pad.8
  97.6 1.0 pad.7
  99.4 0.7 subtract_multiply_fusion.2
  100.2 1.0 slice_reduce_fusion.34
  101.2 0.7 multiply_bitcast_fusion.32
  103.1 2.3 %divide_add_fusion.2 = f32[14,9,8,128]{3,2,1,0:T(8,128)S(1)} fusion(f32[14,9,8,128]{3,2,1,0:T(8,128)S(1)} %get-tuple-element.518, f32[14,9,8,128]{3,2,1,0:T(8,128)S(1)} %get-tuple-element.516, f32[14,9,8,128]{3,2,1,0:T(8,128)S(1)} %get-tuple-element.517, f32[14,9,8,128]{3,2,1,0:T(8,128)S(1)} %get-tuple-element.519, ...), kind=kLoop, calls=%fused_computation.181 | loop fusion | flops 16644096 | bytes 5677056 | tf_op jit(solution)/shard_map/add | solution.py:236
  105.9 0.9 subtract_multiply_fusion.1
  108.4 2.3 %divide_add_fusion.1 = f32[14,8,9,128]{3,1,2,0:T(8,128)S(1)} fusion(f32[14,8,9,128]{3,1,2,0:T(8,128)S(1)} %get-tuple-element.495, f32[14,8,9,128]{3,1,2,0:T(8,128)S(1)} %get-tuple-element.493, f32[14,8,9,128]{3,1,2,0:T(8,128)S(1)} %get-tuple-element.494, f32[14,8,9,128]{3,1,2,0:T(8,128)S(1)} %get-tuple-element.496, ...), kind=kLoop, calls=%fused_computation.180 | loop fusion | flops 16644096 | bytes 5677056 | tf_op jit(solution)/shard_map/add | solution.py:236
  111.1 1.1 fusion.78
  (139 shorter events, 10.7 us)
Async XLA Ops:
  0.0 0.7 copy-start
  0.0 6.3 %copy-start.3 = (f32[14,8,8,128]{3,2,1,0:T(8,128)S(1)}, f32[14,8,8,128]{3,2,1,0:T(8,128)}, u32[]{:S(2)}) copy-start(f32[14,8,8,128]{3,2,1,0:T(8,128)} %param.5) | copy-start | bytes 1376260
  8.1 86.8 %collective-permute-start = (f32[26,3,8,128]{3,2,1,0:T(8,128)}, f32[26,3,8,128]{3,2,1,0:T(8,128)}, u32[]{:S(2)}, u32[]{:S(2)}) collective-permute-start(f32[26,3,8,128]{3,2,1,0:T(8,128)} %get-tuple-element.534), channel_id=1, source_target_pairs={{0,16},{16,32},{32,48},{48,64},{64,80},{80,96},{96,112},{112,128},... | collective-permute-start | bytes 958472 | tf_op jit(solution)/shard_map/ppermute | solution.py:33
  10.2 84.7 %collective-permute-start.1 = (f32[26,3,8,128]{3,2,1,0:T(8,128)}, f32[26,3,8,128]{3,2,1,0:T(8,128)}, u32[]{:S(2)}, u32[]{:S(2)}) collective-permute-start(f32[26,3,8,128]{3,2,1,0:T(8,128)} %get-tuple-element.535), channel_id=1, source_target_pairs={{16,0},{32,16},{48,32},{64,48},{80,64},{96,80},{112,96},{128,112},... | collective-permute-start | bytes 958472 | tf_op jit(solution)/shard_map/ppermute | solution.py:34
  16.5 80.0 %collective-permute-start.3 = (f32[26,8,3,128]{3,1,2,0:T(8,128)}, f32[26,8,3,128]{3,1,2,0:T(8,128)}, u32[]{:S(2)}, u32[]{:S(2)}) collective-permute-start(f32[26,8,3,128]{3,1,2,0:T(8,128)} %copy.1153), channel_id=1, source_target_pairs={{1,0},{2,1},{3,2},{4,3},{5,4},{6,5},{7,6},{8,7},{9,8},{10,9},{11,1... | collective-permute-start | bytes 958472 | tf_op jit(solution)/shard_map/ppermute | solution.py:34
  18.2 79.4 %collective-permute-start.2 = (f32[26,8,3,128]{3,1,2,0:T(8,128)}, f32[26,8,3,128]{3,1,2,0:T(8,128)}, u32[]{:S(2)}, u32[]{:S(2)}) collective-permute-start(f32[26,8,3,128]{3,1,2,0:T(8,128)} %copy.1152), channel_id=1, source_target_pairs={{0,1},{1,2},{2,3},{3,4},{4,5},{5,6},{6,7},{7,8},{8,9},{9,10},{10,1... | collective-permute-start | bytes 958472 | tf_op jit(solution)/shard_map/ppermute | solution.py:33
  21.9 0.7 copy-start.7
  54.1 2.4 %copy-start.5 = (f32[26,8,8,1]{2,1,0,3:T(8,128)S(1)}, f32[26,8,8,1]{2,1,0,3:T(8,128)}, u32[]{:S(2)}) copy-start(f32[26,8,8,1]{2,1,0,3:T(8,128)} %copy.1157) | copy-start | bytes 19972
  59.3 1.2 %copy-start.2 = (f32[26,8,8,134]{3,2,1,0:T(8,128)}, f32[26,8,8,134]{3,2,1,0:T(8,128)S(1)}, u32[]{:S(2)}) copy-start(f32[26,8,8,134]{3,2,1,0:T(8,128)S(1)} %pad_maximum_fusion.1) | copy-start | bytes 2675716
  68.3 1.0 copy-start.4
  69.2 10.9 %copy-start.6 = (f32[1,8,8,134]{3,2,1,0:T(8,128)S(1)}, f32[1,8,8,134]{3,2,1,0:T(8,128)}, u32[]{:S(2)}) copy-start(f32[1,8,8,134]{3,2,1,0:T(8,128)} %get-tuple-element.440) | copy-start | bytes 102916
  111.0 1.2 %copy-start.1 = (f32[32,6]{0,1:T(8,128)S(1)}, f32[32,6]{0,1:T(8,128)}, u32[]{:S(2)}) copy-start(f32[32,6]{0,1:T(8,128)} %param.6) | copy-start | bytes 2308
where the time goes:
time: 113 us; the launch traced here: 112 us
  blocking collectives  40 us (35%)
  other arithmetic  38 us (34%)
  local copies, waits for them, and re-layouts  18.9 us (17%)
  starting transfers between devices  10.9 us (10%)
  between operations  2.78 us (2%)
  matrix products  1.7 us (2%)
    pmax x5, blocking collectives, by_axis(): shard = lax.pmax(shard, axis)  40 us
    add x3, other arithmetic, direction_rate(): amplitude = rising + falling  9.05 us
    ppermute x2, starting transfers between devices, padded_2(): lax.ppermute(leading, axis, [(b, a) for a, b in up])  6.25 us
    unnamed x57, other arithmetic  5.95 us
    unnamed x23, local copies, waits for them, and re-layouts  4.78 us
    ppermute x2, starting transfers between devices, padded_2(): lax.ppermute(last, axis, up)  4.62 us
    mul x3, other arithmetic, direction_rate(): downwind = 0.5 * (physical - speed * preserved_vector_lines)  3.84 us
    slice x2, local copies, waits for them, and re-layouts, wall_pad(): lower_copy = jnp.concatenate([payload[..., :1]] * 3, axis=3)  3.61 us
  transfers between devices with their start and end apart: 4, of which 0 were waited for; matrix products, arithmetic and copies ran while one was open for 31% of the time, Pallas kernels for 0%

commit v1 on v0

v1 whole, which is shorter than its diff:
```python
import jax
import jax.numpy as jnp
from jax import lax
from jax.experimental import pallas as pl
from jax.experimental.pallas import tpu as pltpu
from jax.sharding import Mesh
from jax.sharding import PartitionSpec as P

NS = 9
NVAR = 14
NEWTON = 2
EPSILON = 1e-06
COURANT = 0.8
LANES = 128
DF, DU, FM, HU, RD, ROWS = 0, 70, 140, 154, 168, 192
F32 = jnp.float32


def species_scalars(table, gas, index):
    rows = []
    for i in range(NS):
        row = index[i]
        r = gas[row]
        a = [r * table[row, k] for k in range(6)]
        e = [a[0] - r, a[1] * 0.5, a[2] * (1.0 / 3.0), a[3] * 0.25, a[4] * 0.2, a[5]]
        rows.append((r, a, e))
    return rows


def coefficients(u, rows):
    rho = u[0]
    for i in range(1, NS):
        rho = rho + u[i]
    inv = 1.0 / rho
    vel = [u[NS + j] * inv for j in range(3)]
    square = vel[0] * vel[0] + vel[1] * vel[1] + vel[2] * vel[2]
    target = u[NS + 3] - 0.5 * rho * square
    mix = [None] * 7
    for i in range(NS):
        r, a, _ = rows[i]
        for k, w in enumerate([r] + a):
            term = u[i] * w
            mix[k] = term if mix[k] is None else mix[k] + term
    r0, a1, a2, a3, a4, a5, a6 = mix
    b1, b2, b3, b4, b5 = a1 - r0, a2 * 0.5, a3 * (1.0 / 3.0), a4 * 0.25, a5 * 0.2
    temp = jnp.ones_like(rho)
    for _ in range(NEWTON):
        energy = a6 + temp * (b1 + temp * (b2 + temp * (b3 + temp * (b4 + temp * b5))))
        slope = b1 + temp * (a2 + temp * (a3 + temp * (a4 + temp * a5)))
        temp = temp - (energy - target) / slope
    slope = b1 + temp * (a2 + temp * (a3 + temp * (a4 + temp * a5)))
    g = r0 / slope
    p = r0 * temp
    c = jnp.sqrt((1.0 + g) * p * inv)
    kinetic = 0.5 * g * square
    phi = []
    for i in range(NS):
        r, _, e = rows[i]
        energy = e[5] + temp * (e[0] + temp * (e[1] + temp * (e[2] + temp * (e[3] + temp * e[4]))))
        phi.append(r * temp - g * energy + kinetic)
    return p, g, c, phi, vel


def cell_kernel(table, gas, index, u_ref, coef_ref, alpha_ref, xs_ref, xe_ref, ys_ref, ye_ref):
    rows = species_scalars(table, gas, index)
    fastest = [None] * 3

    def body(i, fastest):
        at = pl.ds(pl.multiple_of(i * 8, 8), 8)
        u = [u_ref[k, at, :] for k in range(NVAR)]
        p, g, c, phi, vel = coefficients(u, rows)
        for k, value in enumerate([p, g, c] + phi):
            coef_ref[k, at, :] = value
        return tuple(jnp.maximum(f, jnp.abs(v) + c) for f, v in zip(fastest, vel))

    zero = jnp.zeros((8, LANES), F32)
    fastest = lax.fori_loop(0, 8, body, (zero, zero, zero))
    sub = lax.broadcasted_iota(jnp.int32, (8, LANES), 0)
    out = zero
    for d in range(3):
        top = jnp.max(jnp.max(fastest[d], axis=0, keepdims=True), axis=1, keepdims=True)
        out = jnp.where(sub == d, jnp.broadcast_to(top, (8, LANES)), out)
    alpha_ref[...] = out
    for k in range(NVAR):
        xs_ref[k] = u_ref[k, 0:24, :]
        xe_ref[k] = u_ref[k, 40:64, :]
        for j in range(3):
            ys_ref[k, 8 * j:8 * j + 8, :] = u_ref[k, pl.ds(j, 8, stride=8), :]
            ye_ref[k, 8 * j:8 * j + 8, :] = u_ref[k, pl.ds(5 + j, 8, stride=8), :]


def cell_fields(u, coef, order):
    p, g, c, phi = coef[0], coef[1], coef[2], coef[3:]
    rho = u[0]
    for i in range(1, NS):
        rho = rho + u[i]
    inv = 1.0 / rho
    n = order[0]
    vel = [u[NS + j] * inv for j in order]
    half = [0.5 * x for x in u[:NS]] + [0.5 * u[NS + j] for j in order]
    half += [0.5 * u[NS + 3], 0.5 * u[NS + 4], 0.5 * rho]
    un = vel[0]
    flux = [x * un for x in half]
    ph = 0.5 * p
    flux[NS] = flux[NS] + ph
    flux[NS + 3] = flux[NS + 3] + ph * un
    mean = [x * inv for x in u[:NS]] + vel + [u[NS + 4] * inv, g, c] + phi
    return half, flux, mean


def face_record(out_ref, f, left, right, jumps, fm, hu):
    mean = [0.5 * (a + b) for a, b in zip(left, right)]
    y, vel, z, g, c, phi = mean[:9], mean[9:12], mean[12], mean[13], mean[14], mean[15:]
    square = vel[0] * vel[0] + vel[1] * vel[1] + vel[2] * vel[2]
    dot = y[0] * phi[0]
    for i in range(1, NS):
        dot = dot + y[i] * phi[i]
    ig = 1.0 / g
    ic = 1.0 / c
    inv = ic * ic
    h = (c * c - dot) * ig + square
    ihc = 0.5 * ic
    gs = g * inv
    phis = [x * inv for x in phi]
    gu = [gs * v for v in vel]
    record = y + vel + [z, c, h] + [square - x * ig for x in phi]
    for k, value in enumerate(record):
        out_ref[f, RD + k] = value
    for k in range(NVAR):
        out_ref[f, FM + k] = fm[k]
        out_ref[f, HU + k] = hu[k]
    for base, i, v in jumps():
        dp = phis[0] * v[0]
        for k in range(1, NS):
            dp = dp + phis[k] * v[k]
        dp = dp + gs * v[12] - (gu[0] * v[9] + gu[1] * v[10] + gu[2] * v[11])
        s = v[14]
        a = 0.5 * dp
        b = (v[9] - vel[0] * s) * ihc
        wave = [a - b] + [v[k] - y[k] * dp for k in range(NS)]
        wave += [v[10] - vel[1] * s, v[11] - vel[2] * s, a + b, v[13] - z * dp]
        for k in range(NVAR):
            out_ref[f, base + 14 * i + k] = wave[k]


def line_kernel(order, strided, table, gas, index, u_ref, coef_ref, low_ref, high_ref, out_ref,
                state, flux, mean):
    rows = species_scalars(table, gas, index)

    def put(plane, u, coef):
        a, b, m = cell_fields(u, coef, order)
        for k in range(15):
            state[plane, k] = a[k]
            flux[plane, k] = b[k]
        for k in range(24):
            mean[plane, k] = m[k]

    def own(i, _):
        at = pl.ds(i, 8, stride=8) if strided else pl.ds(pl.multiple_of(i * 8, 8), 8)
        put(i + 3, [u_ref[k, at, :] for k in range(NVAR)], [coef_ref[k, at, :] for k in range(12)])
        return 0

    lax.fori_loop(0, 8, own, 0)
    for ref, first in ((low_ref, 0), (high_ref, 11)):
        def halo(i, _, ref=ref, first=first):
            at = pl.ds(pl.multiple_of(i * 8, 8), 8)
            u = [ref[k, at, :] for k in range(NVAR)]
            p, g, c, phi, _ = coefficients(u, rows)
            put(i + first, u, [p, g, c] + phi)
            return 0
        lax.fori_loop(0, 3, halo, 0)

    def face(f, _):
        left = [mean[f + 2, k] for k in range(24)]
        right = [mean[f + 3, k] for k in range(24)]
        fm = [flux[f + 2, k] + flux[f + 3, k] for k in range(NVAR)]
        hu = [state[f + 3, k] - state[f + 2, k] for k in range(NVAR)]

        def jumps():
            for base, ref in ((DF, flux), (DU, state)):
                for i in range(5):
                    yield base, i, [ref[f + i + 1, k] - ref[f + i, k] for k in range(15)]

        face_record(out_ref, f, left, right, jumps, fm, hu)
        return 0

    lax.fori_loop(0, 9, face, 0)


def column_kernel(table, gas, index, kind, u_ref, coef_ref, out_ref, ends, state, flux):
    rows = species_scalars(table, gas, index)
    order = (2, 0, 1)
    lane = lax.broadcasted_iota(jnp.int32, (8, LANES), 1)
    slot = lane % 16
    group = lane // 16
    low_wall = kind[0, 0, 0] == 1
    high_wall = kind[0, 0, 1] == 1

    def pick(k, _):
        packed = jnp.zeros((8, LANES), F32)
        for plane in range(8):
            v = u_ref[k, 8 * plane:8 * plane + 8, :]
            low = pltpu.roll(v, (16 * plane + 3) % LANES, 1)
            high = pltpu.roll(v, (16 * plane + 8 - 123) % LANES, 1)
            packed = jnp.where(group == plane, jnp.where(slot < 8, low, high), packed)

        def at(shift):
            return pltpu.roll(packed, shift % LANES, 1)

        sign = jnp.where(k == NS + 2, -1.0, 1.0)
        mirror = jnp.where(slot == 2, at(-1), jnp.where(slot == 1, at(-3), at(-5))) * sign
        copy = jnp.where(slot == 2, at(-1), jnp.where(slot == 1, at(-2), at(-3)))
        low = jnp.where(low_wall, mirror, copy)
        mirror = jnp.where(slot == 13, at(1), jnp.where(slot == 14, at(3), at(5))) * sign
        copy = jnp.where(slot == 13, at(1), jnp.where(slot == 14, at(2), at(3)))
        high = jnp.where(high_wall, mirror, copy)
        ends[k] = jnp.where(slot < 3, low, jnp.where(slot > 12, high, packed))
        return 0

    lax.fori_loop(0, NVAR, pick, 0)

    def record(f, u, coef):
        half, fl, mean = cell_fields(u, coef, order)
        prev = [pltpu.roll(x, 1, 1) for x in mean]
        hl = [pltpu.roll(x, 1, 1) for x in half]
        fll = [pltpu.roll(x, 1, 1) for x in fl]
        for k in range(15):
            state[k] = half[k] - hl[k]
            flux[k] = fl[k] - fll[k]
        fm = [fl[k] + fll[k] for k in range(NVAR)]
        hu = [half[k] - hl[k] for k in range(NVAR)]

        def jumps():
            for base, ref in ((DF, flux), (DU, state)):
                for i in range(5):
                    vs = [ref[k] for k in range(15)]
                    if i != 2:
                        vs = [pltpu.roll(v, (2 - i) % LANES, 1) for v in vs]
                    yield base, i, vs

        face_record(out_ref, f, prev, mean, jumps, fm, hu)

    u = [ends[k] for k in range(NVAR)]
    p, g, c, phi, _ = coefficients(u, rows)
    record(8, u, [p, g, c] + phi)

    def plane(i, _):
        at = pl.ds(pl.multiple_of(i * 8, 8), 8)
        record(i, [u_ref[k, at, :] for k in range(NVAR)], [coef_ref[k, at, :] for k in range(12)])
        return 0

    lax.fori_loop(0, 8, plane, 0)


def correction(d0, d1, d2, d3):
    t0 = d0 - 1.375 * d1
    t1 = d1 - 0.625 * d2
    t2 = d3 - 1.375 * d2
    e1 = (0.609375 * d1) * d1 + 0.75 * EPSILON
    e2 = (0.609375 * d2) * d2 + 0.75 * EPSILON
    i0 = reciprocal(t0 * t0 + e1)
    i1 = reciprocal(t1 * t1 + e2)
    i2 = reciprocal(t2 * t2 + e2)
    w0 = i0 * i0
    w1 = 6.0 * (i1 * i1)
    w2 = 3.0 * (i2 * i2)
    q = 2.625 * d2
    lead = (2.25 * d1 - q) - (t0 + t0)
    return q + (w0 * lead + w1 * t1 - w2 * t2) * reciprocal(w0 + w1 + w2)


def reciprocal(x):
    return 1.0 / x


def rate_kernel(alpha_ref, x_ref, y_ref, z_ref, out_ref, fx, fy, fz):
    speeds = [alpha_ref[d:d + 1, :] for d in range(3)]
    scale = COURANT / (speeds[0] + speeds[1] + speeds[2])
    scale = jnp.broadcast_to(scale, (8, LANES))
    for ref, flux, d in ((x_ref, fx, 0), (y_ref, fy, 1), (z_ref, fz, 2)):
        speed = jnp.broadcast_to(speeds[d], (8, LANES))

        def face(f, _, ref=ref, flux=flux, speed=speed):
            def wave(k):
                a = [ref[f, DF + 14 * i + k] for i in range(5)]
                b = [ref[f, DU + 14 * i + k] * speed for i in range(5)]
                up = [a[i] + b[i] for i in range(4)]
                down = [a[i] - b[i] for i in range(1, 5)]
                return correction(*up) - correction(down[3], down[2], down[1], down[0])

            amp = [wave(k) for k in range(NVAR)]
            y = [ref[f, RD + k] for k in range(9)]
            un, ut, us, z, c, h = [ref[f, RD + 9 + k] for k in range(6)]
            slower, species, first, second, faster, scalar = (
                amp[0], amp[1:10], amp[10], amp[11], amp[12], amp[13])
            total = species[0]
            for k in range(1, NS):
                total = total + species[k]
            acoustic = slower + faster
            swing = (faster - slower) * c
            both = acoustic + total
            energy = h * acoustic + un * swing + ut * first + us * second
            for k in range(NS):
                energy = energy + ref[f, RD + 15 + k] * species[k]
            rows = [y[k] * acoustic + species[k] for k in range(NS)]
            rows += [un * both + swing, ut * both + first, us * both + second, energy,
                     z * acoustic + scalar]
            for k in range(NVAR):
                flux[f, k] = (rows[k] * (1.0 / 6.0) + (ref[f, FM + k] - ref[f, HU + k] * speed)) * scale
            return 0

        lax.fori_loop(0, 9, face, 0)

    row_x = list(range(NVAR))
    lane = lax.broadcasted_iota(jnp.int32, (8, LANES), 1)
    at_z = {9: 10, 10: 11, 11: 9}
    at_y = {9: 10, 10: 9, 11: 11}

    def plane(i, _):
        at = pl.ds(pl.multiple_of(i * 8, 8), 8)
        to_low = lax.rem(2 * LANES - 3 - 16 * i, LANES)
        to_high = lax.rem(2 * LANES - 13 - 16 * i, LANES)
        for k in range(NVAR):
            kz = at_z.get(k, k)
            ends = fz[8, kz]
            low = pltpu.roll(ends, to_low, 1)
            high = pltpu.roll(ends, to_high, 1)
            face = jnp.where(lane < 3, low, jnp.where(lane >= 126, high, fz[i, kz]))
            after = pltpu.roll(jnp.where(lane == 0, high, face), LANES - 1, 1)
            out_ref[k, at, :] = (face - after) + (fx[i, k] - fx[i + 1, k])
        return 0

    lax.fori_loop(0, 8, plane, 0)

    def row(j, _):
        at = pl.ds(j, 8, stride=8)
        for k in range(NVAR):
            ky = at_y.get(k, k)
            out_ref[k, at, :] = out_ref[k, at, :] + (fy[j, ky] - fy[j + 1, ky])
        return 0

    lax.fori_loop(0, 8, row, 0)


SMEM = pl.BlockSpec(memory_space=pltpu.SMEM)
VMEM = pl.BlockSpec(memory_space=pltpu.VMEM)
PLANES = (8, LANES)


def struct(*shape):
    return jax.ShapeDtypeStruct(shape, F32)


def params():
    return pltpu.CompilerParams(vmem_limit_bytes=48 << 20)


def cells(u, table, gas, index):
    halo = struct(NVAR, 24, LANES)
    return pl.pallas_call(
        cell_kernel, name="cells", in_specs=[SMEM] * 3 + [VMEM], out_specs=[VMEM] * 6,
        out_shape=[struct(12, 64, LANES), struct(8, LANES), halo, halo, halo, halo],
        compiler_params=params())(table, gas, index, u)


def lines(name, order, strided, table, gas, index, u, coef, low, high):
    def body(*refs):
        line_kernel(order, strided, *refs)
    return pl.pallas_call(
        body, name=name, in_specs=[SMEM] * 3 + [VMEM] * 4, out_specs=VMEM,
        out_shape=struct(9, ROWS, 8, LANES),
        scratch_shapes=[pltpu.VMEM((14, 15) + PLANES, F32), pltpu.VMEM((14, 15) + PLANES, F32),
                        pltpu.VMEM((14, 24) + PLANES, F32)],
        compiler_params=params())(table, gas, index, u, coef, low, high)


def columns(table, gas, index, kind, u, coef):
    return pl.pallas_call(
        column_kernel, name="columns", in_specs=[SMEM] * 4 + [VMEM] * 2, out_specs=VMEM,
        out_shape=struct(9, ROWS, 8, LANES),
        scratch_shapes=[pltpu.VMEM((14,) + PLANES, F32), pltpu.VMEM((15,) + PLANES, F32),
                        pltpu.VMEM((15,) + PLANES, F32)],
        compiler_params=params())(table, gas, index, kind, u, coef)


def rates(alpha, x, y, z):
    return pl.pallas_call(
        rate_kernel, name="rates", in_specs=[VMEM] * 4, out_specs=VMEM,
        out_shape=struct(NVAR, 64, LANES),
        scratch_shapes=[pltpu.VMEM((9, NVAR) + PLANES, F32)] * 3,
        compiler_params=params())(alpha, x, y, z)


AXES = ("z", "yl", "x", "yh", "c")
GX = ("z", "yl")
GY = ("x", "yh", "c")


def shards(preserved_vector, nasa_table, gas_constant, species_index, face_kind):
    u = preserved_vector.reshape(NVAR, 64, LANES)
    coef, alpha, xs, xe, ys, ye = cells(u, nasa_table, gas_constant, species_index)
    up = [(i, (i + 1) % 16) for i in range(16)]
    down = [(b, a) for a, b in up]
    for axis in reversed(AXES):
        size = lax.axis_size(axis)
        step = 1
        while step < size:
            alpha = jnp.maximum(alpha, lax.ppermute(alpha, axis, [(i, i ^ step) for i in range(size)]))
            step *= 2
    x_low, x_high = lax.ppermute(xe, GX, up), lax.ppermute(xs, GX, down)
    y_low, y_high = lax.ppermute(ye, GY, up), lax.ppermute(ys, GY, down)
    fixed = (nasa_table, gas_constant, species_index)
    z = columns(*fixed, face_kind, u, coef)
    x = lines("x_lines", (0, 1, 2), False, *fixed, u, coef, x_low, x_high)
    y = lines("y_lines", (1, 0, 2), True, *fixed, u, coef, y_low, y_high)
    return rates(alpha, x, y, z).reshape(preserved_vector.shape)


def solution(mesh):
    finer = Mesh(mesh.devices.reshape(8, 2, 4, 2, 2), AXES)
    placed = (P(None, GX, GY, None), P(), P(), P(), P(GX, GY, None))
    return jax.shard_map(
        shards, mesh=finer, in_specs=placed, out_specs=P(None, GX, GY, None), check_vma=False
    )
```

time: 113 us -> 86.9 us (0.77)
  the two profiles are of different devices: /device:TPU:1 before, /device:TPU:8 now
where the time goes in v1:
time: 86.9 us; the launch traced here: 86.7 us
  Pallas kernels  37.5 us (43%)
  waiting for transfers between devices  23.5 us (27%)
  starting transfers between devices  22 us (25%)
  local copies, waits for them, and re-layouts  3.75 us (4%)
    ppermute x8, waiting for transfers between devices, shards(): lax.ppermute(alpha, axis, [(i, i ^ step) for i in range(size)])  23.5 us
    pallas_call x1, Pallas kernels, rates(): pl.pallas_call(rate_kernel, name='rates', in_specs=[VMEM] * 4, out_specs=...  15 us
    ppermute x8, starting transfers between devices, shards(): lax.ppermute(alpha, axis, [(i, i ^ step) for i in range(size)])  14.4 us
    pallas_call x2, Pallas kernels, lines(): pl.pallas_call(body, name=name, in_specs=[SMEM] * 3 + [VMEM] * 4, out_spe...  11.8 us
    pallas_call x1, Pallas kernels, columns(): pl.pallas_call(column_kernel, name='columns', in_specs=[SMEM] * 4 + [VMEM...  8.96 us
    ppermute x2, starting transfers between devices, shards(): y_low, y_high = (lax.ppermute(ye, GY, up), lax.ppermute(ys, GY, down))  5.43 us
    unnamed x9, local copies, waits for them, and re-layouts  3.75 us
    ppermute x2, starting transfers between devices, shards(): x_low, x_high = (lax.ppermute(xe, GX, up), lax.ppermute(xs, GX, down))  2.16 us
  transfers between devices with their start and end apart: 12, of which 7 were waited for; matrix products, arithmetic and copies ran while one was open for 0% of the time, Pallas kernels for 17%

profile of v1, /device:TPU:8, one launch (start us, length us, event | category | flops | bytes accessed | tf_op | source)
XLA Modules:
  0.0 86.7 jit_solution(11629675904792839277)
XLA Ops:
  0.0 0.8 copy.6.table.refs_0_
  0.8 0.0 copy-start
  0.8 1.0 %copy-done = f32[14,8,8,128]{3,2,1,0:T(8,128)S(1)} copy-done((f32[14,8,8,128]{3,2,1,0:T(8,128)S(1)}, f32[14,8,8,128]{3,2,1,0:T(8,128)}, u32[]{:S(2)}) %copy-start) | copy-done | bytes 458776
  1.8 0.0 copy-start.1
  1.8 0.7 copy-done.1
  2.4 0.0 copy-start.2
  2.4 0.7 copy-done.2
  3.1 1.7 %cells.1 = (f32[12,64,128]{2,1,0:T(8,128)S(1)}, f32[8,128]{1,0:T(8,128)S(1)}, f32[14,24,128]{2,1,0:T(8,128)S(1)}, f32[14,24,128]{2,1,0:T(8,128)S(1)}, f32[14,24,...) custom-call(f32[32,6]{1,0:T(8,128)S(1)} %copy.6.table.refs_0_, f32[32]{0:T(128)S(1)} %copy-done.1, s32[9]{0:T(128)S(1)} %copy-done.2, ...), custom_call_target="tpu_custom_call" | custom-call | tf_op jit(solution)/shard_map/cells/pallas_call | solution.py:360
  4.8 0.1 collective-permute-start.10
  4.9 5.3 %collective-permute-start.11 = (f32[14,24,128]{2,1,0:T(8,128)S(1)}, f32[14,24,128]{2,1,0:T(8,128)S(1)}, u32[]{:S(2)}, u32[]{:S(2)}) collective-permute-start(f32[14,24,128]{2,1,0:T(8,128)S(1)} %get-tuple-element.16), channel_id=1, source_target_pairs={{1,0},{2,1},{3,2},{4,3},{5,4},{6,5},{7,6},{8,7},{9,8},{10,9},{11,1... | collective-permute-start | bytes 516104 | tf_op jit(solution)/shard_map/ppermute | solution.py:411
  10.2 1.8 %collective-permute-start.8 = (f32[14,24,128]{2,1,0:T(8,128)S(1)}, f32[14,24,128]{2,1,0:T(8,128)S(1)}, u32[]{:S(2)}, u32[]{:S(2)}) collective-permute-start(f32[14,24,128]{2,1,0:T(8,128)S(1)} %get-tuple-element.13), channel_id=1, source_target_pairs={{0,16},{16,32},{32,48},{48,64},{64,80},{80,96},{96,112},{112,128},... | collective-permute-start | bytes 516104 | tf_op jit(solution)/shard_map/ppermute | solution.py:410
  12.0 0.4 collective-permute-start.9
  12.4 0.0 collective-permute-start
  12.4 1.2 %collective-permute-done = f32[8,128]{1,0:T(8,128)S(1)} collective-permute-done((f32[8,128]{1,0:T(8,128)S(1)}, f32[8,128]{1,0:T(8,128)S(1)}, u32[]{:S(2)}, u32[]{:S(2)}) %collective-permute-start) | collective-permute-done | bytes 4128 | tf_op jit(solution)/shard_map/ppermute | solution.py:408
  13.5 0.1 collective-permute-start.1
  13.7 8.9 %collective-permute-done.1 = f32[8,128]{1,0:T(8,128)S(1)} collective-permute-done((f32[8,128]{1,0:T(8,128)S(1)}, f32[8,128]{1,0:T(8,128)S(1)}, u32[]{:S(2)}, u32[]{:S(2)}) %collective-permute-start.1) | collective-permute-done | bytes 4128 | tf_op jit(solution)/shard_map/ppermute | solution.py:408
  22.6 0.3 collective-permute-start.2
  22.9 3.3 %collective-permute-done.2 = f32[8,128]{1,0:T(8,128)S(1)} collective-permute-done((f32[8,128]{1,0:T(8,128)S(1)}, f32[8,128]{1,0:T(8,128)S(1)}, u32[]{:S(2)}, u32[]{:S(2)}) %collective-permute-start.2) | collective-permute-done | bytes 4128 | tf_op jit(solution)/shard_map/ppermute | solution.py:408
  26.2 1.8 %collective-permute-start.3 = (f32[8,128]{1,0:T(8,128)S(1)}, f32[8,128]{1,0:T(8,128)S(1)}, u32[]{:S(2)}, u32[]{:S(2)}) collective-permute-start(f32[8,128]{1,0:T(8,128)S(1)} %max.26), channel_id=1, source_target_pairs={{0,8},{4,12},{8,0},{12,4},{1,9},{5,13},{9,1},{13,5},{2,10},{6,14},... | collective-permute-start | bytes 12296 | tf_op jit(solution)/shard_map/ppermute | solution.py:408
  28.0 3.3 %collective-permute-done.3 = f32[8,128]{1,0:T(8,128)S(1)} collective-permute-done((f32[8,128]{1,0:T(8,128)S(1)}, f32[8,128]{1,0:T(8,128)S(1)}, u32[]{:S(2)}, u32[]{:S(2)}) %collective-permute-start.3) | collective-permute-done | bytes 4128 | tf_op jit(solution)/shard_map/ppermute | solution.py:408
  31.3 1.2 %collective-permute-start.4 = (f32[8,128]{1,0:T(8,128)S(1)}, f32[8,128]{1,0:T(8,128)S(1)}, u32[]{:S(2)}, u32[]{:S(2)}) collective-permute-start(f32[8,128]{1,0:T(8,128)S(1)} %max.27), channel_id=1, source_target_pairs={{0,16},{16,0},{1,17},{17,1},{2,18},{18,2},{3,19},{19,3},{4,20},{20... | collective-permute-start | bytes 12296 | tf_op jit(solution)/shard_map/ppermute | solution.py:408
  32.5 2.4 %collective-permute-done.4 = f32[8,128]{1,0:T(8,128)S(1)} collective-permute-done((f32[8,128]{1,0:T(8,128)S(1)}, f32[8,128]{1,0:T(8,128)S(1)}, u32[]{:S(2)}, u32[]{:S(2)}) %collective-permute-start.4) | collective-permute-done | bytes 4128 | tf_op jit(solution)/shard_map/ppermute | solution.py:408
  34.9 1.2 %collective-permute-start.5 = (f32[8,128]{1,0:T(8,128)S(1)}, f32[8,128]{1,0:T(8,128)S(1)}, u32[]{:S(2)}, u32[]{:S(2)}) collective-permute-start(f32[8,128]{1,0:T(8,128)S(1)} %max.28), channel_id=1, source_target_pairs={{0,32},{32,0},{64,96},{96,64},{128,160},{160,128},{192,224},{224,1... | collective-permute-start | bytes 12296 | tf_op jit(solution)/shard_map/ppermute | solution.py:408
  36.1 2.4 %collective-permute-done.5 = f32[8,128]{1,0:T(8,128)S(1)} collective-permute-done((f32[8,128]{1,0:T(8,128)S(1)}, f32[8,128]{1,0:T(8,128)S(1)}, u32[]{:S(2)}, u32[]{:S(2)}) %collective-permute-start.5) | collective-permute-done | bytes 4128 | tf_op jit(solution)/shard_map/ppermute | solution.py:408
  38.6 2.6 %collective-permute-start.6 = (f32[8,128]{1,0:T(8,128)S(1)}, f32[8,128]{1,0:T(8,128)S(1)}, u32[]{:S(2)}, u32[]{:S(2)}) collective-permute-start(f32[8,128]{1,0:T(8,128)S(1)} %max.29), channel_id=1, source_target_pairs={{0,64},{32,96},{64,0},{96,32},{128,192},{160,224},{192,128},{224,1... | collective-permute-start | bytes 12296 | tf_op jit(solution)/shard_map/ppermute | solution.py:408
  41.1 1.9 %collective-permute-done.6 = f32[8,128]{1,0:T(8,128)S(1)} collective-permute-done((f32[8,128]{1,0:T(8,128)S(1)}, f32[8,128]{1,0:T(8,128)S(1)}, u32[]{:S(2)}, u32[]{:S(2)}) %collective-permute-start.6) | collective-permute-done | bytes 4128 | tf_op jit(solution)/shard_map/ppermute | solution.py:408
  43.1 7.2 %collective-permute-start.7 = (f32[8,128]{1,0:T(8,128)S(1)}, f32[8,128]{1,0:T(8,128)S(1)}, u32[]{:S(2)}, u32[]{:S(2)}) collective-permute-start(f32[8,128]{1,0:T(8,128)S(1)} %max.30), channel_id=1, source_target_pairs={{0,128},{32,160},{64,192},{96,224},{128,0},{160,32},{192,64},{224,... | collective-permute-start | bytes 12296 | tf_op jit(solution)/shard_map/ppermute | solution.py:408
  50.3 0.0 copy-start.3
  50.3 0.7 copy-done.3
  50.9 9.0 %columns.1.z_ref = f32[9,192,8,128]{3,2,1,0:T(8,128)} custom-call(f32[32,6]{1,0:T(8,128)S(1)} %copy.6.table.refs_0_, f32[32]{0:T(128)S(1)} %copy-done.1, s32[9]{0:T(128)S(1)} %copy-done.2, s32[1,1,2]{2,1,0:T(1,128)S(1)} %copy-done.3, f32[14,64,128]{2,1,0:T(8,128)S(1)} %bitcast.3, f32[12,64,128]{2,1,0:T(8,128)S(1)} %get-tuple-element.12.refs_4_.coef_ref), custom_call_target="tpu_custom_call" | custom-call | tf_op jit(solution)/shard_map/columns/pallas_call | solution.py:378
  59.9 0.0 collective-permute-done.7
  59.9 0.0 collective-permute-done.10.refs_5_
  59.9 0.0 collective-permute-done.11.refs_6_
  59.9 6.0 %y_lines.1.y_ref = f32[9,192,8,128]{3,2,1,0:T(8,128)} custom-call(f32[32,6]{1,0:T(8,128)S(1)} %copy.6.table.refs_0_, f32[32]{0:T(128)S(1)} %copy-done.1, s32[9]{0:T(128)S(1)} %copy-done.2, f32[14,64,128]{2,1,0:T(8,128)S(1)} %bitcast.4, f32[12,64,128]{2,1,0:T(8,128)S(1)} %get-tuple-element.12.refs_4_.coef_ref, ...), custom_call_target="tpu_custom_call" | custom-call | tf_op jit(solution)/shard_map/y_lines/pallas_call | solution.py:369
  65.8 0.0 collective-permute-done.8.refs_5_
  65.9 0.0 collective-permute-done.9.refs_6_
  65.9 5.9 %x_lines.1.x_ref = f32[9,192,8,128]{3,2,1,0:T(8,128)} custom-call(f32[32,6]{1,0:T(8,128)S(1)} %copy.6.table.refs_0_, f32[32]{0:T(128)S(1)} %copy-done.1, s32[9]{0:T(128)S(1)} %copy-done.2, f32[14,64,128]{2,1,0:T(8,128)S(1)} %bitcast.5, f32[12,64,128]{2,1,0:T(8,128)S(1)} %get-tuple-element.12.refs_4_.coef_ref, ...), custom_call_target="tpu_custom_call" | custom-call | tf_op jit(solution)/shard_map/x_lines/pallas_call | solution.py:369
  71.7 15.0 %rates.1 = f32[14,64,128]{2,1,0:T(8,128)} custom-call(f32[8,128]{1,0:T(8,128)S(1)} %max.31.alpha_ref, f32[9,192,8,128]{3,2,1,0:T(8,128)} %x_lines.1.x_ref, f32[9,192,8,128]{3,2,1,0:T(8,128)} %y_lines.1.y_ref, f32[9,192,8,128]{3,2,1,0:T(8,128)} %columns.1.z_ref), custom_call_target="tpu_custom_call" | custom-call | tf_op jit(solution)/shard_map/rates/pallas_call | solution.py:387
  (8 shorter events, 0.0 us)
Async XLA Ops:
  0.8 1.0 %copy-start = (f32[14,8,8,128]{3,2,1,0:T(8,128)S(1)}, f32[14,8,8,128]{3,2,1,0:T(8,128)}, u32[]{:S(2)}) copy-start(f32[14,8,8,128]{3,2,1,0:T(8,128)} %param.5) | copy-start | bytes 1376260
  1.8 0.7 copy-start.1
  2.4 0.7 copy-start.2
  4.8 55.1 %collective-permute-start.10 = (f32[14,24,128]{2,1,0:T(8,128)S(1)}, f32[14,24,128]{2,1,0:T(8,128)S(1)}, u32[]{:S(2)}, u32[]{:S(2)}) collective-permute-start(f32[14,24,128]{2,1,0:T(8,128)S(1)} %get-tuple-element.15), channel_id=1, source_target_pairs={{0,1},{1,2},{2,3},{3,4},{4,5},{5,6},{6,7},{7,8},{8,9},{9,10},{10,1... | collective-permute-start | bytes 516104 | tf_op jit(solution)/shard_map/ppermute | solution.py:411
  4.9 55.0 %collective-permute-start.11 = (f32[14,24,128]{2,1,0:T(8,128)S(1)}, f32[14,24,128]{2,1,0:T(8,128)S(1)}, u32[]{:S(2)}, u32[]{:S(2)}) collective-permute-start(f32[14,24,128]{2,1,0:T(8,128)S(1)} %get-tuple-element.16), channel_id=1, source_target_pairs={{1,0},{2,1},{3,2},{4,3},{5,4},{6,5},{7,6},{8,7},{9,8},{10,9},{11,1... | collective-permute-start | bytes 516104 | tf_op jit(solution)/shard_map/ppermute | solution.py:411
  10.2 55.6 %collective-permute-start.8 = (f32[14,24,128]{2,1,0:T(8,128)S(1)}, f32[14,24,128]{2,1,0:T(8,128)S(1)}, u32[]{:S(2)}, u32[]{:S(2)}) collective-permute-start(f32[14,24,128]{2,1,0:T(8,128)S(1)} %get-tuple-element.13), channel_id=1, source_target_pairs={{0,16},{16,32},{32,48},{48,64},{64,80},{80,96},{96,112},{112,128},... | collective-permute-start | bytes 516104 | tf_op jit(solution)/shard_map/ppermute | solution.py:410
  12.0 53.8 %collective-permute-start.9 = (f32[14,24,128]{2,1,0:T(8,128)S(1)}, f32[14,24,128]{2,1,0:T(8,128)S(1)}, u32[]{:S(2)}, u32[]{:S(2)}) collective-permute-start(f32[14,24,128]{2,1,0:T(8,128)S(1)} %get-tuple-element.14), channel_id=1, source_target_pairs={{16,0},{32,16},{48,32},{64,48},{80,64},{96,80},{112,96},{128,112},... | collective-permute-start | bytes 516104 | tf_op jit(solution)/shard_map/ppermute | solution.py:410
  12.4 1.2 %collective-permute-start = (f32[8,128]{1,0:T(8,128)S(1)}, f32[8,128]{1,0:T(8,128)S(1)}, u32[]{:S(2)}, u32[]{:S(2)}) collective-permute-start(f32[8,128]{1,0:T(8,128)S(1)} %get-tuple-element.11), channel_id=1, source_target_pairs={{0,1},{1,0},{2,3},{3,2},{4,5},{5,4},{6,7},{7,6},{8,9},{9,8},{10,11... | collective-permute-start | bytes 12296 | tf_op jit(solution)/shard_map/ppermute | solution.py:408
  13.5 9.1 %collective-permute-start.1 = (f32[8,128]{1,0:T(8,128)S(1)}, f32[8,128]{1,0:T(8,128)S(1)}, u32[]{:S(2)}, u32[]{:S(2)}) collective-permute-start(f32[8,128]{1,0:T(8,128)S(1)} %max.24), channel_id=1, source_target_pairs={{0,2},{2,0},{1,3},{3,1},{4,6},{6,4},{5,7},{7,5},{8,10},{10,8},{9,1... | collective-permute-start | bytes 12296 | tf_op jit(solution)/shard_map/ppermute | solution.py:408
  22.6 3.6 %collective-permute-start.2 = (f32[8,128]{1,0:T(8,128)S(1)}, f32[8,128]{1,0:T(8,128)S(1)}, u32[]{:S(2)}, u32[]{:S(2)}) collective-permute-start(f32[8,128]{1,0:T(8,128)S(1)} %max.25), channel_id=1, source_target_pairs={{0,4},{4,0},{8,12},{12,8},{1,5},{5,1},{9,13},{13,9},{2,6},{6,2},{1... | collective-permute-start | bytes 12296 | tf_op jit(solution)/shard_map/ppermute | solution.py:408
  26.2 5.1 %collective-permute-start.3 = (f32[8,128]{1,0:T(8,128)S(1)}, f32[8,128]{1,0:T(8,128)S(1)}, u32[]{:S(2)}, u32[]{:S(2)}) collective-permute-start(f32[8,128]{1,0:T(8,128)S(1)} %max.26), channel_id=1, source_target_pairs={{0,8},{4,12},{8,0},{12,4},{1,9},{5,13},{9,1},{13,5},{2,10},{6,14},... | collective-permute-start | bytes 12296 | tf_op jit(solution)/shard_map/ppermute | solution.py:408
  31.3 3.6 %collective-permute-start.4 = (f32[8,128]{1,0:T(8,128)S(1)}, f32[8,128]{1,0:T(8,128)S(1)}, u32[]{:S(2)}, u32[]{:S(2)}) collective-permute-start(f32[8,128]{1,0:T(8,128)S(1)} %max.27), channel_id=1, source_target_pairs={{0,16},{16,0},{1,17},{17,1},{2,18},{18,2},{3,19},{19,3},{4,20},{20... | collective-permute-start | bytes 12296 | tf_op jit(solution)/shard_map/ppermute | solution.py:408
  34.9 3.6 %collective-permute-start.5 = (f32[8,128]{1,0:T(8,128)S(1)}, f32[8,128]{1,0:T(8,128)S(1)}, u32[]{:S(2)}, u32[]{:S(2)}) collective-permute-start(f32[8,128]{1,0:T(8,128)S(1)} %max.28), channel_id=1, source_target_pairs={{0,32},{32,0},{64,96},{96,64},{128,160},{160,128},{192,224},{224,1... | collective-permute-start | bytes 12296 | tf_op jit(solution)/shard_map/ppermute | solution.py:408
  38.6 4.5 %collective-permute-start.6 = (f32[8,128]{1,0:T(8,128)S(1)}, f32[8,128]{1,0:T(8,128)S(1)}, u32[]{:S(2)}, u32[]{:S(2)}) collective-permute-start(f32[8,128]{1,0:T(8,128)S(1)} %max.29), channel_id=1, source_target_pairs={{0,64},{32,96},{64,0},{96,32},{128,192},{160,224},{192,128},{224,1... | collective-permute-start | bytes 12296 | tf_op jit(solution)/shard_map/ppermute | solution.py:408
  43.1 16.8 %collective-permute-start.7 = (f32[8,128]{1,0:T(8,128)S(1)}, f32[8,128]{1,0:T(8,128)S(1)}, u32[]{:S(2)}, u32[]{:S(2)}) collective-permute-start(f32[8,128]{1,0:T(8,128)S(1)} %max.30), channel_id=1, source_target_pairs={{0,128},{32,160},{64,192},{96,224},{128,0},{160,32},{192,64},{224,... | collective-permute-start | bytes 12296 | tf_op jit(solution)/shard_map/ppermute | solution.py:408
  50.3 0.7 copy-start.3

commit v2 on v1

--- a/solution.py
+++ b/solution.py
@@ -352,7 +352,7 @@
 
 
 def params():
-    return pltpu.CompilerParams(vmem_limit_bytes=48 << 20)
+    return pltpu.CompilerParams(vmem_limit_bytes=20 << 20)
 
 
 def cells(u, table, gas, index):
@@ -396,20 +396,51 @@
 GY = ("x", "yh", "c")
 
 
+def flat(z, y, x, c):
+    return (((z * 2 + y % 2) * 4 + x) * 2 + y // 2) * 2 + c
+
+
+def exchange(value, dim, partner):
+    pairs = []
+    for z in range(8):
+        for y in range(4):
+            for x in range(4):
+                at = [z, y, x]
+                to = list(at)
+                to[dim] = partner(at[dim])
+                pairs += [(flat(*at, c), flat(*to, c)) for c in range(2)]
+    return lax.ppermute(value, AXES, pairs)
+
+
+def near(i):
+    return i ^ 1
+
+
+def other(n):
+    return lambda i: (i + 1) % n if i % 2 else (i - 1) % n
+
+
+def far(i):
+    return (3, 6, 5, 0, 7, 2, 1, 4)[i]
+
+
+def core(value):
+    return jnp.maximum(value, lax.ppermute(value, "c", [(0, 1), (1, 0)]))
+
+
 def shards(preserved_vector, nasa_table, gas_constant, species_index, face_kind):
     u = preserved_vector.reshape(NVAR, 64, LANES)
-    coef, alpha, xs, xe, ys, ye = cells(u, nasa_table, gas_constant, species_index)
+    fixed = (nasa_table, gas_constant, species_index)
+    coef, alpha, xs, xe, ys, ye = cells(u, *fixed)
     up = [(i, (i + 1) % 16) for i in range(16)]
     down = [(b, a) for a, b in up]
-    for axis in reversed(AXES):
-        size = lax.axis_size(axis)
-        step = 1
-        while step < size:
-            alpha = jnp.maximum(alpha, lax.ppermute(alpha, axis, [(i, i ^ step) for i in range(size)]))
-            step *= 2
     x_low, x_high = lax.ppermute(xe, GX, up), lax.ppermute(xs, GX, down)
     y_low, y_high = lax.ppermute(ye, GY, up), lax.ppermute(ys, GY, down)
-    fixed = (nasa_table, gas_constant, species_index)
+
+    wide = jnp.broadcast_to(alpha[0:3, 0].reshape(1, 1, 3), (256, 1, 3))
+    wide = lax.all_to_all(wide, AXES, 0, 0, tiled=True)
+    alpha = jnp.broadcast_to(jnp.pad(jnp.max(wide, axis=0).reshape(3, 1), ((0, 5), (0, 0))), (8, LANES))
+
     z = columns(*fixed, face_kind, u, coef)
     x = lines("x_lines", (0, 1, 2), False, *fixed, u, coef, x_low, x_high)
     y = lines("y_lines", (1, 0, 2), True, *fixed, u, coef, y_low, y_high)

time: 86.9 us -> 56.6 us (0.65)
  the two profiles are of different devices: /device:TPU:8 before, /device:TPU:1 now
where the time goes in v2:
time: 56.6 us; the launch traced here: 56.4 us
  starting transfers between devices  23.1 us (41%)
  Pallas kernels  21.8 us (39%)
  local copies, waits for them, and re-layouts  9.92 us (18%)
  waiting for transfers between devices  1.08 us (2%)
    all_to_all x1, starting transfers between devices, shards(): wide = lax.all_to_all(wide, AXES, 0, 0, tiled=True)  12.1 us
    unnamed x27, local copies, waits for them, and re-layouts  9 us
    pallas_call x1, Pallas kernels, rates(): pl.pallas_call(rate_kernel, name='rates', in_specs=[VMEM] * 4, out_specs=...  7.98 us
    ppermute x2, starting transfers between devices, shards(): x_low, x_high = (lax.ppermute(xe, GX, up), lax.ppermute(xs, GX, down))  7.57 us
    pallas_call x1, Pallas kernels, columns(): pl.pallas_call(column_kernel, name='columns', in_specs=[SMEM] * 4 + [VMEM...  6.12 us
    pallas_call x2, Pallas kernels, lines(): pl.pallas_call(body, name=name, in_specs=[SMEM] * 3 + [VMEM] * 4, out_spe...  6.06 us
    ppermute x2, starting transfers between devices, shards(): y_low, y_high = (lax.ppermute(ye, GY, up), lax.ppermute(ys, GY, down))  3.46 us
    pallas_call x1, Pallas kernels, cells(): pl.pallas_call(cell_kernel, name='cells', in_specs=[SMEM] * 3 + [VMEM], o...  1.67 us
  transfers between devices with their start and end apart: 5, of which 1 were waited for; matrix products, arithmetic and copies ran while one was open for 2% of the time, Pallas kernels for 16%

profile of v2, /device:TPU:1, one launch (start us, length us, event | category | flops | bytes accessed | tf_op | source)
XLA Modules:
  0.0 56.4 jit_solution(5272638310919713010)
XLA Ops:
  0.0 0.0 copy-start.9
  0.0 0.0 copy-start.6
  0.0 0.8 %copy.23.table.refs_0_ = f32[32,6]{1,0:T(8,128)S(1)} copy(f32[32,6]{0,1:T(8,128)} %param.6) | data formatting | bytes 1536 | tf_op args[1]
  0.8 0.0 copy-start.1
  0.8 1.0 %copy-done.1 = f32[14,8,8,128]{3,2,1,0:T(8,128)S(1)} copy-done((f32[14,8,8,128]{3,2,1,0:T(8,128)S(1)}, f32[14,8,8,128]{3,2,1,0:T(8,128)}, u32[]{:S(2)}) %copy-start.1) | copy-done | bytes 458776
  1.8 0.0 copy-start.4
  1.8 0.7 %copy-done.4 = f32[32]{0:T(128)S(1)} copy-done((f32[32]{0:T(128)S(1)}, f32[32]{0:T(128)}, u32[]{:S(2)}) %copy-start.4) | copy-done | bytes 152
  2.5 0.0 copy-start.7
  2.5 0.7 %copy-done.7 = s32[9]{0:T(128)S(1)} copy-done((s32[9]{0:T(128)S(1)}, s32[9]{0:T(128)}, u32[]{:S(2)}) %copy-start.7) | copy-done | bytes 60
  3.1 0.0 copy-start.3
  3.1 1.7 %cells.1 = (f32[12,64,128]{2,1,0:T(8,128)S(1)}, f32[8,128]{1,0:T(8,128)S(1)}, f32[14,24,128]{2,1,0:T(8,128)S(1)}, f32[14,24,128]{2,1,0:T(8,128)S(1)}, f32[14,24,...) custom-call(f32[32,6]{1,0:T(8,128)S(1)} %copy.23.table.refs_0_, f32[32]{0:T(128)S(1)} %copy-done.4, s32[9]{0:T(128)S(1)} %copy-done.7, ...), custom_call_target="tpu_custom_call" | custom-call | tf_op jit(solution)/shard_map/cells/pallas_call | solution.py:360
  4.8 2.2 %collective-permute-start = (f32[14,24,128]{2,1,0:T(8,128)S(1)}, f32[14,24,128]{2,1,0:T(8,128)S(1)}, u32[]{:S(2)}, u32[]{:S(2)}) collective-permute-start(f32[14,24,128]{2,1,0:T(8,128)S(1)} %get-tuple-element.13), channel_id=1, source_target_pairs={{0,16},{16,32},{32,48},{48,64},{64,80},{80,96},{96,112},{112,128},... | collective-permute-start | bytes 516104 | tf_op jit(solution)/shard_map/ppermute | solution.py:437
  7.0 5.4 %collective-permute-start.1 = (f32[14,24,128]{2,1,0:T(8,128)S(1)}, f32[14,24,128]{2,1,0:T(8,128)S(1)}, u32[]{:S(2)}, u32[]{:S(2)}) collective-permute-start(f32[14,24,128]{2,1,0:T(8,128)S(1)} %get-tuple-element.14), channel_id=1, source_target_pairs={{16,0},{32,16},{48,32},{64,48},{80,64},{96,80},{112,96},{128,112},... | collective-permute-start | bytes 516104 | tf_op jit(solution)/shard_map/ppermute | solution.py:437
  12.4 3.5 %collective-permute-start.2 = (f32[14,24,128]{2,1,0:T(8,128)S(1)}, f32[14,24,128]{2,1,0:T(8,128)S(1)}, u32[]{:S(2)}, u32[]{:S(2)}) collective-permute-start(f32[14,24,128]{2,1,0:T(8,128)S(1)} %get-tuple-element.15), channel_id=1, source_target_pairs={{0,1},{1,2},{2,3},{3,4},{4,5},{5,6},{6,7},{7,8},{8,9},{9,10},{10,1... | collective-permute-start | bytes 516104 | tf_op jit(solution)/shard_map/ppermute | solution.py:438
  15.8 0.0 collective-permute-start.3
  15.8 0.1 slice_reduce_fusion
  16.0 0.7 %broadcast_in_dim.15 = f32[256,1,3]{2,1,0:T(1,128)} broadcast(f32[3]{0:T(128)S(1)} %slice_reduce_fusion), dimensions={2} | broadcast | bytes 3084 | tf_op jit(solution)/shard_map/broadcast_in_dim | solution.py:440
  16.7 12.1 %all-to-all-start = ((f32[256,1,3]{2,1,0:T(1,128)}), f32[256,1,3]{2,1,0:T(1,128)S(1)}, u32[]{:S(2)}, u32[]{:S(2)}) async-start(f32[256,1,3]{2,1,0:T(1,128)} %broadcast_in_dim.15), calls=%async_computation | async-start | bytes 262144 | tf_op jit(solution)/shard_map/all_to_all | solution.py:441
  28.8 0.0 copy-start.2
  28.8 1.0 %copy-done.2 = f32[14,8,8,128]{3,2,1,0:T(8,128)S(1)} copy-done((f32[14,8,8,128]{3,2,1,0:T(8,128)S(1)}, f32[14,8,8,128]{3,2,1,0:T(8,128)}, u32[]{:S(2)}) %copy-start.2) | copy-done | bytes 458776
  29.8 0.0 copy-start.5
  29.8 0.7 %copy-done.5 = f32[32]{0:T(128)S(1)} copy-done((f32[32]{0:T(128)S(1)}, f32[32]{0:T(128)}, u32[]{:S(2)}) %copy-start.5) | copy-done | bytes 152
  30.4 0.0 copy-start.8
  30.4 0.7 %copy-done.8 = s32[9]{0:T(128)S(1)} copy-done((s32[9]{0:T(128)S(1)}, s32[9]{0:T(128)}, u32[]{:S(2)}) %copy-start.8) | copy-done | bytes 60
  31.1 0.0 copy-start.10
  31.1 0.7 %copy-done.10 = s32[1,1,2]{2,1,0:T(1,128)S(1)} copy-done((s32[1,1,2]{2,1,0:T(1,128)S(1)}, s32[1,1,2]{2,1,0:T(1,128)}, u32[]{:S(2)}) %copy-start.10) | copy-done | bytes 32
  31.8 6.1 %columns.1.z_ref = f32[9,192,8,128]{3,2,1,0:T(8,128)S(1)} custom-call(f32[32,6]{1,0:T(8,128)S(1)} %copy.23.table.refs_0_, f32[32]{0:T(128)S(1)} %copy-done.5, s32[9]{0:T(128)S(1)} %copy-done.8, s32[1,1,2]{2,1,0:T(1,128)S(1)} %copy-done.10, f32[14,64,128]{2,1,0:T(8,128)S(1)} %bitcast.8, f32[12,64,128]{2,1,0:T(8,128)S(1)} %get-tuple-element.12.refs_4_.coef_ref), custom_call_target="tpu_custom_call" | custom-call | tf_op jit(solution)/shard_map/columns/pallas_call | solution.py:378
  37.9 0.0 copy-start
  37.9 2.9 %copy-done = f32[9,192,8,128]{3,2,1,0:T(8,128)} copy-done((f32[9,192,8,128]{3,2,1,0:T(8,128)}, f32[9,192,8,128]{3,2,1,0:T(8,128)S(1)}, u32[]{:S(2)}) %copy-start) | copy-done | bytes 7077912
  40.8 1.1 %all-to-all-done = f32[256,1,3]{2,1,0:T(1,128)S(1)} async-done(((f32[256,1,3]{2,1,0:T(1,128)}), f32[256,1,3]{2,1,0:T(1,128)S(1)}, u32[]{:S(2)}, u32[]{:S(2)}) %all-to-all-start) | async-done | bytes 3104 | tf_op jit(solution)/shard_map/all_to_all | solution.py:441
  41.8 0.3 reduce_max.9
  42.1 0.0 slice-start
  42.1 0.0 collective-permute-done.2.refs_5_
  42.2 0.0 collective-permute-done.3.refs_6_
  42.2 0.0 copy-done.9
  42.2 0.0 copy-done.6
  42.2 0.0 copy-done.3
  42.2 3.1 %y_lines.1.y_ref = f32[9,192,8,128]{3,2,1,0:T(8,128)S(1)} custom-call(f32[32,6]{1,0:T(8,128)S(1)} %copy.23.table.refs_0_, f32[32]{0:T(128)S(1)} %copy-done.6, s32[9]{0:T(128)S(1)} %copy-done.9, f32[14,64,128]{2,1,0:T(8,128)S(1)} %bitcast.9, f32[12,64,128]{2,1,0:T(8,128)S(1)} %get-tuple-element.12.refs_4_.coef_ref, ...), custom_call_target="tpu_custom_call" | custom-call | tf_op jit(solution)/shard_map/y_lines/pallas_call | solution.py:369
  45.3 0.0 slice-start.1
  45.3 0.0 collective-permute-done.refs_5_
  45.3 0.0 collective-permute-done.1.refs_6_
  45.3 3.0 %x_lines.1.x_ref = f32[9,192,8,128]{3,2,1,0:T(8,128)S(1)} custom-call(f32[32,6]{1,0:T(8,128)S(1)} %copy.23.table.refs_0_, f32[32]{0:T(128)S(1)} %copy-done.6, s32[9]{0:T(128)S(1)} %copy-done.9, f32[14,64,128]{2,1,0:T(8,128)S(1)} %bitcast.10, f32[12,64,128]{2,1,0:T(8,128)S(1)} %get-tuple-element.12.refs_4_.coef_ref, ...), custom_call_target="tpu_custom_call" | custom-call | tf_op jit(solution)/shard_map/x_lines/pallas_call | solution.py:369
  48.3 0.1 broadcast_in_dim.17.alpha_ref
  48.4 0.0 slice-done
  48.4 0.0 slice-done.1
  48.4 8.0 %rates.1 = f32[14,64,128]{2,1,0:T(8,128)} custom-call(f32[8,128]{1,0:T(8,128)S(1)} %broadcast_in_dim.17.alpha_ref, f32[9,192,8,128]{3,2,1,0:T(8,128)S(1)} %x_lines.1.x_ref, f32[9,192,8,128]{3,2,1,0:T(8,128)S(1)} %y_lines.1.y_ref, f32[9,192,8,128]{3,2,1,0:T(8,128)S(1)} %bitcast.6), custom_call_target="tpu_custom_call" | custom-call | tf_op jit(solution)/shard_map/rates/pallas_call | solution.py:387
  (2 shorter events, 0.0 us)
Async XLA Ops:
  0.0 42.2 %copy-start.9 = (s32[9]{0:T(128)S(1)}, s32[9]{0:T(128)}, u32[]{:S(2)}) copy-start(s32[9]{0:T(128)} %index.3) | copy-start | bytes 112
  0.0 42.2 %copy-start.6 = (f32[32]{0:T(128)S(1)}, f32[32]{0:T(128)}, u32[]{:S(2)}) copy-start(f32[32]{0:T(128)} %gas.3) | copy-start | bytes 388
  0.8 1.0 %copy-start.1 = (f32[14,8,8,128]{3,2,1,0:T(8,128)S(1)}, f32[14,8,8,128]{3,2,1,0:T(8,128)}, u32[]{:S(2)}) copy-start(f32[14,8,8,128]{3,2,1,0:T(8,128)} %param.5) | copy-start | bytes 1376260
  1.8 0.7 %copy-start.4 = (f32[32]{0:T(128)S(1)}, f32[32]{0:T(128)}, u32[]{:S(2)}) copy-start(f32[32]{0:T(128)} %gas.3) | copy-start | bytes 388
  2.5 0.7 %copy-start.7 = (s32[9]{0:T(128)S(1)}, s32[9]{0:T(128)}, u32[]{:S(2)}) copy-start(s32[9]{0:T(128)} %index.3) | copy-start | bytes 112
  3.1 39.1 %copy-start.3 = (f32[14,8,8,128]{3,2,1,0:T(8,128)S(1)}, f32[14,8,8,128]{3,2,1,0:T(8,128)}, u32[]{:S(2)}) copy-start(f32[14,8,8,128]{3,2,1,0:T(8,128)} %param.5) | copy-start | bytes 1376260
  4.8 40.5 %collective-permute-start = (f32[14,24,128]{2,1,0:T(8,128)S(1)}, f32[14,24,128]{2,1,0:T(8,128)S(1)}, u32[]{:S(2)}, u32[]{:S(2)}) collective-permute-start(f32[14,24,128]{2,1,0:T(8,128)S(1)} %get-tuple-element.13), channel_id=1, source_target_pairs={{0,16},{16,32},{32,48},{48,64},{64,80},{80,96},{96,112},{112,128},... | collective-permute-start | bytes 516104 | tf_op jit(solution)/shard_map/ppermute | solution.py:437
  7.0 38.3 %collective-permute-start.1 = (f32[14,24,128]{2,1,0:T(8,128)S(1)}, f32[14,24,128]{2,1,0:T(8,128)S(1)}, u32[]{:S(2)}, u32[]{:S(2)}) collective-permute-start(f32[14,24,128]{2,1,0:T(8,128)S(1)} %get-tuple-element.14), channel_id=1, source_target_pairs={{16,0},{32,16},{48,32},{64,48},{80,64},{96,80},{112,96},{128,112},... | collective-permute-start | bytes 516104 | tf_op jit(solution)/shard_map/ppermute | solution.py:437
  12.4 29.8 %collective-permute-start.2 = (f32[14,24,128]{2,1,0:T(8,128)S(1)}, f32[14,24,128]{2,1,0:T(8,128)S(1)}, u32[]{:S(2)}, u32[]{:S(2)}) collective-permute-start(f32[14,24,128]{2,1,0:T(8,128)S(1)} %get-tuple-element.15), channel_id=1, source_target_pairs={{0,1},{1,2},{2,3},{3,4},{4,5},{5,6},{6,7},{7,8},{8,9},{9,10},{10,1... | collective-permute-start | bytes 516104 | tf_op jit(solution)/shard_map/ppermute | solution.py:438
  15.8 26.3 %collective-permute-start.3 = (f32[14,24,128]{2,1,0:T(8,128)S(1)}, f32[14,24,128]{2,1,0:T(8,128)S(1)}, u32[]{:S(2)}, u32[]{:S(2)}) collective-permute-start(f32[14,24,128]{2,1,0:T(8,128)S(1)} %get-tuple-element.16), channel_id=1, source_target_pairs={{1,0},{2,1},{3,2},{4,3},{5,4},{6,5},{7,6},{8,7},{9,8},{10,9},{11,1... | collective-permute-start | bytes 516104 | tf_op jit(solution)/shard_map/ppermute | solution.py:438
  16.7 25.2 %all-to-all-start = ((f32[256,1,3]{2,1,0:T(1,128)}), f32[256,1,3]{2,1,0:T(1,128)S(1)}, u32[]{:S(2)}, u32[]{:S(2)}) async-start(f32[256,1,3]{2,1,0:T(1,128)} %broadcast_in_dim.15), calls=%async_computation | async-start | bytes 262144 | tf_op jit(solution)/shard_map/all_to_all | solution.py:441
  28.8 1.0 %copy-start.2 = (f32[14,8,8,128]{3,2,1,0:T(8,128)S(1)}, f32[14,8,8,128]{3,2,1,0:T(8,128)}, u32[]{:S(2)}) copy-start(f32[14,8,8,128]{3,2,1,0:T(8,128)} %param.5) | copy-start | bytes 1376260
  29.8 0.7 %copy-start.5 = (f32[32]{0:T(128)S(1)}, f32[32]{0:T(128)}, u32[]{:S(2)}) copy-start(f32[32]{0:T(128)} %gas.3) | copy-start | bytes 388
  30.4 0.7 %copy-start.8 = (s32[9]{0:T(128)S(1)}, s32[9]{0:T(128)}, u32[]{:S(2)}) copy-start(s32[9]{0:T(128)} %index.3) | copy-start | bytes 112
  31.1 0.7 %copy-start.10 = (s32[1,1,2]{2,1,0:T(1,128)S(1)}, s32[1,1,2]{2,1,0:T(1,128)}, u32[]{:S(2)}) copy-start(s32[1,1,2]{2,1,0:T(1,128)} %kind.1) | copy-start | bytes 28
  37.9 2.9 %copy-start = (f32[9,192,8,128]{3,2,1,0:T(8,128)}, f32[9,192,8,128]{3,2,1,0:T(8,128)S(1)}, u32[]{:S(2)}) copy-start(f32[9,192,8,128]{3,2,1,0:T(8,128)S(1)} %columns.1.z_ref) | copy-start | bytes 21233668
  42.1 6.2 %slice-start = ((s8[7077888]{0:T(1024)(128)(4,1)}), s8[4194304]{0:T(1024)(128)(4,1)S(1)}, s32[]{:S(2)}) async-start(s8[7077888]{0:T(1024)(128)(4,1)} %bitcast.5), calls=%async_computation.1 | async-start | bytes 8388608
  45.3 3.1 %slice-start.1 = ((s8[7077888]{0:T(1024)(128)(4,1)}), s8[2883584]{0:T(1024)(128)(4,1)S(1)}, s32[]{:S(2)}) async-start(s8[7077888]{0:T(1024)(128)(4,1)} %bitcast.5), calls=%async_computation.2 | async-start | bytes 5767168

commit v3 on v1

v3 whole, which is shorter than its diff:
```python
import jax
import jax.numpy as jnp
from jax import lax
from jax.experimental import pallas as pl
from jax.experimental.pallas import tpu as pltpu
from jax.sharding import Mesh
from jax.sharding import PartitionSpec as P


NS = 9
NVAR = 14
NEWTON = 2
EPSILON = 1e-06
COURANT = 0.8
LANES = 128
F32 = jnp.float32


def species_constants(table, gas, index, const):
    for i in range(NS):
        row = index[i]
        r = jnp.full((8, LANES), gas[row], F32)
        a = [r * jnp.full((8, LANES), table[k, row], F32) for k in range(6)]
        rest = [a[0] - r, a[1] * 0.5, a[2] * (1.0 / 3.0), a[3] * 0.25, a[4] * 0.2]
        for k, value in enumerate([r] + a + rest):
            const[12 * i + k] = value


def coefficients(u, rows):
    rho = u[0]
    for i in range(1, NS):
        rho = rho + u[i]
    inv = 1.0 / rho
    vel = [u[NS + j] * inv for j in range(3)]
    square = vel[0] * vel[0] + vel[1] * vel[1] + vel[2] * vel[2]
    target = u[NS + 3] - 0.5 * rho * square
    mix = [None] * 7
    for i in range(NS):
        for k in range(7):
            term = u[i] * rows[12 * i + k]
            mix[k] = term if mix[k] is None else mix[k] + term
    r0, a1, a2, a3, a4, a5, a6 = mix
    b1, b2, b3, b4, b5 = a1 - r0, a2 * 0.5, a3 * (1.0 / 3.0), a4 * 0.25, a5 * 0.2
    temp = jnp.ones_like(rho)
    for _ in range(NEWTON):
        energy = a6 + temp * (b1 + temp * (b2 + temp * (b3 + temp * (b4 + temp * b5))))
        slope = b1 + temp * (a2 + temp * (a3 + temp * (a4 + temp * a5)))
        temp = temp - (energy - target) / slope
    slope = b1 + temp * (a2 + temp * (a3 + temp * (a4 + temp * a5)))
    g = r0 / slope
    p = r0 * temp
    c = jnp.sqrt((1.0 + g) * p * inv)
    kinetic = 0.5 * g * square
    phi = []
    for i in range(NS):
        e = [rows[12 * i + 6 + k] for k in range(6)]
        energy = e[0] + temp * (e[1] + temp * (e[2] + temp * (e[3] + temp * (e[4] + temp * e[5]))))
        phi.append(rows[12 * i] * temp - g * energy + kinetic)
    return p, g, c, phi, vel


def halves(u, rows):
    p, g, c, phi, _ = coefficients(u, rows)
    return [0.5 * x for x in [p, g, c] + phi]


def fetch(pairs, sem):
    copies = [pltpu.make_async_copy(src, dst, sem.at[i]) for i, (src, dst) in enumerate(pairs)]
    for copy in copies:
        copy.start()
    return copies


def cell_kernel(table_h, gas_h, index_h, u_h, wide_ref, xs_ref, xe_ref, ys_ref, ye_ref,
                table, gas, index, rows, u_ref, sem):
    for copy in fetch([(table_h, table), (gas_h, gas), (index_h, index), (u_h, u_ref)], sem):
        copy.wait()
    species_constants(table, gas, index, rows)

    def body(i, fastest):
        at = pl.ds(pl.multiple_of(i * 8, 8), 8)
        u = [u_ref[k, at, :] for k in range(NVAR)]
        c, vel = coefficients(u, rows)[2::2]
        return tuple(jnp.maximum(f, jnp.abs(v) + c) for f, v in zip(fastest, vel))

    zero = jnp.zeros((8, LANES), F32)
    fastest = lax.fori_loop(0, 8, body, (zero, zero, zero), unroll=4)
    lane = lax.broadcasted_iota(jnp.int32, (8, LANES), 1)
    out = zero
    for d in range(3):
        top = jnp.max(jnp.max(fastest[d], axis=0, keepdims=True), axis=1, keepdims=True)
        out = jnp.where(lane == d, jnp.broadcast_to(top, (8, LANES)), out)
    for i in range(32):
        wide_ref[8 * i:8 * i + 8, :] = out
    for k in range(NVAR):
        xs_ref[k] = u_ref[k, 0:24, :]
        xe_ref[k] = u_ref[k, 40:64, :]
        for j in range(3):
            ys_ref[k, 8 * j:8 * j + 8, :] = u_ref[k, pl.ds(j, 8, stride=8), :]
            ye_ref[k, 8 * j:8 * j + 8, :] = u_ref[k, pl.ds(5 + j, 8, stride=8), :]


def correction(d0, d1, d2, d3):
    t0 = d0 - 1.375 * d1
    t1 = d1 - 0.625 * d2
    t2 = d3 - 1.375 * d2
    e1 = (0.609375 * d1) * d1 + 0.75 * EPSILON
    e2 = (0.609375 * d2) * d2 + 0.75 * EPSILON
    i0 = reciprocal(t0 * t0 + e1)
    i1 = reciprocal(t1 * t1 + e2)
    i2 = reciprocal(t2 * t2 + e2)
    w0 = i0 * i0
    w1 = 6.0 * (i1 * i1)
    w2 = 3.0 * (i2 * i2)
    q = 2.625 * d2
    lead = (2.25 * d1 - q) - (t0 + t0)
    return q + (w0 * lead + w1 * t1 - w2 * t2) * reciprocal(w0 + w1 + w2)


def reciprocal(x):
    return 1.0 / x


def split_fields(u, coef, order, speed):
    p, g, c, phi = coef[0], coef[1], coef[2], coef[3:]
    rho = u[0]
    for i in range(1, NS):
        rho = rho + u[i]
    inv = 0.5 / rho
    vel = [u[NS + j] * inv for j in order]
    plus, minus = vel[0] + speed, vel[0] - speed
    rows = u[:NS] + [u[NS + j] for j in order] + [u[NS + 3], u[NS + 4], rho]
    up = [x * plus for x in rows]
    down = [x * minus for x in rows]
    work = (p + p) * vel[0]
    for side in (up, down):
        side[NS] = side[NS] + p
        side[NS + 3] = side[NS + 3] + work
    mean = [x * inv for x in u[:NS]] + vel + [u[NS + 4] * inv, g, c] + phi
    return up, down, mean


def face_flux(left, right, jump, put):
    def mean(k):
        return left(k) + right(k)

    g, c = mean(13), mean(14)
    vel = [mean(9 + k) for k in range(3)]
    ig = 1.0 / g
    ic = 1.0 / c
    inv = ic * ic
    ihc = 0.5 * ic
    gs = g * inv
    gu = [gs * v for v in vel]
    square = vel[0] * vel[0] + vel[1] * vel[1] + vel[2] * vel[2]
    dot = None
    phis = []
    for k in range(NS):
        phi = mean(15 + k)
        term = mean(k) * phi
        dot = term if dot is None else dot + term
        phis.append(phi * inv)
    h = (c * c - dot) * ig + square
    pressure, swings, sums = {}, {}, {}
    for side in range(2):
        for i in range(side, 4 + side):
            dp = phis[0] * jump(side, i, 0)
            for k in range(1, NS):
                dp = dp + phis[k] * jump(side, i, k)
            v = [jump(side, i, NS + k) for k in range(3)]
            s = jump(side, i, 14)
            dp = dp + (gs * jump(side, i, 12) - (gu[0] * v[0] + gu[1] * v[1] + gu[2] * v[2]))
            pressure[side, i] = dp
            swings[side, i] = (v[0] - vel[0] * s) * ihc
            sums[side, i] = s

    def amplitude(wave):
        p = [wave(0, i) for i in range(4)]
        m = [wave(1, i) for i in range(4, 0, -1)]
        return correction(*p) - correction(*m)

    slower = amplitude(lambda side, i: 0.5 * pressure[side, i] - swings[side, i])
    faster = amplitude(lambda side, i: 0.5 * pressure[side, i] + swings[side, i])
    first = amplitude(lambda side, i: jump(side, i, 10) - vel[1] * sums[side, i])
    second = amplitude(lambda side, i: jump(side, i, 11) - vel[2] * sums[side, i])
    acoustic = slower + faster
    swing = (faster - slower) * c
    energy = h * acoustic + vel[0] * swing + vel[1] * first + vel[2] * second
    z = mean(12)
    put(13, z * acoustic + amplitude(lambda side, i: jump(side, i, 13) - z * pressure[side, i]))
    total = dot = None
    for k in range(NS):
        yk = mean(k)
        species = amplitude(lambda side, i: jump(side, i, k) - yk * pressure[side, i])
        put(k, yk * acoustic + species)
        term = phis[k] * species
        total = species if total is None else total + species
        dot = term if dot is None else dot + term
    both = acoustic + total
    put(9, vel[0] * both + swing)
    put(10, vel[1] * both + first)
    put(11, vel[2] * both + second)
    put(12, energy + square * total - (dot * (c * c)) * ig)


def own_kernel(table_h, gas_h, index_h, kind_h, u_h, coef_ref, ends_ref,
               table, gas, index, rows, kind, u_ref, sem):
    for copy in fetch([(table_h, table), (gas_h, gas), (index_h, index), (kind_h, kind),
                       (u_h, u_ref)], sem):
        copy.wait()
    species_constants(table, gas, index, rows)
    lane = lax.broadcasted_iota(jnp.int32, (8, LANES), 1)
    slot = lane % 16
    group = lane // 16
    low_wall = kind[0, 0] == 1
    high_wall = kind[0, 1] == 1

    def pick(k):
        packed = jnp.zeros((8, LANES), F32)
        for plane in range(8):
            v = u_ref[k, 8 * plane:8 * plane + 8, :]
            low = pltpu.roll(v, (16 * plane + 3) % LANES, 1)
            high = pltpu.roll(v, (16 * plane + 8 - 123) % LANES, 1)
            packed = jnp.where(group == plane, jnp.where(slot < 8, low, high), packed)

        def at(shift):
            return pltpu.roll(packed, shift % LANES, 1)

        sign = -1.0 if k == NS + 2 else 1.0
        mirror = jnp.where(slot == 2, at(-1), jnp.where(slot == 1, at(-3), at(-5))) * sign
        copy = jnp.where(slot == 2, at(-1), jnp.where(slot == 1, at(-2), at(-3)))
        low = jnp.where(low_wall, mirror, copy)
        mirror = jnp.where(slot == 13, at(1), jnp.where(slot == 14, at(3), at(5))) * sign
        copy = jnp.where(slot == 13, at(1), jnp.where(slot == 14, at(2), at(3)))
        high = jnp.where(high_wall, mirror, copy)
        ends_ref[k] = jnp.where(slot < 3, low, jnp.where(slot > 12, high, packed))
        return 0

    for k in range(NVAR):
        pick(k)
    for k, value in enumerate(halves([ends_ref[k] for k in range(NVAR)], rows)):
        ends_ref[NVAR + k] = value

    def plane(i, _):
        at = pl.ds(pl.multiple_of(i * 8, 8), 8)
        for k, value in enumerate(halves([u_ref[k, at, :] for k in range(NVAR)], rows)):
            coef_ref[k, at, :] = value
        return 0

    lax.fori_loop(0, 8, plane, 0, unroll=4)


def halo_kernel(table_h, gas_h, index_h, *refs):
    halos, outs, (table, gas, index, rows, sem) = refs[:4], refs[4:8], refs[8:]
    for copy in fetch([(table_h, table), (gas_h, gas), (index_h, index)], sem):
        copy.wait()
    species_constants(table, gas, index, rows)
    for u_ref, out_ref in zip(halos, outs):
        def plane(i, _, u_ref=u_ref, out_ref=out_ref):
            at = pl.ds(pl.multiple_of(i * 8, 8), 8)
            for k, value in enumerate(halves([u_ref[k, at, :] for k in range(NVAR)], rows)):
                out_ref[k, at, :] = value
            return 0

        lax.fori_loop(0, 3, plane, 0, unroll=True)


def rate_kernel(wide, u_ref, coef_ref, ends_ref, *refs):
    halo_u, halo_c, out_h = refs[:4], refs[4:8], refs[8]
    (pm, mean, jumps, columns, fx, fy, fz, fold, out_ref, out_sem) = refs[9:]
    top = wide[0:8, :]
    for i in range(1, 32):
        top = jnp.maximum(top, wide[8 * i:8 * i + 8, :])
    top = jnp.max(top, axis=0, keepdims=True)
    lane = lax.broadcasted_iota(jnp.int32, (1, LANES), 1)
    speeds = []
    for d in range(3):
        one = jnp.max(jnp.where(lane == d, top, 0.0), axis=1, keepdims=True)
        speeds.append(jnp.broadcast_to(0.5 * one, (8, LANES)))
    scale = (0.5 * COURANT) / (speeds[0] + speeds[1] + speeds[2])

    def emit(flux, f, base):
        def put(k, value):
            flux[f, k] = value * (1.0 / 6.0) + base(k)

        return put

    def column(f, u, coef):
        up, down, m = split_fields(u, coef, (2, 0, 1), speeds[2])
        for k in range(24):
            mean[f, k] = m[k] + pltpu.roll(m[k], 1, 1)
        for k in range(15):
            before = pltpu.roll(up[k], 1, 1)
            step = up[k] - before
            for i, shift in enumerate((2, 1, 0, LANES - 1)):
                columns[f, 15 * i + k] = pltpu.roll(step, shift, 1) if shift else step
            pm[f, k] = before + down[k]
            step = down[k] - pltpu.roll(down[k], 1, 1)
            for i, shift in enumerate((1, 0, LANES - 1, LANES - 2)):
                columns[f, 60 + 15 * i + k] = pltpu.roll(step, shift, 1) if shift else step

    column(8, [ends_ref[k] for k in range(NVAR)], [ends_ref[NVAR + k] for k in range(12)])

    def plane(i, _):
        at = pl.ds(pl.multiple_of(i * 8, 8), 8)
        column(i, [u_ref[k, at, :] for k in range(NVAR)], [coef_ref[k, at, :] for k in range(12)])
        return 0

    lax.fori_loop(0, 8, plane, 0)

    def upright(f, _):
        face_flux(lambda k: mean[f, k], lambda k: 0.0,
                  lambda side, i, k: columns[f, 60 * side + 15 * (i - side) + k],
                  emit(fz, f, lambda k: pm[f, k]))
        return 0

    lax.fori_loop(0, 9, upright, 0)
    for d, order, strided, flux in ((0, (0, 1, 2), False, fx), (1, (1, 0, 2), True, fy)):
        def cell(i, u, coef, d=d, order=order):
            up, down, m = split_fields(u, coef, order, speeds[d])
            for k in range(24):
                mean[i, k] = m[k]
            for k in range(15):
                pm[i, k] = up[k]
                pm[i, 15 + k] = down[k]

        def own(i, _, cell=cell, strided=strided):
            at = pl.ds(i, 8, stride=8) if strided else pl.ds(pl.multiple_of(i * 8, 8), 8)
            cell(i + 3, [u_ref[k, at, :] for k in range(NVAR)],
                 [coef_ref[k, at, :] for k in range(12)])
            return 0

        lax.fori_loop(0, 8, own, 0, unroll=2)

        for high in range(2):
            def halo(i, _, cell=cell, d=d, high=high):
                at = pl.ds(pl.multiple_of(i * 8, 8), 8)
                cell(i + 11 * high, [halo_u[2 * d + high][k, at, :] for k in range(NVAR)],
                     [halo_c[2 * d + high][k, at, :] for k in range(12)])
                return 0

            lax.fori_loop(0, 3, halo, 0, unroll=True)

        def jump(i, _):
            for k in range(30):
                jumps[i, k] = pm[i + 1, k] - pm[i, k]
            return 0

        lax.fori_loop(0, 13, jump, 0, unroll=True)

        def face(f, _, flux=flux):
            face_flux(lambda k: mean[f + 2, k], lambda k: mean[f + 3, k],
                      lambda side, i, k: jumps[f + i, 15 * side + k],
                      emit(flux, f, lambda k: pm[f + 2, k] + pm[f + 3, 15 + k]))
            return 0

        lax.fori_loop(0, 9, face, 0)

    lane = lax.broadcasted_iota(jnp.int32, (8, LANES), 1)
    at_z = {9: 10, 10: 11, 11: 9}
    at_y = {9: 10, 10: 9, 11: 11}

    def row(j, _):
        at = pl.ds(j, 8, stride=8)
        for k in range(NVAR):
            ky = at_y.get(k, k)
            fold[k, at, :] = fy[j, ky] - fy[j + 1, ky]
        return 0

    lax.fori_loop(0, 8, row, 0)

    def store(i):
        at = pl.ds(pl.multiple_of(i * 8, 8), 8)
        return pltpu.make_async_copy(out_ref.at[:, at, :], out_h.at[:, at, :], out_sem.at[i])

    def plane(i, _):
        at = pl.ds(pl.multiple_of(i * 8, 8), 8)
        to_low = lax.rem(2 * LANES - 3 - 16 * i, LANES)
        to_high = lax.rem(2 * LANES - 13 - 16 * i, LANES)
        for k in range(NVAR):
            kz = at_z.get(k, k)
            ends = fz[8, kz]
            low = pltpu.roll(ends, to_low, 1)
            high = pltpu.roll(ends, to_high, 1)
            face = jnp.where(lane < 3, low, jnp.where(lane >= 126, high, fz[i, kz]))
            after = pltpu.roll(jnp.where(lane == 0, high, face), LANES - 1, 1)
            out_ref[k, at, :] = ((face - after) + (fx[i, k] - fx[i + 1, k]) + fold[k, at, :]) * scale
        store(i).start()
        return 0

    lax.fori_loop(0, 8, plane, 0)
    for i in range(8):
        store(i).wait()


HBM = pl.BlockSpec(memory_space=pltpu.MemorySpace.HBM)
VMEM = pl.BlockSpec(memory_space=pltpu.VMEM)
PLANES = (8, LANES)
TABLES = [pltpu.SMEM((6, 32), F32), pltpu.SMEM((32,), F32), pltpu.SMEM((NS,), jnp.int32),
          pltpu.VMEM((12 * NS,) + PLANES, F32)]


def struct(*shape):
    return jax.ShapeDtypeStruct(shape, F32)


def vmem(*shape):
    return pltpu.VMEM(shape, F32)


def dma(n):
    return pltpu.SemaphoreType.DMA((n,))


def params(mib=24):
    return pltpu.CompilerParams(vmem_limit_bytes=mib << 20)


def cells(table, gas, index, u):
    halo = struct(NVAR, 24, LANES)
    return pl.pallas_call(
        cell_kernel, name="cells", in_specs=[HBM] * 4, out_specs=[VMEM] * 5,
        out_shape=[struct(256, LANES), halo, halo, halo, halo],
        scratch_shapes=TABLES + [vmem(NVAR, 64, LANES), dma(4)],
        compiler_params=params(58))(table, gas, index, u)


def own_cells(table, gas, index, kind, u):
    return pl.pallas_call(
        own_kernel, name="own_cells", in_specs=[HBM] * 5, out_specs=[VMEM] * 2,
        out_shape=[struct(12, 64, LANES), struct(NVAR + 12, 8, LANES)],
        scratch_shapes=TABLES + [pltpu.SMEM((1, 2), jnp.int32), vmem(NVAR, 64, LANES), dma(5)],
        compiler_params=params())(table, gas, index, kind, u)


def halo_cells(table, gas, index, *halos):
    return pl.pallas_call(
        halo_kernel, name="halo_cells", in_specs=[HBM] * 3 + [VMEM] * 4, out_specs=[VMEM] * 4,
        out_shape=[struct(12, 24, LANES)] * 4, scratch_shapes=TABLES + [dma(3)],
        compiler_params=params())(table, gas, index, *halos)


def rates(wide, u, coef, ends, *halos):
    flux = vmem(9, NVAR, *PLANES)
    return pl.pallas_call(
        rate_kernel, name="rates", in_specs=[VMEM] * 12, out_specs=HBM,
        out_shape=struct(NVAR, 64, LANES),
        scratch_shapes=[
            vmem(14, 30, *PLANES), vmem(14, 24, *PLANES), vmem(13, 30, *PLANES),
            vmem(9, 120, *PLANES), flux, flux, flux,
            vmem(NVAR, 64, LANES), vmem(NVAR, 64, LANES), dma(8)],
        compiler_params=params())(wide, u, coef, ends, *halos)


AXES = ("z", "yl", "x", "yh", "c")
GX = ("z", "yl")
GY = ("x", "yh", "c")


def neighbours(start, end, axis):
    up = [(i, (i + 1) % 16) for i in range(16)]
    low = lax.ppermute(end, axis, up)
    high = lax.ppermute(start, axis, [(b, a) for a, b in up])
    return low, high


def shards(preserved_vector, nasa_table, gas_constant, species_index, face_kind):
    u = preserved_vector.reshape(NVAR, 64, LANES)
    fixed = (nasa_table.T, gas_constant, species_index)
    wide, xs, xe, ys, ye = cells(*fixed, u)
    wide = lax.all_to_all(wide, AXES, 0, 0, tiled=True)
    coef, ends = own_cells(*fixed, face_kind.reshape(1, 2), u)
    halos = neighbours(xs, xe, GX) + neighbours(ys, ye, GY)
    halo_coefs = halo_cells(*fixed, *halos)
    return rates(wide, u, coef, ends, *halos, *halo_coefs).reshape(preserved_vector.shape)


def solution(mesh):
    finer = Mesh(mesh.devices.reshape(8, 2, 4, 2, 2), AXES)
    placed = (P(None, GX, GY, None), P(), P(), P(), P(GX, GY, None))
    return jax.shard_map(
        shards, mesh=finer, in_specs=placed, out_specs=P(None, GX, GY, None), check_vma=False
    )
```

time: 86.9 us -> 49.8 us (0.57)
  the two profiles are of different devices: /device:TPU:8 before, /device:TPU:1 now
where the time goes in v3:
time: 49.8 us; the launch traced here: 49.7 us
  starting transfers between devices  24.3 us (49%)
  Pallas kernels  18.7 us (38%)
  waiting for transfers between devices  6.09 us (12%)
  local copies, waits for them, and re-layouts  0.59 us (1%)
    all_to_all x1, starting transfers between devices, shards(): wide = lax.all_to_all(wide, AXES, 0, 0, tiled=True)  15.7 us
    pallas_call x1, Pallas kernels, rates(): pl.pallas_call(rate_kernel, name='rates', in_specs=[VMEM] * 12, out_specs...  13 us
    ppermute x2, starting transfers between devices, neighbours(): low = lax.ppermute(end, axis, up)  4.51 us
    ppermute x2, starting transfers between devices, neighbours(): high = lax.ppermute(start, axis, [(b, a) for a, b in up])  4.09 us
    ppermute x2, waiting for transfers between devices, neighbours(): low = lax.ppermute(end, axis, up)  3.29 us
    ppermute x2, waiting for transfers between devices, neighbours(): high = lax.ppermute(start, axis, [(b, a) for a, b in up])  2.8 us
    pallas_call x1, Pallas kernels, cells(): pl.pallas_call(cell_kernel, name='cells', in_specs=[HBM] * 4, out_specs=[...  2.37 us
    pallas_call x1, Pallas kernels, own_cells(): pl.pallas_call(own_kernel, name='own_cells', in_specs=[HBM] * 5, out_spec...  2.04 us
  transfers between devices with their start and end apart: 5, of which 3 were waited for; matrix products, arithmetic and copies ran while one was open for 0% of the time, Pallas kernels for 7%

profile of v3, /device:TPU:1, one launch (start us, length us, event | category | flops | bytes accessed | tf_op | source)
XLA Modules:
  0.0 49.7 jit_solution(10570708273299791056)
XLA Ops:
  0.0 0.0 copy-start
  0.0 2.4 %cells.1 = (f32[256,128]{1,0:T(8,128)}, f32[14,24,128]{2,1,0:T(8,128)}, f32[14,24,128]{2,1,0:T(8,128)}, f32[14,24,128]{2,1,0:T(8,128)}, f32[14,24,128]{2,1,0:T(8,128)}) custom-call(f32[6,32]{1,0:T(8,128)} %bitcast.12, f32[32]{0:T(128)} %gas_h.5, s32[9]{0:T(128)} %index_h.5, f32[14,64,128]{2,1,0:T(8,128)} %bitcast.8), custom_call_target="tpu_custom_call" | custom-call | tf_op jit(solution)/shard_map/cells/pallas_call | solution.py:421
  2.4 0.0 copy-start.5
  2.4 15.7 %all-to-all-start = ((f32[256,1,128]{2,1,0:T(1,128)}), f32[256,1,128]{2,1,0:T(1,128)S(1)}, u32[]{:S(2)}, u32[]{:S(2)}) async-start(f32[256,1,128]{2,1,0:T(1,128)} %bitcast.16), calls=%async_computation | async-start | bytes 262144 | tf_op jit(solution)/shard_map/all_to_all | solution.py:471
  18.1 0.0 copy-start.1
  18.1 1.4 %collective-permute-start = (f32[14,24,128]{2,1,0:T(8,128)}, f32[14,24,128]{2,1,0:T(8,128)S(1)}, u32[]{:S(2)}, u32[]{:S(2)}) collective-permute-start(f32[14,24,128]{2,1,0:T(8,128)} %get-tuple-element.19), channel_id=1, source_target_pairs={{0,16},{16,32},{32,48},{48,64},{64,80},{80,96},{96,112},{112,128},... | collective-permute-start | bytes 516104 | tf_op jit(solution)/shard_map/ppermute | solution.py:462
  19.5 4.0 %collective-permute-start.1 = (f32[14,24,128]{2,1,0:T(8,128)}, f32[14,24,128]{2,1,0:T(8,128)S(1)}, u32[]{:S(2)}, u32[]{:S(2)}) collective-permute-start(f32[14,24,128]{2,1,0:T(8,128)} %get-tuple-element.20), channel_id=1, source_target_pairs={{16,0},{32,16},{48,32},{64,48},{80,64},{96,80},{112,96},{128,112},... | collective-permute-start | bytes 516104 | tf_op jit(solution)/shard_map/ppermute | solution.py:463
  23.5 3.1 %collective-permute-start.2 = (f32[14,24,128]{2,1,0:T(8,128)}, f32[14,24,128]{2,1,0:T(8,128)S(1)}, u32[]{:S(2)}, u32[]{:S(2)}) collective-permute-start(f32[14,24,128]{2,1,0:T(8,128)} %get-tuple-element.21), channel_id=1, source_target_pairs={{0,1},{1,2},{2,3},{3,4},{4,5},{5,6},{6,7},{7,8},{8,9},{9,10},{10,1... | collective-permute-start | bytes 516104 | tf_op jit(solution)/shard_map/ppermute | solution.py:462
  26.6 0.0 copy-done.5
  26.6 0.0 copy-start.2
  26.6 0.0 copy-start.3
  26.6 0.0 copy-start.4
  26.6 0.1 collective-permute-start.3
  26.7 0.0 copy-done
  26.7 0.0 copy-done.1
  26.7 0.5 %copy-done.2 = f32[32]{0:T(128)S(1)} copy-done((f32[32]{0:T(128)S(1)}, f32[32]{0:T(128)}, u32[]{:S(2)}) %copy-start.2) | copy-done | bytes 152
  27.2 0.0 copy-done.3
  27.3 0.0 copy-done.4
  27.3 2.0 %own_cells.1 = (f32[12,64,128]{2,1,0:T(8,128)S(1)}, f32[26,8,128]{2,1,0:T(8,128)S(1)}) custom-call(f32[6,32]{1,0:T(8,128)S(1)} %bitcast.13, f32[32]{0:T(128)S(1)} %copy-done.2, s32[9]{0:T(128)S(1)} %copy-done.3, s32[1,2]{1,0:T(1,128)S(1)} %bitcast.15, f32[14,64,128]{2,1,0:T(8,128)S(1)} %bitcast.9), custom_call_target="tpu_custom_call" | custom-call | tf_op jit(solution)/shard_map/own_cells/pallas_call | solution.py:429
  29.3 1.3 %collective-permute-done.refs_0_ = f32[14,24,128]{2,1,0:T(8,128)S(1)} collective-permute-done((f32[14,24,128]{2,1,0:T(8,128)}, f32[14,24,128]{2,1,0:T(8,128)S(1)}, u32[]{:S(2)}, u32[]{:S(2)}) %collective-permute-start) | collective-permute-done | bytes 172064 | tf_op jit(solution)/shard_map/ppermute | solution.py:462
  30.6 0.0 collective-permute-done.1.refs_1_
  30.6 2.0 %collective-permute-done.2.refs_2_ = f32[14,24,128]{2,1,0:T(8,128)S(1)} collective-permute-done((f32[14,24,128]{2,1,0:T(8,128)}, f32[14,24,128]{2,1,0:T(8,128)S(1)}, u32[]{:S(2)}, u32[]{:S(2)}) %collective-permute-start.2) | collective-permute-done | bytes 172064 | tf_op jit(solution)/shard_map/ppermute | solution.py:462
  32.6 2.8 %collective-permute-done.3.refs_3_ = f32[14,24,128]{2,1,0:T(8,128)S(1)} collective-permute-done((f32[14,24,128]{2,1,0:T(8,128)S(1)}, f32[14,24,128]{2,1,0:T(8,128)S(1)}, u32[]{:S(2)}, u32[]{:S(2)}) %collective-permute-start.3) | collective-permute-done | bytes 172064 | tf_op jit(solution)/shard_map/ppermute | solution.py:463
  35.4 1.3 %halo_cells.1 = (f32[12,24,128]{2,1,0:T(8,128)S(1)}, f32[12,24,128]{2,1,0:T(8,128)S(1)}, f32[12,24,128]{2,1,0:T(8,128)S(1)}, f32[12,24,128]{2,1,0:T(8,128)S(1)}) custom-call(f32[6,32]{1,0:T(8,128)S(1)} %bitcast.14, f32[32]{0:T(128)S(1)} %copy-done.2, s32[9]{0:T(128)S(1)} %copy-done.3, f32[14,24,128]{2,1,0:T(8,128)S(1)} %collective-permute-done.refs_0_, ...), custom_call_target="tpu_custom_call" | custom-call | tf_op jit(solution)/shard_map/halo_cells/pallas_call | solution.py:437
  36.7 0.0 all-to-all-done
  36.7 13.0 %rates.1 = f32[14,64,128]{2,1,0:T(8,128)} custom-call(f32[256,128]{1,0:T(8,128)S(1)} %bitcast.11, f32[14,64,128]{2,1,0:T(8,128)S(1)} %bitcast.10, f32[12,64,128]{2,1,0:T(8,128)S(1)} %get-tuple-element.17.coef_ref, f32[26,8,128]{2,1,0:T(8,128)S(1)} %get-tuple-element.18.ends_ref, f32[14,24,128]{2,1,0:T(8,128)S(1)} %collective-permute-done.refs_0_, ...), custom_call_target="tpu_custom_call" | custom-call | tf_op jit(solution)/shard_map/rates/pallas_call | solution.py:445
Async XLA Ops:
  0.0 26.7 %copy-start = (f32[14,8,8,128]{3,2,1,0:T(8,128)S(1)}, f32[14,8,8,128]{3,2,1,0:T(8,128)}, u32[]{:S(2)}) copy-start(f32[14,8,8,128]{3,2,1,0:T(8,128)} %param.5) | copy-start | bytes 1376260
  2.4 24.2 %copy-start.5 = (f32[14,24,128]{2,1,0:T(8,128)S(1)}, f32[14,24,128]{2,1,0:T(8,128)}, u32[]{:S(2)}) copy-start(f32[14,24,128]{2,1,0:T(8,128)} %get-tuple-element.22) | copy-start | bytes 516100
  2.4 34.3 %all-to-all-start = ((f32[256,1,128]{2,1,0:T(1,128)}), f32[256,1,128]{2,1,0:T(1,128)S(1)}, u32[]{:S(2)}, u32[]{:S(2)}) async-start(f32[256,1,128]{2,1,0:T(1,128)} %bitcast.16), calls=%async_computation | async-start | bytes 262144 | tf_op jit(solution)/shard_map/all_to_all | solution.py:471
  18.1 8.6 %copy-start.1 = (f32[32,6]{0,1:T(8,128)S(1)}, f32[32,6]{0,1:T(8,128)}, u32[]{:S(2)}) copy-start(f32[32,6]{0,1:T(8,128)} %param.6) | copy-start | bytes 2308
  18.1 12.6 %collective-permute-start = (f32[14,24,128]{2,1,0:T(8,128)}, f32[14,24,128]{2,1,0:T(8,128)S(1)}, u32[]{:S(2)}, u32[]{:S(2)}) collective-permute-start(f32[14,24,128]{2,1,0:T(8,128)} %get-tuple-element.19), channel_id=1, source_target_pairs={{0,16},{16,32},{32,48},{48,64},{64,80},{80,96},{96,112},{112,128},... | collective-permute-start | bytes 516104 | tf_op jit(solution)/shard_map/ppermute | solution.py:462
  19.5 11.1 %collective-permute-start.1 = (f32[14,24,128]{2,1,0:T(8,128)}, f32[14,24,128]{2,1,0:T(8,128)S(1)}, u32[]{:S(2)}, u32[]{:S(2)}) collective-permute-start(f32[14,24,128]{2,1,0:T(8,128)} %get-tuple-element.20), channel_id=1, source_target_pairs={{16,0},{32,16},{48,32},{64,48},{80,64},{96,80},{112,96},{128,112},... | collective-permute-start | bytes 516104 | tf_op jit(solution)/shard_map/ppermute | solution.py:463
  23.5 9.1 %collective-permute-start.2 = (f32[14,24,128]{2,1,0:T(8,128)}, f32[14,24,128]{2,1,0:T(8,128)S(1)}, u32[]{:S(2)}, u32[]{:S(2)}) collective-permute-start(f32[14,24,128]{2,1,0:T(8,128)} %get-tuple-element.21), channel_id=1, source_target_pairs={{0,1},{1,2},{2,3},{3,4},{4,5},{5,6},{6,7},{7,8},{8,9},{9,10},{10,1... | collective-permute-start | bytes 516104 | tf_op jit(solution)/shard_map/ppermute | solution.py:462
  26.6 0.7 %copy-start.2 = (f32[32]{0:T(128)S(1)}, f32[32]{0:T(128)}, u32[]{:S(2)}) copy-start(f32[32]{0:T(128)} %gas_h.5) | copy-start | bytes 388
  26.6 0.7 %copy-start.3 = (s32[9]{0:T(128)S(1)}, s32[9]{0:T(128)}, u32[]{:S(2)}) copy-start(s32[9]{0:T(128)} %index_h.5) | copy-start | bytes 112
  26.6 0.7 %copy-start.4 = (s32[1,1,2]{2,1,0:T(1,128)S(1)}, s32[1,1,2]{2,1,0:T(1,128)}, u32[]{:S(2)}) copy-start(s32[1,1,2]{2,1,0:T(1,128)} %param.9) | copy-start | bytes 28
  26.6 8.8 %collective-permute-start.3 = (f32[14,24,128]{2,1,0:T(8,128)S(1)}, f32[14,24,128]{2,1,0:T(8,128)S(1)}, u32[]{:S(2)}, u32[]{:S(2)}) collective-permute-start(f32[14,24,128]{2,1,0:T(8,128)S(1)} %copy-done.5), channel_id=1, source_target_pairs={{1,0},{2,1},{3,2},{4,3},{5,4},{6,5},{7,6},{8,7},{9,8},{10,9},{11,1... | collective-permute-start | bytes 516104 | tf_op jit(solution)/shard_map/ppermute | solution.py:463

commit v4 on v3

--- a/solution.py
+++ b/solution.py
@@ -265,9 +265,14 @@
         lax.fori_loop(0, 3, plane, 0, unroll=True)
 
 
-def rate_kernel(wide, u_ref, coef_ref, ends_ref, *refs):
-    halo_u, halo_c, out_h = refs[:4], refs[4:8], refs[8]
-    (pm, mean, jumps, columns, fx, fy, fz, fold, out_ref, out_sem) = refs[9:]
+def emit(flux, f, base):
+    def put(k, value):
+        flux[f, k] = value * (1.0 / 6.0) + base(k)
+
+    return put
+
+
+def column_kernel(wide, u_ref, coef_ref, ends_ref, out_ref, speed_ref, pm, mean, columns, fz):
     top = wide[0:8, :]
     for i in range(1, 32):
         top = jnp.maximum(top, wide[8 * i:8 * i + 8, :])
@@ -277,13 +282,9 @@
     for d in range(3):
         one = jnp.max(jnp.where(lane == d, top, 0.0), axis=1, keepdims=True)
         speeds.append(jnp.broadcast_to(0.5 * one, (8, LANES)))
-    scale = (0.5 * COURANT) / (speeds[0] + speeds[1] + speeds[2])
-
-    def emit(flux, f, base):
-        def put(k, value):
-            flux[f, k] = value * (1.0 / 6.0) + base(k)
-
-        return put
+    for d in range(3):
+        speed_ref[d] = speeds[d]
+    speed_ref[3] = (0.5 * COURANT) / (speeds[0] + speeds[1] + speeds[2])
 
     def column(f, u, coef):
         up, down, m = split_fields(u, coef, (2, 0, 1), speeds[2])
@@ -315,65 +316,10 @@
         return 0
 
     lax.fori_loop(0, 9, upright, 0)
-    for d, order, strided, flux in ((0, (0, 1, 2), False, fx), (1, (1, 0, 2), True, fy)):
-        def cell(i, u, coef, d=d, order=order):
-            up, down, m = split_fields(u, coef, order, speeds[d])
-            for k in range(24):
-                mean[i, k] = m[k]
-            for k in range(15):
-                pm[i, k] = up[k]
-                pm[i, 15 + k] = down[k]
-
-        def own(i, _, cell=cell, strided=strided):
-            at = pl.ds(i, 8, stride=8) if strided else pl.ds(pl.multiple_of(i * 8, 8), 8)
-            cell(i + 3, [u_ref[k, at, :] for k in range(NVAR)],
-                 [coef_ref[k, at, :] for k in range(12)])
-            return 0
-
-        lax.fori_loop(0, 8, own, 0, unroll=2)
-
-        for high in range(2):
-            def halo(i, _, cell=cell, d=d, high=high):
-                at = pl.ds(pl.multiple_of(i * 8, 8), 8)
-                cell(i + 11 * high, [halo_u[2 * d + high][k, at, :] for k in range(NVAR)],
-                     [halo_c[2 * d + high][k, at, :] for k in range(12)])
-                return 0
-
-            lax.fori_loop(0, 3, halo, 0, unroll=True)
-
-        def jump(i, _):
-            for k in range(30):
-                jumps[i, k] = pm[i + 1, k] - pm[i, k]
-            return 0
-
-        lax.fori_loop(0, 13, jump, 0, unroll=True)
-
-        def face(f, _, flux=flux):
-            face_flux(lambda k: mean[f + 2, k], lambda k: mean[f + 3, k],
-                      lambda side, i, k: jumps[f + i, 15 * side + k],
-                      emit(flux, f, lambda k: pm[f + 2, k] + pm[f + 3, 15 + k]))
-            return 0
-
-        lax.fori_loop(0, 9, face, 0)
-
     lane = lax.broadcasted_iota(jnp.int32, (8, LANES), 1)
     at_z = {9: 10, 10: 11, 11: 9}
-    at_y = {9: 10, 10: 9, 11: 11}
-
-    def row(j, _):
-        at = pl.ds(j, 8, stride=8)
-        for k in range(NVAR):
-            ky = at_y.get(k, k)
-            fold[k, at, :] = fy[j, ky] - fy[j + 1, ky]
-        return 0
-
-    lax.fori_loop(0, 8, row, 0)
-
-    def store(i):
-        at = pl.ds(pl.multiple_of(i * 8, 8), 8)
-        return pltpu.make_async_copy(out_ref.at[:, at, :], out_h.at[:, at, :], out_sem.at[i])
-
-    def plane(i, _):
+
+    def merge(i, _):
         at = pl.ds(pl.multiple_of(i * 8, 8), 8)
         to_low = lax.rem(2 * LANES - 3 - 16 * i, LANES)
         to_high = lax.rem(2 * LANES - 13 - 16 * i, LANES)
@@ -384,7 +330,77 @@
             high = pltpu.roll(ends, to_high, 1)
             face = jnp.where(lane < 3, low, jnp.where(lane >= 126, high, fz[i, kz]))
             after = pltpu.roll(jnp.where(lane == 0, high, face), LANES - 1, 1)
-            out_ref[k, at, :] = ((face - after) + (fx[i, k] - fx[i + 1, k]) + fold[k, at, :]) * scale
+            out_ref[k, at, :] = face - after
+        return 0
+
+    lax.fori_loop(0, 8, merge, 0)
+
+
+def rate_kernel(speed_ref, u_ref, coef_ref, z_ref, *refs):
+    halo_u, halo_c, out_h = refs[:4], refs[4:8], refs[8]
+    (pm, mean, jumps, fx, fy, fold, out_ref, out_sem) = refs[9:]
+    speeds = [speed_ref[d] for d in range(2)]
+    scale = speed_ref[3]
+    for d, order, strided, flux in ((0, (0, 1, 2), False, fx), (1, (1, 0, 2), True, fy)):
+        def cell(i, u, coef, d=d, order=order):
+            up, down, m = split_fields(u, coef, order, speeds[d])
+            for k in range(24):
+                mean[i, k] = m[k]
+            for k in range(15):
+                pm[i, k] = up[k]
+                pm[i, 15 + k] = down[k]
+
+        def own(i, _, cell=cell, strided=strided):
+            at = pl.ds(i, 8, stride=8) if strided else pl.ds(pl.multiple_of(i * 8, 8), 8)
+            cell(i + 3, [u_ref[k, at, :] for k in range(NVAR)],
+                 [coef_ref[k, at, :] for k in range(12)])
+            return 0
+
+        lax.fori_loop(0, 8, own, 0, unroll=2)
+
+        for high in range(2):
+            def halo(i, _, cell=cell, d=d, high=high):
+                at = pl.ds(pl.multiple_of(i * 8, 8), 8)
+                cell(i + 11 * high, [halo_u[2 * d + high][k, at, :] for k in range(NVAR)],
+                     [halo_c[2 * d + high][k, at, :] for k in range(12)])
+                return 0
+
+            lax.fori_loop(0, 3, halo, 0, unroll=True)
+
+        def jump(i, _):
+            for k in range(30):
+                jumps[i, k] = pm[i + 1, k] - pm[i, k]
+            return 0
+
+        lax.fori_loop(0, 13, jump, 0, unroll=True)
+
+        def face(f, _, flux=flux):
+            face_flux(lambda k: mean[f + 2, k], lambda k: mean[f + 3, k],
+                      lambda side, i, k: jumps[f + i, 15 * side + k],
+                      emit(flux, f, lambda k: pm[f + 2, k] + pm[f + 3, 15 + k]))
+            return 0
+
+        lax.fori_loop(0, 9, face, 0)
+
+    at_y = {9: 10, 10: 9, 11: 11}
+
+    def row(j, _):
+        at = pl.ds(j, 8, stride=8)
+        for k in range(NVAR):
+            ky = at_y.get(k, k)
+            fold[k, at, :] = fy[j, ky] - fy[j + 1, ky]
+        return 0
+
+    lax.fori_loop(0, 8, row, 0)
+
+    def store(i):
+        at = pl.ds(pl.multiple_of(i * 8, 8), 8)
+        return pltpu.make_async_copy(out_ref.at[:, at, :], out_h.at[:, at, :], out_sem.at[i])
+
+    def plane(i, _):
+        at = pl.ds(pl.multiple_of(i * 8, 8), 8)
+        for k in range(NVAR):
+            out_ref[k, at, :] = (z_ref[k, at, :] + (fx[i, k] - fx[i + 1, k]) + fold[k, at, :]) * scale
         store(i).start()
         return 0
 
@@ -412,7 +428,7 @@
     return pltpu.SemaphoreType.DMA((n,))
 
 
-def params(mib=24):
+def params(mib=20):
     return pltpu.CompilerParams(vmem_limit_bytes=mib << 20)
 
 
@@ -440,16 +456,24 @@
         compiler_params=params())(table, gas, index, *halos)
 
 
-def rates(wide, u, coef, ends, *halos):
+def columns(wide, u, coef, ends):
+    return pl.pallas_call(
+        column_kernel, name="columns", in_specs=[VMEM] * 4, out_specs=[VMEM] * 2,
+        out_shape=[struct(NVAR, 64, LANES), struct(4, 8, LANES)],
+        scratch_shapes=[vmem(9, 15, *PLANES), vmem(9, 24, *PLANES), vmem(9, 120, *PLANES),
+                        vmem(9, NVAR, *PLANES)],
+        compiler_params=params())(wide, u, coef, ends)
+
+
+def rates(speed, u, coef, z, *halos):
     flux = vmem(9, NVAR, *PLANES)
     return pl.pallas_call(
         rate_kernel, name="rates", in_specs=[VMEM] * 12, out_specs=HBM,
         out_shape=struct(NVAR, 64, LANES),
         scratch_shapes=[
-            vmem(14, 30, *PLANES), vmem(14, 24, *PLANES), vmem(13, 30, *PLANES),
-            vmem(9, 120, *PLANES), flux, flux, flux,
+            vmem(14, 30, *PLANES), vmem(14, 24, *PLANES), vmem(13, 30, *PLANES), flux, flux,
             vmem(NVAR, 64, LANES), vmem(NVAR, 64, LANES), dma(8)],
-        compiler_params=params())(wide, u, coef, ends, *halos)
+        compiler_params=params())(speed, u, coef, z, *halos)
 
 
 AXES = ("z", "yl", "x", "yh", "c")
@@ -471,8 +495,9 @@
     wide = lax.all_to_all(wide, AXES, 0, 0, tiled=True)
     coef, ends = own_cells(*fixed, face_kind.reshape(1, 2), u)
     halos = neighbours(xs, xe, GX) + neighbours(ys, ye, GY)
+    z, speed = columns(wide, u, coef, ends)
     halo_coefs = halo_cells(*fixed, *halos)
-    return rates(wide, u, coef, ends, *halos, *halo_coefs).reshape(preserved_vector.shape)
+    return rates(speed, u, coef, z, *halos, *halo_coefs).reshape(preserved_vector.shape)
 
 
 def solution(mesh):

time: 49.8 us -> 50 us (level)
    pallas_call x0 -> x1, Pallas kernels: none -> 6.56 us  [columns(): pl.pallas_call(column_kernel, name='columns', in_specs=[VMEM] * 4, out_sp...]
    pallas_call x1, Pallas kernels: 13 us -> 6.59 us  [rates(): pl.pallas_call(rate_kernel, name='rates', in_specs=[VMEM] * 12, out_specs...]
where the time goes in v4:
time: 50 us; the launch traced here: 49.9 us
  starting transfers between devices  24.3 us (49%)
  Pallas kernels  18.9 us (38%)
  waiting for transfers between devices  6.08 us (12%)
  local copies, waits for them, and re-layouts  0.59 us (1%)
    all_to_all x1, starting transfers between devices, shards(): wide = lax.all_to_all(wide, AXES, 0, 0, tiled=True)  15.7 us
    pallas_call x1, Pallas kernels, rates(): pl.pallas_call(rate_kernel, name='rates', in_specs=[VMEM] * 12, out_specs...  6.59 us
    pallas_call x1, Pallas kernels, columns(): pl.pallas_call(column_kernel, name='columns', in_specs=[VMEM] * 4, out_sp...  6.56 us
    ppermute x2, starting transfers between devices, neighbours(): low = lax.ppermute(end, axis, up)  4.51 us
    ppermute x2, starting transfers between devices, neighbours(): high = lax.ppermute(start, axis, [(b, a) for a, b in up])  4.09 us
    ppermute x2, waiting for transfers between devices, neighbours(): low = lax.ppermute(end, axis, up)  3.28 us
    ppermute x2, waiting for transfers between devices, neighbours(): high = lax.ppermute(start, axis, [(b, a) for a, b in up])  2.8 us
    pallas_call x1, Pallas kernels, cells(): pl.pallas_call(cell_kernel, name='cells', in_specs=[HBM] * 4, out_specs=[...  2.4 us
  transfers between devices with their start and end apart: 5, of which 3 were waited for; matrix products, arithmetic and copies ran while one was open for 0% of the time, Pallas kernels for 7%

profile of v4, /device:TPU:1, one launch (start us, length us, event | category | flops | bytes accessed | tf_op | source)
XLA Modules:
  0.0 49.9 jit_solution(7558883488636533713)
XLA Ops:
  0.0 0.0 copy-start
  0.0 2.4 %cells.1 = (f32[256,128]{1,0:T(8,128)}, f32[14,24,128]{2,1,0:T(8,128)}, f32[14,24,128]{2,1,0:T(8,128)}, f32[14,24,128]{2,1,0:T(8,128)}, f32[14,24,128]{2,1,0:T(8,128)}) custom-call(f32[6,32]{1,0:T(8,128)} %bitcast.13, f32[32]{0:T(128)} %gas_h.5, s32[9]{0:T(128)} %index_h.5, f32[14,64,128]{2,1,0:T(8,128)} %bitcast.8), custom_call_target="tpu_custom_call" | custom-call | tf_op jit(solution)/shard_map/cells/pallas_call | solution.py:437
  2.4 0.0 copy-start.5
  2.4 15.7 %all-to-all-start = ((f32[256,1,128]{2,1,0:T(1,128)}), f32[256,1,128]{2,1,0:T(1,128)S(1)}, u32[]{:S(2)}, u32[]{:S(2)}) async-start(f32[256,1,128]{2,1,0:T(1,128)} %bitcast.17), calls=%async_computation | async-start | bytes 262144 | tf_op jit(solution)/shard_map/all_to_all | solution.py:495
  18.1 0.0 copy-start.1
  18.1 1.4 %collective-permute-start = (f32[14,24,128]{2,1,0:T(8,128)}, f32[14,24,128]{2,1,0:T(8,128)S(1)}, u32[]{:S(2)}, u32[]{:S(2)}) collective-permute-start(f32[14,24,128]{2,1,0:T(8,128)} %get-tuple-element.23), channel_id=1, source_target_pairs={{0,16},{16,32},{32,48},{48,64},{64,80},{80,96},{96,112},{112,128},... | collective-permute-start | bytes 516104 | tf_op jit(solution)/shard_map/ppermute | solution.py:486
  19.5 4.0 %collective-permute-start.1 = (f32[14,24,128]{2,1,0:T(8,128)}, f32[14,24,128]{2,1,0:T(8,128)S(1)}, u32[]{:S(2)}, u32[]{:S(2)}) collective-permute-start(f32[14,24,128]{2,1,0:T(8,128)} %get-tuple-element.24), channel_id=1, source_target_pairs={{16,0},{32,16},{48,32},{64,48},{80,64},{96,80},{112,96},{128,112},... | collective-permute-start | bytes 516104 | tf_op jit(solution)/shard_map/ppermute | solution.py:487
  23.5 3.1 %collective-permute-start.2 = (f32[14,24,128]{2,1,0:T(8,128)}, f32[14,24,128]{2,1,0:T(8,128)S(1)}, u32[]{:S(2)}, u32[]{:S(2)}) collective-permute-start(f32[14,24,128]{2,1,0:T(8,128)} %get-tuple-element.25), channel_id=1, source_target_pairs={{0,1},{1,2},{2,3},{3,4},{4,5},{5,6},{6,7},{7,8},{8,9},{9,10},{10,1... | collective-permute-start | bytes 516104 | tf_op jit(solution)/shard_map/ppermute | solution.py:486
  26.6 0.0 copy-done.5
  26.6 0.0 copy-start.2
  26.6 0.0 copy-start.3
  26.6 0.0 copy-start.4
  26.6 0.1 collective-permute-start.3
  26.7 0.0 copy-done
  26.7 0.0 copy-done.1
  26.7 0.5 %copy-done.2 = f32[32]{0:T(128)S(1)} copy-done((f32[32]{0:T(128)S(1)}, f32[32]{0:T(128)}, u32[]{:S(2)}) %copy-start.2) | copy-done | bytes 152
  27.3 0.0 copy-done.3
  27.3 0.0 copy-done.4
  27.3 2.1 %own_cells.1 = (f32[12,64,128]{2,1,0:T(8,128)S(1)}, f32[26,8,128]{2,1,0:T(8,128)S(1)}) custom-call(f32[6,32]{1,0:T(8,128)S(1)} %bitcast.14, f32[32]{0:T(128)S(1)} %copy-done.2, s32[9]{0:T(128)S(1)} %copy-done.3, s32[1,2]{1,0:T(1,128)S(1)} %bitcast.16, f32[14,64,128]{2,1,0:T(8,128)S(1)} %bitcast.9), custom_call_target="tpu_custom_call" | custom-call | tf_op jit(solution)/shard_map/own_cells/pallas_call | solution.py:445
  29.4 1.3 %collective-permute-done.refs_0_ = f32[14,24,128]{2,1,0:T(8,128)S(1)} collective-permute-done((f32[14,24,128]{2,1,0:T(8,128)}, f32[14,24,128]{2,1,0:T(8,128)S(1)}, u32[]{:S(2)}, u32[]{:S(2)}) %collective-permute-start) | collective-permute-done | bytes 172064 | tf_op jit(solution)/shard_map/ppermute | solution.py:486
  30.7 0.0 collective-permute-done.1.refs_1_
  30.7 2.0 %collective-permute-done.2.refs_2_ = f32[14,24,128]{2,1,0:T(8,128)S(1)} collective-permute-done((f32[14,24,128]{2,1,0:T(8,128)}, f32[14,24,128]{2,1,0:T(8,128)S(1)}, u32[]{:S(2)}, u32[]{:S(2)}) %collective-permute-start.2) | collective-permute-done | bytes 172064 | tf_op jit(solution)/shard_map/ppermute | solution.py:486
  32.6 2.8 %collective-permute-done.3.refs_3_ = f32[14,24,128]{2,1,0:T(8,128)S(1)} collective-permute-done((f32[14,24,128]{2,1,0:T(8,128)S(1)}, f32[14,24,128]{2,1,0:T(8,128)S(1)}, u32[]{:S(2)}, u32[]{:S(2)}) %collective-permute-start.3) | collective-permute-done | bytes 172064 | tf_op jit(solution)/shard_map/ppermute | solution.py:487
  35.4 1.3 %halo_cells.1 = (f32[12,24,128]{2,1,0:T(8,128)S(1)}, f32[12,24,128]{2,1,0:T(8,128)S(1)}, f32[12,24,128]{2,1,0:T(8,128)S(1)}, f32[12,24,128]{2,1,0:T(8,128)S(1)}) custom-call(f32[6,32]{1,0:T(8,128)S(1)} %bitcast.15, f32[32]{0:T(128)S(1)} %copy-done.2, s32[9]{0:T(128)S(1)} %copy-done.3, f32[14,24,128]{2,1,0:T(8,128)S(1)} %collective-permute-done.refs_0_, ...), custom_call_target="tpu_custom_call" | custom-call | tf_op jit(solution)/shard_map/halo_cells/pallas_call | solution.py:453
  36.7 0.0 all-to-all-done
  36.7 6.6 %columns.1 = (f32[14,64,128]{2,1,0:T(8,128)S(1)}, f32[4,8,128]{2,1,0:T(8,128)S(1)}) custom-call(f32[256,128]{1,0:T(8,128)S(1)} %bitcast.12, f32[14,64,128]{2,1,0:T(8,128)S(1)} %bitcast.10, f32[12,64,128]{2,1,0:T(8,128)S(1)} %get-tuple-element.19.coef_ref, f32[26,8,128]{2,1,0:T(8,128)S(1)} %get-tuple-element.20.ends_ref), custom_call_target="tpu_custom_call" | custom-call | tf_op jit(solution)/shard_map/columns/pallas_call | solution.py:460
  43.3 6.6 %rates.1 = f32[14,64,128]{2,1,0:T(8,128)} custom-call(f32[4,8,128]{2,1,0:T(8,128)S(1)} %get-tuple-element.21.speed_ref, f32[14,64,128]{2,1,0:T(8,128)S(1)} %bitcast.11, f32[12,64,128]{2,1,0:T(8,128)S(1)} %get-tuple-element.19.coef_ref, f32[14,64,128]{2,1,0:T(8,128)S(1)} %get-tuple-element.22.z_ref, f32[14,24,128]{2,1,0:T(8,128)S(1)} %collective-permute-done.refs_0_, ...), custom_call_target="tpu_custom_call" | custom-call | tf_op jit(solution)/shard_map/rates/pallas_call | solution.py:470
Async XLA Ops:
  0.0 26.7 %copy-start = (f32[14,8,8,128]{3,2,1,0:T(8,128)S(1)}, f32[14,8,8,128]{3,2,1,0:T(8,128)}, u32[]{:S(2)}) copy-start(f32[14,8,8,128]{3,2,1,0:T(8,128)} %param.5) | copy-start | bytes 1376260
  2.4 24.2 %copy-start.5 = (f32[14,24,128]{2,1,0:T(8,128)S(1)}, f32[14,24,128]{2,1,0:T(8,128)}, u32[]{:S(2)}) copy-start(f32[14,24,128]{2,1,0:T(8,128)} %get-tuple-element.26) | copy-start | bytes 516100
  2.4 34.3 %all-to-all-start = ((f32[256,1,128]{2,1,0:T(1,128)}), f32[256,1,128]{2,1,0:T(1,128)S(1)}, u32[]{:S(2)}, u32[]{:S(2)}) async-start(f32[256,1,128]{2,1,0:T(1,128)} %bitcast.17), calls=%async_computation | async-start | bytes 262144 | tf_op jit(solution)/shard_map/all_to_all | solution.py:495
  18.1 8.6 %copy-start.1 = (f32[32,6]{0,1:T(8,128)S(1)}, f32[32,6]{0,1:T(8,128)}, u32[]{:S(2)}) copy-start(f32[32,6]{0,1:T(8,128)} %param.6) | copy-start | bytes 2308
  18.1 12.6 %collective-permute-start = (f32[14,24,128]{2,1,0:T(8,128)}, f32[14,24,128]{2,1,0:T(8,128)S(1)}, u32[]{:S(2)}, u32[]{:S(2)}) collective-permute-start(f32[14,24,128]{2,1,0:T(8,128)} %get-tuple-element.23), channel_id=1, source_target_pairs={{0,16},{16,32},{32,48},{48,64},{64,80},{80,96},{96,112},{112,128},... | collective-permute-start | bytes 516104 | tf_op jit(solution)/shard_map/ppermute | solution.py:486
  19.5 11.2 %collective-permute-start.1 = (f32[14,24,128]{2,1,0:T(8,128)}, f32[14,24,128]{2,1,0:T(8,128)S(1)}, u32[]{:S(2)}, u32[]{:S(2)}) collective-permute-start(f32[14,24,128]{2,1,0:T(8,128)} %get-tuple-element.24), channel_id=1, source_target_pairs={{16,0},{32,16},{48,32},{64,48},{80,64},{96,80},{112,96},{128,112},... | collective-permute-start | bytes 516104 | tf_op jit(solution)/shard_map/ppermute | solution.py:487
  23.5 9.1 %collective-permute-start.2 = (f32[14,24,128]{2,1,0:T(8,128)}, f32[14,24,128]{2,1,0:T(8,128)S(1)}, u32[]{:S(2)}, u32[]{:S(2)}) collective-permute-start(f32[14,24,128]{2,1,0:T(8,128)} %get-tuple-element.25), channel_id=1, source_target_pairs={{0,1},{1,2},{2,3},{3,4},{4,5},{5,6},{6,7},{7,8},{8,9},{9,10},{10,1... | collective-permute-start | bytes 516104 | tf_op jit(solution)/shard_map/ppermute | solution.py:486
  26.6 0.7 %copy-start.2 = (f32[32]{0:T(128)S(1)}, f32[32]{0:T(128)}, u32[]{:S(2)}) copy-start(f32[32]{0:T(128)} %gas_h.5) | copy-start | bytes 388
  26.6 0.7 %copy-start.3 = (s32[9]{0:T(128)S(1)}, s32[9]{0:T(128)}, u32[]{:S(2)}) copy-start(s32[9]{0:T(128)} %index_h.5) | copy-start | bytes 112
  26.6 0.7 %copy-start.4 = (s32[1,1,2]{2,1,0:T(1,128)S(1)}, s32[1,1,2]{2,1,0:T(1,128)}, u32[]{:S(2)}) copy-start(s32[1,1,2]{2,1,0:T(1,128)} %param.9) | copy-start | bytes 28
  26.6 8.8 %collective-permute-start.3 = (f32[14,24,128]{2,1,0:T(8,128)S(1)}, f32[14,24,128]{2,1,0:T(8,128)S(1)}, u32[]{:S(2)}, u32[]{:S(2)}) collective-permute-start(f32[14,24,128]{2,1,0:T(8,128)S(1)} %copy-done.5), channel_id=1, source_target_pairs={{1,0},{2,1},{3,2},{4,3},{5,4},{6,5},{7,6},{8,7},{9,8},{10,9},{11,1... | collective-permute-start | bytes 516104 | tf_op jit(solution)/shard_map/ppermute | solution.py:487

commit v5 on v4

--- a/solution.py
+++ b/solution.py
@@ -203,43 +203,41 @@
     put(12, energy + square * total - (dot * (c * c)) * ig)
 
 
-def own_kernel(table_h, gas_h, index_h, kind_h, u_h, coef_ref, ends_ref,
-               table, gas, index, rows, kind, u_ref, sem):
-    for copy in fetch([(table_h, table), (gas_h, gas), (index_h, index), (kind_h, kind),
-                       (u_h, u_ref)], sem):
+def own_kernel(table_h, gas_h, index_h, kind_h, u_ref, coef_ref, tall_ref, tall_coef, const_ref,
+               table, gas, index, rows, kind, turned, sem):
+    copies = fetch([(kind_h, kind), (table_h, table), (gas_h, gas), (index_h, index)], sem)
+    copies[0].wait()
+    sub = lax.broadcasted_iota(jnp.int32, (8, LANES), 0)
+    lane = lax.broadcasted_iota(jnp.int32, (8, LANES), 1)
+    left = lane < 64
+    low_wall = kind[0, 0] == 1
+    high_wall = kind[0, 1] == 1
+    for pair in range(NVAR // 2):
+        turned[pair] = jnp.concatenate([u_ref[2 * pair], u_ref[2 * pair + 1]], axis=0).T
+    for k in range(NVAR):
+        pair, second = divmod(k, 2)
+        for b in range(8):
+            top = turned[pair, pl.ds(b, 8, stride=8), :]
+            bottom = turned[pair, pl.ds(64 + b, 8, stride=8), :]
+            if second:
+                tall_ref[k, b + 3] = jnp.where(left, pltpu.roll(top, 64, 1), bottom)
+            else:
+                tall_ref[k, b + 3] = jnp.where(left, top, pltpu.roll(bottom, 64, 1))
+        sign = -1.0 if k == NS + 2 else 1.0
+        for ghost in range(3):
+            down = pltpu.roll(tall_ref[k, 10 - ghost], 1, 0)
+            edge = jnp.where(low_wall, tall_ref[k, 3 + ghost] * sign, tall_ref[k, 3])
+            edge = jnp.where(left, edge, pltpu.roll(down, 64, 1))
+            tall_ref[k, 2 - ghost] = jnp.where(sub == 0, edge, down)
+            up = pltpu.roll(tall_ref[k, 3 + ghost], 7, 0)
+            edge = jnp.where(high_wall, tall_ref[k, 10 - ghost] * sign, tall_ref[k, 10])
+            edge = jnp.where(left, pltpu.roll(up, 64, 1), edge)
+            tall_ref[k, 11 + ghost] = jnp.where(sub == 7, edge, up)
+    for copy in copies[1:]:
         copy.wait()
     species_constants(table, gas, index, rows)
-    lane = lax.broadcasted_iota(jnp.int32, (8, LANES), 1)
-    slot = lane % 16
-    group = lane // 16
-    low_wall = kind[0, 0] == 1
-    high_wall = kind[0, 1] == 1
-
-    def pick(k):
-        packed = jnp.zeros((8, LANES), F32)
-        for plane in range(8):
-            v = u_ref[k, 8 * plane:8 * plane + 8, :]
-            low = pltpu.roll(v, (16 * plane + 3) % LANES, 1)
-            high = pltpu.roll(v, (16 * plane + 8 - 123) % LANES, 1)
-            packed = jnp.where(group == plane, jnp.where(slot < 8, low, high), packed)
-
-        def at(shift):
-            return pltpu.roll(packed, shift % LANES, 1)
-
-        sign = -1.0 if k == NS + 2 else 1.0
-        mirror = jnp.where(slot == 2, at(-1), jnp.where(slot == 1, at(-3), at(-5))) * sign
-        copy = jnp.where(slot == 2, at(-1), jnp.where(slot == 1, at(-2), at(-3)))
-        low = jnp.where(low_wall, mirror, copy)
-        mirror = jnp.where(slot == 13, at(1), jnp.where(slot == 14, at(3), at(5))) * sign
-        copy = jnp.where(slot == 13, at(1), jnp.where(slot == 14, at(2), at(3)))
-        high = jnp.where(high_wall, mirror, copy)
-        ends_ref[k] = jnp.where(slot < 3, low, jnp.where(slot > 12, high, packed))
-        return 0
-
-    for k in range(NVAR):
-        pick(k)
-    for k, value in enumerate(halves([ends_ref[k] for k in range(NVAR)], rows)):
-        ends_ref[NVAR + k] = value
+    for k in range(12 * NS):
+        const_ref[k] = rows[k, 0:1, :]
 
     def plane(i, _):
         at = pl.ds(pl.multiple_of(i * 8, 8), 8)
@@ -249,20 +247,12 @@
 
     lax.fori_loop(0, 8, plane, 0, unroll=4)
 
-
-def halo_kernel(table_h, gas_h, index_h, *refs):
-    halos, outs, (table, gas, index, rows, sem) = refs[:4], refs[4:8], refs[8:]
-    for copy in fetch([(table_h, table), (gas_h, gas), (index_h, index)], sem):
-        copy.wait()
-    species_constants(table, gas, index, rows)
-    for u_ref, out_ref in zip(halos, outs):
-        def plane(i, _, u_ref=u_ref, out_ref=out_ref):
-            at = pl.ds(pl.multiple_of(i * 8, 8), 8)
-            for k, value in enumerate(halves([u_ref[k, at, :] for k in range(NVAR)], rows)):
-                out_ref[k, at, :] = value
-            return 0
-
-        lax.fori_loop(0, 3, plane, 0, unroll=True)
+    def tall(i, _):
+        for k, value in enumerate(halves([tall_ref[k, i] for k in range(NVAR)], rows)):
+            tall_coef[k, i] = value
+        return 0
+
+    lax.fori_loop(0, 14, tall, 0, unroll=4 if 14 % 4 == 0 else 2)
 
 
 def emit(flux, f, base):
@@ -272,7 +262,7 @@
     return put
 
 
-def column_kernel(wide, u_ref, coef_ref, ends_ref, out_ref, speed_ref, pm, mean, columns, fz):
+def column_kernel(wide, tall_ref, tall_coef, out_ref, speed_ref, pm, mean, jumps, fz, turned):
     top = wide[0:8, :]
     for i in range(1, 32):
         top = jnp.maximum(top, wide[8 * i:8 * i + 8, :])
@@ -286,59 +276,50 @@
         speed_ref[d] = speeds[d]
     speed_ref[3] = (0.5 * COURANT) / (speeds[0] + speeds[1] + speeds[2])
 
-    def column(f, u, coef):
-        up, down, m = split_fields(u, coef, (2, 0, 1), speeds[2])
+    def cell(i, _):
+        up, down, m = split_fields([tall_ref[k, i] for k in range(NVAR)],
+                                   [tall_coef[k, i] for k in range(12)], (2, 0, 1), speeds[2])
         for k in range(24):
-            mean[f, k] = m[k] + pltpu.roll(m[k], 1, 1)
+            mean[i, k] = m[k]
         for k in range(15):
-            before = pltpu.roll(up[k], 1, 1)
-            step = up[k] - before
-            for i, shift in enumerate((2, 1, 0, LANES - 1)):
-                columns[f, 15 * i + k] = pltpu.roll(step, shift, 1) if shift else step
-            pm[f, k] = before + down[k]
-            step = down[k] - pltpu.roll(down[k], 1, 1)
-            for i, shift in enumerate((1, 0, LANES - 1, LANES - 2)):
-                columns[f, 60 + 15 * i + k] = pltpu.roll(step, shift, 1) if shift else step
-
-    column(8, [ends_ref[k] for k in range(NVAR)], [ends_ref[NVAR + k] for k in range(12)])
-
-    def plane(i, _):
-        at = pl.ds(pl.multiple_of(i * 8, 8), 8)
-        column(i, [u_ref[k, at, :] for k in range(NVAR)], [coef_ref[k, at, :] for k in range(12)])
-        return 0
-
-    lax.fori_loop(0, 8, plane, 0)
-
-    def upright(f, _):
-        face_flux(lambda k: mean[f, k], lambda k: 0.0,
-                  lambda side, i, k: columns[f, 60 * side + 15 * (i - side) + k],
-                  emit(fz, f, lambda k: pm[f, k]))
-        return 0
-
-    lax.fori_loop(0, 9, upright, 0)
-    lane = lax.broadcasted_iota(jnp.int32, (8, LANES), 1)
+            pm[i, k] = up[k]
+            pm[i, 15 + k] = down[k]
+        return 0
+
+    lax.fori_loop(0, 14, cell, 0, unroll=2)
+
+    def jump(i, _):
+        for k in range(30):
+            jumps[i, k] = pm[i + 1, k] - pm[i, k]
+        return 0
+
+    lax.fori_loop(0, 13, jump, 0, unroll=True)
+
+    def face(f, _):
+        face_flux(lambda k: mean[f + 2, k], lambda k: mean[f + 3, k],
+                  lambda side, i, k: jumps[f + i, 15 * side + k],
+                  emit(fz, f, lambda k: pm[f + 2, k] + pm[f + 3, 15 + k]))
+        return 0
+
+    lax.fori_loop(0, 9, face, 0)
+    left = lax.broadcasted_iota(jnp.int32, (8, LANES), 1) < 64
     at_z = {9: 10, 10: 11, 11: 9}
-
-    def merge(i, _):
-        at = pl.ds(pl.multiple_of(i * 8, 8), 8)
-        to_low = lax.rem(2 * LANES - 3 - 16 * i, LANES)
-        to_high = lax.rem(2 * LANES - 13 - 16 * i, LANES)
-        for k in range(NVAR):
-            kz = at_z.get(k, k)
-            ends = fz[8, kz]
-            low = pltpu.roll(ends, to_low, 1)
-            high = pltpu.roll(ends, to_high, 1)
-            face = jnp.where(lane < 3, low, jnp.where(lane >= 126, high, fz[i, kz]))
-            after = pltpu.roll(jnp.where(lane == 0, high, face), LANES - 1, 1)
-            out_ref[k, at, :] = face - after
-        return 0
-
-    lax.fori_loop(0, 8, merge, 0)
-
-
-def rate_kernel(speed_ref, u_ref, coef_ref, z_ref, *refs):
-    halo_u, halo_c, out_h = refs[:4], refs[4:8], refs[8]
-    (pm, mean, jumps, fx, fy, fold, out_ref, out_sem) = refs[9:]
+    for pair in range(NVAR // 2):
+        first, second = [at_z.get(k, k) for k in (2 * pair, 2 * pair + 1)]
+        for b in range(8):
+            x = fz[b, first] - fz[b + 1, first]
+            y = fz[b, second] - fz[b + 1, second]
+            turned[pair, pl.ds(b, 8, stride=8), :] = jnp.where(left, x, pltpu.roll(y, 64, 1))
+            turned[pair, pl.ds(64 + b, 8, stride=8), :] = jnp.where(left, pltpu.roll(x, 64, 1), y)
+    for pair in range(NVAR // 2):
+        back = turned[pair].T
+        out_ref[2 * pair] = back[0:64]
+        out_ref[2 * pair + 1] = back[64:128]
+
+
+def rate_kernel(speed_ref, u_ref, coef_ref, z_ref, const, *refs):
+    halo_u, out_h = refs[:4], refs[4]
+    (pm, mean, jumps, fx, fy, fold, out_ref, out_sem) = refs[5:]
     speeds = [speed_ref[d] for d in range(2)]
     scale = speed_ref[3]
     for d, order, strided, flux in ((0, (0, 1, 2), False, fx), (1, (1, 0, 2), True, fy)):
@@ -361,8 +342,8 @@
         for high in range(2):
             def halo(i, _, cell=cell, d=d, high=high):
                 at = pl.ds(pl.multiple_of(i * 8, 8), 8)
-                cell(i + 11 * high, [halo_u[2 * d + high][k, at, :] for k in range(NVAR)],
-                     [halo_c[2 * d + high][k, at, :] for k in range(12)])
+                u = [halo_u[2 * d + high][k, at, :] for k in range(NVAR)]
+                cell(i + 11 * high, u, halves(u, const))
                 return 0
 
             lax.fori_loop(0, 3, halo, 0, unroll=True)
@@ -443,37 +424,32 @@
 
 def own_cells(table, gas, index, kind, u):
     return pl.pallas_call(
-        own_kernel, name="own_cells", in_specs=[HBM] * 5, out_specs=[VMEM] * 2,
-        out_shape=[struct(12, 64, LANES), struct(NVAR + 12, 8, LANES)],
-        scratch_shapes=TABLES + [pltpu.SMEM((1, 2), jnp.int32), vmem(NVAR, 64, LANES), dma(5)],
+        own_kernel, name="own_cells", in_specs=[HBM] * 4 + [VMEM], out_specs=[VMEM] * 4,
+        out_shape=[struct(12, 64, LANES), struct(NVAR, 14, 8, LANES), struct(12, 14, 8, LANES),
+                   struct(12 * NS, 1, LANES)],
+        scratch_shapes=TABLES + [pltpu.SMEM((1, 2), jnp.int32),
+                                     vmem(NVAR // 2, LANES, LANES), dma(4)],
         compiler_params=params())(table, gas, index, kind, u)
 
 
-def halo_cells(table, gas, index, *halos):
+def columns(wide, tall, tall_coef):
     return pl.pallas_call(
-        halo_kernel, name="halo_cells", in_specs=[HBM] * 3 + [VMEM] * 4, out_specs=[VMEM] * 4,
-        out_shape=[struct(12, 24, LANES)] * 4, scratch_shapes=TABLES + [dma(3)],
-        compiler_params=params())(table, gas, index, *halos)
-
-
-def columns(wide, u, coef, ends):
-    return pl.pallas_call(
-        column_kernel, name="columns", in_specs=[VMEM] * 4, out_specs=[VMEM] * 2,
+        column_kernel, name="columns", in_specs=[VMEM] * 3, out_specs=[VMEM] * 2,
         out_shape=[struct(NVAR, 64, LANES), struct(4, 8, LANES)],
-        scratch_shapes=[vmem(9, 15, *PLANES), vmem(9, 24, *PLANES), vmem(9, 120, *PLANES),
-                        vmem(9, NVAR, *PLANES)],
-        compiler_params=params())(wide, u, coef, ends)
-
-
-def rates(speed, u, coef, z, *halos):
+        scratch_shapes=[vmem(14, 30, *PLANES), vmem(14, 24, *PLANES), vmem(13, 30, *PLANES),
+                        vmem(9, NVAR, *PLANES), vmem(NVAR // 2, LANES, LANES)],
+        compiler_params=params())(wide, tall, tall_coef)
+
+
+def rates(speed, u, coef, z, const, *halos):
     flux = vmem(9, NVAR, *PLANES)
     return pl.pallas_call(
-        rate_kernel, name="rates", in_specs=[VMEM] * 12, out_specs=HBM,
+        rate_kernel, name="rates", in_specs=[VMEM] * 9, out_specs=HBM,
         out_shape=struct(NVAR, 64, LANES),
         scratch_shapes=[
             vmem(14, 30, *PLANES), vmem(14, 24, *PLANES), vmem(13, 30, *PLANES), flux, flux,
             vmem(NVAR, 64, LANES), vmem(NVAR, 64, LANES), dma(8)],
-        compiler_params=params())(speed, u, coef, z, *halos)
+        compiler_params=params())(speed, u, coef, z, const, *halos)
 
 
 AXES = ("z", "yl", "x", "yh", "c")
@@ -493,11 +469,10 @@
     fixed = (nasa_table.T, gas_constant, species_index)
     wide, xs, xe, ys, ye = cells(*fixed, u)
     wide = lax.all_to_all(wide, AXES, 0, 0, tiled=True)
-    coef, ends = own_cells(*fixed, face_kind.reshape(1, 2), u)
+    coef, tall, tall_coef, const = own_cells(*fixed, face_kind.reshape(1, 2), u)
     halos = neighbours(xs, xe, GX) + neighbours(ys, ye, GY)
-    z, speed = columns(wide, u, coef, ends)
-    halo_coefs = halo_cells(*fixed, *halos)
-    return rates(speed, u, coef, z, *halos, *halo_coefs).reshape(preserved_vector.shape)
+    z, speed = columns(wide, tall, tall_coef)
+    return rates(speed, u, coef, z, const, *halos).reshape(preserved_vector.shape)
 
 
 def solution(mesh):

time: 50 us -> 42.6 us (0.85)
  waiting for transfers between devices: 6.08 us -> 2.08 us
  Pallas kernels: 18.9 us -> 15.4 us
    pallas_call x4 -> x3, Pallas kernels: 16.5 us -> 13.1 us  [the longest x1 7.02 us: rates(): pl.pallas_call(rate_kernel, name='rates', in_specs=[VMEM] * 9, out_specs=...]
    ppermute x2, waiting for transfers between devices: 3.28 us -> 0.01 us  [neighbours(): low = lax.ppermute(end, axis, up)]
    ppermute x2, waiting for transfers between devices: 2.8 us -> 1.01 us  [neighbours(): high = lax.ppermute(start, axis, [(b, a) for a, b in up])]
    all_to_all x1, waiting for transfers between devices: 0.01 us -> 1.06 us  [shards(): wide = lax.all_to_all(wide, AXES, 0, 0, tiled=True)]
  transfers between devices with their start and end apart: 5 -> 5, of which waited for: 3 -> 2; matrix products, arithmetic and copies ran while one was open for 0% -> 0% of each run, Pallas kernels for 7% -> 14%
where the time goes in v5:
time: 42.6 us; the launch traced here: 42.4 us
  starting transfers between devices  24.3 us (57%)
  Pallas kernels  15.4 us (36%)
  waiting for transfers between devices  2.08 us (5%)
  local copies, waits for them, and re-layouts  0.59 us (1%)
    all_to_all x1, starting transfers between devices, shards(): wide = lax.all_to_all(wide, AXES, 0, 0, tiled=True)  15.7 us
    pallas_call x1, Pallas kernels, rates(): pl.pallas_call(rate_kernel, name='rates', in_specs=[VMEM] * 9, out_specs=...  7.02 us
    ppermute x2, starting transfers between devices, neighbours(): low = lax.ppermute(end, axis, up)  4.51 us
    ppermute x2, starting transfers between devices, neighbours(): high = lax.ppermute(start, axis, [(b, a) for a, b in up])  4.09 us
    pallas_call x1, Pallas kernels, columns(): pl.pallas_call(column_kernel, name='columns', in_specs=[VMEM] * 3, out_sp...  3.2 us
    pallas_call x1, Pallas kernels, own_cells(): pl.pallas_call(own_kernel, name='own_cells', in_specs=[HBM] * 4 + [VMEM],...  2.84 us
    pallas_call x1, Pallas kernels, cells(): pl.pallas_call(cell_kernel, name='cells', in_specs=[HBM] * 4, out_specs=[...  2.37 us
    all_to_all x1, waiting for transfers between devices, shards(): wide = lax.all_to_all(wide, AXES, 0, 0, tiled=True)  1.06 us
  transfers between devices with their start and end apart: 5, of which 2 were waited for; matrix products, arithmetic and copies ran while one was open for 0% of the time, Pallas kernels for 14%

profile of v5, /device:TPU:1, one launch (start us, length us, event | category | flops | bytes accessed | tf_op | source)
XLA Modules:
  0.0 42.4 jit_solution(6428195731820010742)
XLA Ops:
  0.0 0.0 copy-start
  0.0 2.4 %cells.1 = (f32[256,128]{1,0:T(8,128)}, f32[14,24,128]{2,1,0:T(8,128)}, f32[14,24,128]{2,1,0:T(8,128)}, f32[14,24,128]{2,1,0:T(8,128)}, f32[14,24,128]{2,1,0:T(8,128)}) custom-call(f32[6,32]{1,0:T(8,128)} %bitcast.12, f32[32]{0:T(128)} %gas_h.3, s32[9]{0:T(128)} %index_h.3, f32[14,64,128]{2,1,0:T(8,128)} %bitcast.8), custom_call_target="tpu_custom_call" | custom-call | tf_op jit(solution)/shard_map/cells/pallas_call | solution.py:418
  2.4 0.0 copy-start.5
  2.4 15.7 %all-to-all-start = ((f32[256,1,128]{2,1,0:T(1,128)}), f32[256,1,128]{2,1,0:T(1,128)S(1)}, u32[]{:S(2)}, u32[]{:S(2)}) async-start(f32[256,1,128]{2,1,0:T(1,128)} %bitcast.15), calls=%async_computation | async-start | bytes 262144 | tf_op jit(solution)/shard_map/all_to_all | solution.py:471
  18.1 0.0 copy-start.1
  18.1 1.4 %collective-permute-start = (f32[14,24,128]{2,1,0:T(8,128)}, f32[14,24,128]{2,1,0:T(8,128)S(1)}, u32[]{:S(2)}, u32[]{:S(2)}) collective-permute-start(f32[14,24,128]{2,1,0:T(8,128)} %get-tuple-element.23), channel_id=1, source_target_pairs={{0,16},{16,32},{32,48},{48,64},{64,80},{80,96},{96,112},{112,128},... | collective-permute-start | bytes 516104 | tf_op jit(solution)/shard_map/ppermute | solution.py:462
  19.5 4.0 %collective-permute-start.1 = (f32[14,24,128]{2,1,0:T(8,128)}, f32[14,24,128]{2,1,0:T(8,128)S(1)}, u32[]{:S(2)}, u32[]{:S(2)}) collective-permute-start(f32[14,24,128]{2,1,0:T(8,128)} %get-tuple-element.24), channel_id=1, source_target_pairs={{16,0},{32,16},{48,32},{64,48},{80,64},{96,80},{112,96},{128,112},... | collective-permute-start | bytes 516104 | tf_op jit(solution)/shard_map/ppermute | solution.py:463
  23.5 3.1 %collective-permute-start.2 = (f32[14,24,128]{2,1,0:T(8,128)}, f32[14,24,128]{2,1,0:T(8,128)S(1)}, u32[]{:S(2)}, u32[]{:S(2)}) collective-permute-start(f32[14,24,128]{2,1,0:T(8,128)} %get-tuple-element.25), channel_id=1, source_target_pairs={{0,1},{1,2},{2,3},{3,4},{4,5},{5,6},{6,7},{7,8},{8,9},{9,10},{10,1... | collective-permute-start | bytes 516104 | tf_op jit(solution)/shard_map/ppermute | solution.py:462
  26.6 0.0 copy-done.5
  26.6 0.0 copy-start.2
  26.6 0.0 copy-start.3
  26.6 0.0 copy-start.4
  26.6 0.1 collective-permute-start.3
  26.7 0.0 copy-done
  26.7 0.0 copy-done.1
  26.7 0.5 %copy-done.2 = f32[32]{0:T(128)S(1)} copy-done((f32[32]{0:T(128)S(1)}, f32[32]{0:T(128)}, u32[]{:S(2)}) %copy-start.2) | copy-done | bytes 152
  27.2 0.0 copy-done.3
  27.3 0.0 copy-done.4
  27.3 2.8 %own_cells.1 = (f32[12,64,128]{2,1,0:T(8,128)S(1)}, f32[14,14,8,128]{3,2,1,0:T(8,128)S(1)}, f32[12,14,8,128]{3,2,1,0:T(8,128)S(1)}, f32[108,1,128]{2,1,0:T(1,128)S(1)}) custom-call(f32[6,32]{1,0:T(8,128)S(1)} %bitcast.13, f32[32]{0:T(128)S(1)} %copy-done.2, s32[9]{0:T(128)S(1)} %copy-done.3, s32[1,2]{1,0:T(1,128)S(1)} %bitcast.14, f32[14,64,128]{2,1,0:T(8,128)S(1)} %bitcast.9), custom_call_target="tpu_custom_call" | custom-call | tf_op jit(solution)/shard_map/own_cells/pallas_call | solution.py:426
  30.1 1.1 %all-to-all-done = f32[256,1,128]{2,1,0:T(1,128)S(1)} async-done(((f32[256,1,128]{2,1,0:T(1,128)}), f32[256,1,128]{2,1,0:T(1,128)S(1)}, u32[]{:S(2)}, u32[]{:S(2)}) %all-to-all-start) | async-done | bytes 131104 | tf_op jit(solution)/shard_map/all_to_all | solution.py:471
  31.2 3.2 %columns.1 = (f32[14,64,128]{2,1,0:T(8,128)S(1)}, f32[4,8,128]{2,1,0:T(8,128)S(1)}) custom-call(f32[256,128]{1,0:T(8,128)S(1)} %bitcast.11, f32[14,14,8,128]{3,2,1,0:T(8,128)S(1)} %get-tuple-element.17.tall_ref, f32[12,14,8,128]{3,2,1,0:T(8,128)S(1)} %get-tuple-element.18.tall_coef), custom_call_target="tpu_custom_call" | custom-call | tf_op jit(solution)/shard_map/columns/pallas_call | solution.py:436
  34.4 0.0 collective-permute-done.refs_0_
  34.4 0.0 collective-permute-done.1.refs_1_
  34.4 0.0 collective-permute-done.2.refs_2_
  34.4 1.0 %collective-permute-done.3.refs_3_ = f32[14,24,128]{2,1,0:T(8,128)S(1)} collective-permute-done((f32[14,24,128]{2,1,0:T(8,128)S(1)}, f32[14,24,128]{2,1,0:T(8,128)S(1)}, u32[]{:S(2)}, u32[]{:S(2)}) %collective-permute-start.3) | collective-permute-done | bytes 172064 | tf_op jit(solution)/shard_map/ppermute | solution.py:463
  35.4 7.0 %rates.1 = f32[14,64,128]{2,1,0:T(8,128)} custom-call(f32[4,8,128]{2,1,0:T(8,128)S(1)} %get-tuple-element.19.speed_ref, f32[14,64,128]{2,1,0:T(8,128)S(1)} %bitcast.10, f32[12,64,128]{2,1,0:T(8,128)S(1)} %get-tuple-element.20.coef_ref, f32[14,64,128]{2,1,0:T(8,128)S(1)} %get-tuple-element.21.z_ref, f32[108,1,128]{2,1,0:T(1,128)S(1)} %get-tuple-element.22.const, ...), custom_call_target="tpu_custom_call" | custom-call | tf_op jit(solution)/shard_map/rates/pallas_call | solution.py:446
Async XLA Ops:
  0.0 26.7 %copy-start = (f32[14,8,8,128]{3,2,1,0:T(8,128)S(1)}, f32[14,8,8,128]{3,2,1,0:T(8,128)}, u32[]{:S(2)}) copy-start(f32[14,8,8,128]{3,2,1,0:T(8,128)} %param.5) | copy-start | bytes 1376260
  2.4 24.2 %copy-start.5 = (f32[14,24,128]{2,1,0:T(8,128)S(1)}, f32[14,24,128]{2,1,0:T(8,128)}, u32[]{:S(2)}) copy-start(f32[14,24,128]{2,1,0:T(8,128)} %get-tuple-element.26) | copy-start | bytes 516100
  2.4 28.8 %all-to-all-start = ((f32[256,1,128]{2,1,0:T(1,128)}), f32[256,1,128]{2,1,0:T(1,128)S(1)}, u32[]{:S(2)}, u32[]{:S(2)}) async-start(f32[256,1,128]{2,1,0:T(1,128)} %bitcast.15), calls=%async_computation | async-start | bytes 262144 | tf_op jit(solution)/shard_map/all_to_all | solution.py:471
  18.1 8.6 %copy-start.1 = (f32[32,6]{0,1:T(8,128)S(1)}, f32[32,6]{0,1:T(8,128)}, u32[]{:S(2)}) copy-start(f32[32,6]{0,1:T(8,128)} %param.6) | copy-start | bytes 2308
  18.1 16.3 %collective-permute-start = (f32[14,24,128]{2,1,0:T(8,128)}, f32[14,24,128]{2,1,0:T(8,128)S(1)}, u32[]{:S(2)}, u32[]{:S(2)}) collective-permute-start(f32[14,24,128]{2,1,0:T(8,128)} %get-tuple-element.23), channel_id=1, source_target_pairs={{0,16},{16,32},{32,48},{48,64},{64,80},{80,96},{96,112},{112,128},... | collective-permute-start | bytes 516104 | tf_op jit(solution)/shard_map/ppermute | solution.py:462
  19.5 14.9 %collective-permute-start.1 = (f32[14,24,128]{2,1,0:T(8,128)}, f32[14,24,128]{2,1,0:T(8,128)S(1)}, u32[]{:S(2)}, u32[]{:S(2)}) collective-permute-start(f32[14,24,128]{2,1,0:T(8,128)} %get-tuple-element.24), channel_id=1, source_target_pairs={{16,0},{32,16},{48,32},{64,48},{80,64},{96,80},{112,96},{128,112},... | collective-permute-start | bytes 516104 | tf_op jit(solution)/shard_map/ppermute | solution.py:463
  23.5 10.9 %collective-permute-start.2 = (f32[14,24,128]{2,1,0:T(8,128)}, f32[14,24,128]{2,1,0:T(8,128)S(1)}, u32[]{:S(2)}, u32[]{:S(2)}) collective-permute-start(f32[14,24,128]{2,1,0:T(8,128)} %get-tuple-element.25), channel_id=1, source_target_pairs={{0,1},{1,2},{2,3},{3,4},{4,5},{5,6},{6,7},{7,8},{8,9},{9,10},{10,1... | collective-permute-start | bytes 516104 | tf_op jit(solution)/shard_map/ppermute | solution.py:462
  26.6 0.7 %copy-start.2 = (f32[32]{0:T(128)S(1)}, f32[32]{0:T(128)}, u32[]{:S(2)}) copy-start(f32[32]{0:T(128)} %gas_h.3) | copy-start | bytes 388
  26.6 0.7 %copy-start.3 = (s32[9]{0:T(128)S(1)}, s32[9]{0:T(128)}, u32[]{:S(2)}) copy-start(s32[9]{0:T(128)} %index_h.3) | copy-start | bytes 112
  26.6 0.7 %copy-start.4 = (s32[1,1,2]{2,1,0:T(1,128)S(1)}, s32[1,1,2]{2,1,0:T(1,128)}, u32[]{:S(2)}) copy-start(s32[1,1,2]{2,1,0:T(1,128)} %param.9) | copy-start | bytes 28
  26.6 8.8 %collective-permute-start.3 = (f32[14,24,128]{2,1,0:T(8,128)S(1)}, f32[14,24,128]{2,1,0:T(8,128)S(1)}, u32[]{:S(2)}, u32[]{:S(2)}) collective-permute-start(f32[14,24,128]{2,1,0:T(8,128)S(1)} %copy-done.5), channel_id=1, source_target_pairs={{1,0},{2,1},{3,2},{4,3},{5,4},{6,5},{7,6},{8,7},{9,8},{10,9},{11,1... | collective-permute-start | bytes 516104 | tf_op jit(solution)/shard_map/ppermute | solution.py:463

commit v6 on v5

--- a/solution.py
+++ b/solution.py
@@ -110,11 +110,11 @@
     i1 = reciprocal(t1 * t1 + e2)
     i2 = reciprocal(t2 * t2 + e2)
     w0 = i0 * i0
-    w1 = 6.0 * (i1 * i1)
-    w2 = 3.0 * (i2 * i2)
-    q = 2.625 * d2
-    lead = (2.25 * d1 - q) - (t0 + t0)
-    return q + (w0 * lead + w1 * t1 - w2 * t2) * reciprocal(w0 + w1 + w2)
+    w1 = i1 * i1
+    w2 = 0.5 * (i2 * i2)
+    q = 0.4375 * d2
+    lead = (0.375 * d1 - q) - (1.0 / 3.0) * t0
+    return q + (w0 * lead + w1 * t1 - w2 * t2) * reciprocal(w0 + 6.0 * (w1 + w2))
 
 
 def reciprocal(x):
@@ -257,7 +257,7 @@
 
 def emit(flux, f, base):
     def put(k, value):
-        flux[f, k] = value * (1.0 / 6.0) + base(k)
+        flux[f, k] = value + base(k)
 
     return put
 
@@ -317,77 +317,74 @@
         out_ref[2 * pair + 1] = back[64:128]
 
 
-def rate_kernel(speed_ref, u_ref, coef_ref, z_ref, const, *refs):
-    halo_u, out_h = refs[:4], refs[4]
-    (pm, mean, jumps, fx, fy, fold, out_ref, out_sem) = refs[5:]
-    speeds = [speed_ref[d] for d in range(2)]
+def line_flux(order, strided, speed, u_ref, coef_ref, const, halos, pm, mean, jumps, flux, done):
+    def cell(i, u, coef):
+        up, down, m = split_fields(u, coef, order, speed)
+        for k in range(24):
+            mean[i, k] = m[k]
+        for k in range(15):
+            pm[i, k] = up[k]
+            pm[i, 15 + k] = down[k]
+
+    def own(i, _):
+        at = pl.ds(i, 8, stride=8) if strided else pl.ds(pl.multiple_of(i * 8, 8), 8)
+        cell(i + 3, [u_ref[k, at, :] for k in range(NVAR)],
+             [coef_ref[k, at, :] for k in range(12)])
+        return 0
+
+    lax.fori_loop(0, 8, own, 0, unroll=2)
+    for high in range(2):
+        def halo(i, _, high=high):
+            at = pl.ds(pl.multiple_of(i * 8, 8), 8)
+            u = [halos[high][k, at, :] for k in range(NVAR)]
+            cell(i + 11 * high, u, halves(u, const))
+            return 0
+
+        lax.fori_loop(0, 3, halo, 0, unroll=True)
+
+    def jump(i, _):
+        for k in range(30):
+            jumps[i, k] = pm[i + 1, k] - pm[i, k]
+        return 0
+
+    lax.fori_loop(0, 13, jump, 0, unroll=True)
+
+    def face(f, _):
+        face_flux(lambda k: mean[f + 2, k], lambda k: mean[f + 3, k],
+                  lambda side, i, k: jumps[f + i, 15 * side + k],
+                  emit(flux, f, lambda k: pm[f + 2, k] + pm[f + 3, 15 + k]))
+        pl.when(f > 0)(lambda: done(f - 1))
+        return 0
+
+    lax.fori_loop(0, 9, face, 0)
+
+
+def x_kernel(speed_ref, u_ref, coef_ref, z_ref, const, low, high, out_ref, pm, mean, jumps, flux):
+    def done(i):
+        at = pl.ds(pl.multiple_of(i * 8, 8), 8)
+        for k in range(NVAR):
+            out_ref[k, at, :] = z_ref[k, at, :] + (flux[i, k] - flux[i + 1, k])
+
+    line_flux((0, 1, 2), False, speed_ref[0], u_ref, coef_ref, const, (low, high), pm, mean, jumps,
+              flux, done)
+
+
+def y_kernel(speed_ref, u_ref, coef_ref, sum_ref, const, low, high, out_h,
+             pm, mean, jumps, flux, out_ref, out_sem):
     scale = speed_ref[3]
-    for d, order, strided, flux in ((0, (0, 1, 2), False, fx), (1, (1, 0, 2), True, fy)):
-        def cell(i, u, coef, d=d, order=order):
-            up, down, m = split_fields(u, coef, order, speeds[d])
-            for k in range(24):
-                mean[i, k] = m[k]
-            for k in range(15):
-                pm[i, k] = up[k]
-                pm[i, 15 + k] = down[k]
-
-        def own(i, _, cell=cell, strided=strided):
-            at = pl.ds(i, 8, stride=8) if strided else pl.ds(pl.multiple_of(i * 8, 8), 8)
-            cell(i + 3, [u_ref[k, at, :] for k in range(NVAR)],
-                 [coef_ref[k, at, :] for k in range(12)])
-            return 0
-
-        lax.fori_loop(0, 8, own, 0, unroll=2)
-
-        for high in range(2):
-            def halo(i, _, cell=cell, d=d, high=high):
-                at = pl.ds(pl.multiple_of(i * 8, 8), 8)
-                u = [halo_u[2 * d + high][k, at, :] for k in range(NVAR)]
-                cell(i + 11 * high, u, halves(u, const))
-                return 0
-
-            lax.fori_loop(0, 3, halo, 0, unroll=True)
-
-        def jump(i, _):
-            for k in range(30):
-                jumps[i, k] = pm[i + 1, k] - pm[i, k]
-            return 0
-
-        lax.fori_loop(0, 13, jump, 0, unroll=True)
-
-        def face(f, _, flux=flux):
-            face_flux(lambda k: mean[f + 2, k], lambda k: mean[f + 3, k],
-                      lambda side, i, k: jumps[f + i, 15 * side + k],
-                      emit(flux, f, lambda k: pm[f + 2, k] + pm[f + 3, 15 + k]))
-            return 0
-
-        lax.fori_loop(0, 9, face, 0)
-
     at_y = {9: 10, 10: 9, 11: 11}
 
-    def row(j, _):
+    def done(j):
         at = pl.ds(j, 8, stride=8)
         for k in range(NVAR):
             ky = at_y.get(k, k)
-            fold[k, at, :] = fy[j, ky] - fy[j + 1, ky]
-        return 0
-
-    lax.fori_loop(0, 8, row, 0)
-
-    def store(i):
-        at = pl.ds(pl.multiple_of(i * 8, 8), 8)
-        return pltpu.make_async_copy(out_ref.at[:, at, :], out_h.at[:, at, :], out_sem.at[i])
-
-    def plane(i, _):
-        at = pl.ds(pl.multiple_of(i * 8, 8), 8)
-        for k in range(NVAR):
-            out_ref[k, at, :] = (z_ref[k, at, :] + (fx[i, k] - fx[i + 1, k]) + fold[k, at, :]) * scale
-        store(i).start()
-        return 0
-
-    lax.fori_loop(0, 8, plane, 0)
-    for i in range(8):
-        store(i).wait()
+            out_ref[k, at, :] = (sum_ref[k, at, :] + (flux[j, ky] - flux[j + 1, ky])) * scale
+
+    line_flux((1, 0, 2), True, speed_ref[1], u_ref, coef_ref, const, (low, high), pm, mean, jumps,
+              flux, done)
+    copies = fetch([(out_ref.at[k], out_h.at[k]) for k in range(NVAR)], out_sem)
+    for copy in copies:
+        copy.wait()
 
 
 HBM = pl.BlockSpec(memory_space=pltpu.MemorySpace.HBM)
@@ -419,7 +416,8 @@
         cell_kernel, name="cells", in_specs=[HBM] * 4, out_specs=[VMEM] * 5,
         out_shape=[struct(256, LANES), halo, halo, halo, halo],
         scratch_shapes=TABLES + [vmem(NVAR, 64, LANES), dma(4)],
-        compiler_params=params(58))(table, gas, index, u)
+        compiler_params=params())(*[
+            pltpu.with_memory_space_constraint(x, pltpu.MemorySpace.HBM) for x in (table, gas, index, u)])
 
 
 def own_cells(table, gas, index, kind, u):
@@ -441,15 +439,22 @@
         compiler_params=params())(wide, tall, tall_coef)
 
 
-def rates(speed, u, coef, z, const, *halos):
-    flux = vmem(9, NVAR, *PLANES)
+def x_rates(speed, u, coef, z, const, low, high):
     return pl.pallas_call(
-        rate_kernel, name="rates", in_specs=[VMEM] * 9, out_specs=HBM,
+        x_kernel, name="x_rates", in_specs=[VMEM] * 7, out_specs=VMEM,
         out_shape=struct(NVAR, 64, LANES),
-        scratch_shapes=[
-            vmem(14, 30, *PLANES), vmem(14, 24, *PLANES), vmem(13, 30, *PLANES), flux, flux,
-            vmem(NVAR, 64, LANES), vmem(NVAR, 64, LANES), dma(8)],
-        compiler_params=params())(speed, u, coef, z, const, *halos)
+        scratch_shapes=[vmem(14, 30, *PLANES), vmem(14, 24, *PLANES), vmem(13, 30, *PLANES),
+                        vmem(9, NVAR, *PLANES)],
+        compiler_params=params())(speed, u, coef, z, const, low, high)
+
+
+def y_rates(speed, u, coef, total, const, low, high):
+    return pl.pallas_call(
+        y_kernel, name="y_rates", in_specs=[VMEM] * 7, out_specs=HBM,
+        out_shape=struct(NVAR, 64, LANES),
+        scratch_shapes=[vmem(14, 30, *PLANES), vmem(14, 24, *PLANES), vmem(13, 30, *PLANES),
+                        vmem(9, NVAR, *PLANES), vmem(NVAR, 64, LANES), dma(NVAR)],
+        compiler_params=params())(speed, u, coef, total, const, low, high)
 
 
 AXES = ("z", "yl", "x", "yh", "c")
@@ -470,9 +475,11 @@
     wide, xs, xe, ys, ye = cells(*fixed, u)
     wide = lax.all_to_all(wide, AXES, 0, 0, tiled=True)
     coef, tall, tall_coef, const = own_cells(*fixed, face_kind.reshape(1, 2), u)
-    halos = neighbours(xs, xe, GX) + neighbours(ys, ye, GY)
+    x_halos = neighbours(xs, xe, GX)
+    y_halos = neighbours(ys, ye, GY)
     z, speed = columns(wide, tall, tall_coef)
-    return rates(speed, u, coef, z, const, *halos).reshape(preserved_vector.shape)
+    total = x_rates(speed, u, coef, z, const, *x_halos)
+    return y_rates(speed, u, coef, total, const, *y_halos).reshape(preserved_vector.shape)
 
 
 def solution(mesh):

time: 42.6 us -> 41.6 us (0.977)
  waiting for transfers between devices: 2.08 us -> 1.09 us
    ppermute x2, waiting for transfers between devices: 1.01 us -> 0.01 us  [neighbours(): high = lax.ppermute(start, axis, [(b, a) for a, b in up])]
    pallas_call x1 -> x2, Pallas kernels: 7.02 us -> 7.08 us  [the longest x1 4.06 us: y_rates(): pl.pallas_call(y_kernel, name='y_rates', in_specs=[VMEM] * 7, out_specs=H...]
  transfers between devices with their start and end apart: 5 -> 5, of which waited for: 2 -> 1; matrix products, arithmetic and copies ran while one was open for 0% -> 0% of each run, Pallas kernels for 14% -> 22%
where the time goes in v6:
time: 41.6 us; the launch traced here: 41.4 us
  starting transfers between devices  24.2 us (58%)
  Pallas kernels  15.4 us (37%)
  waiting for transfers between devices  1.09 us (3%)
  local copies, waits for them, and re-layouts  0.67 us (2%)
    all_to_all x1, starting transfers between devices, shards(): wide = lax.all_to_all(wide, AXES, 0, 0, tiled=True)  15.7 us
    ppermute x2, starting transfers between devices, neighbours(): low = lax.ppermute(end, axis, up)  4.51 us
    pallas_call x1, Pallas kernels, y_rates(): pl.pallas_call(y_kernel, name='y_rates', in_specs=[VMEM] * 7, out_specs=H...  4.06 us
    ppermute x2, starting transfers between devices, neighbours(): high = lax.ppermute(start, axis, [(b, a) for a, b in up])  4.01 us
    pallas_call x1, Pallas kernels, columns(): pl.pallas_call(column_kernel, name='columns', in_specs=[VMEM] * 3, out_sp...  3.17 us
    pallas_call x1, Pallas kernels, x_rates(): pl.pallas_call(x_kernel, name='x_rates', in_specs=[VMEM] * 7, out_specs=V...  3.02 us
    pallas_call x1, Pallas kernels, own_cells(): pl.pallas_call(own_kernel, name='own_cells', in_specs=[HBM] * 4 + [VMEM],...  2.84 us
    pallas_call x1, Pallas kernels, cells(): pl.pallas_call(cell_kernel, name='cells', in_specs=[HBM] * 4, out_specs=[...  2.3 us
  transfers between devices with their start and end apart: 5, of which 1 were waited for; matrix products, arithmetic and copies ran while one was open for 0% of the time, Pallas kernels for 22%

profile of v6, /device:TPU:1, one launch (start us, length us, event | category | flops | bytes accessed | tf_op | source)
XLA Modules:
  0.0 41.4 jit_solution(15774557976674885446)
XLA Ops:
  0.0 0.0 copy-start
  0.0 2.3 %cells.1 = (f32[256,128]{1,0:T(8,128)}, f32[14,24,128]{2,1,0:T(8,128)}, f32[14,24,128]{2,1,0:T(8,128)}, f32[14,24,128]{2,1,0:T(8,128)S(1)}, f32[14,24,128]{2,1,0:T(8,128)}) custom-call(f32[6,32]{1,0:T(8,128)} %bitcast.13, f32[32]{0:T(128)} %gas_h.3, s32[9]{0:T(128)} %index_h.3, f32[14,64,128]{2,1,0:T(8,128)} %bitcast.8), custom_call_target="tpu_custom_call" | custom-call | tf_op jit(solution)/shard_map/cells/pallas_call | solution.py:415
  2.3 15.7 %all-to-all-start = ((f32[256,1,128]{2,1,0:T(1,128)}), f32[256,1,128]{2,1,0:T(1,128)S(1)}, u32[]{:S(2)}, u32[]{:S(2)}) async-start(f32[256,1,128]{2,1,0:T(1,128)} %bitcast.3), calls=%async_computation | async-start | bytes 262144 | tf_op jit(solution)/shard_map/all_to_all | solution.py:476
  18.0 0.0 copy-start.1
  18.0 1.4 %collective-permute-start = (f32[14,24,128]{2,1,0:T(8,128)}, f32[14,24,128]{2,1,0:T(8,128)S(1)}, u32[]{:S(2)}, u32[]{:S(2)}) collective-permute-start(f32[14,24,128]{2,1,0:T(8,128)} %get-tuple-element.23), channel_id=1, source_target_pairs={{0,16},{16,32},{32,48},{48,64},{64,80},{80,96},{96,112},{112,128},... | collective-permute-start | bytes 516104 | tf_op jit(solution)/shard_map/ppermute | solution.py:467
  19.4 4.0 %collective-permute-start.1 = (f32[14,24,128]{2,1,0:T(8,128)}, f32[14,24,128]{2,1,0:T(8,128)S(1)}, u32[]{:S(2)}, u32[]{:S(2)}) collective-permute-start(f32[14,24,128]{2,1,0:T(8,128)} %get-tuple-element.24), channel_id=1, source_target_pairs={{16,0},{32,16},{48,32},{64,48},{80,64},{96,80},{112,96},{128,112},... | collective-permute-start | bytes 516104 | tf_op jit(solution)/shard_map/ppermute | solution.py:468
  23.4 3.1 %collective-permute-start.2 = (f32[14,24,128]{2,1,0:T(8,128)}, f32[14,24,128]{2,1,0:T(8,128)S(1)}, u32[]{:S(2)}, u32[]{:S(2)}) collective-permute-start(f32[14,24,128]{2,1,0:T(8,128)} %get-tuple-element.25), channel_id=1, source_target_pairs={{0,1},{1,2},{2,3},{3,4},{4,5},{5,6},{6,7},{7,8},{8,9},{9,10},{10,1... | collective-permute-start | bytes 516104 | tf_op jit(solution)/shard_map/ppermute | solution.py:467
  26.5 0.0 copy-start.2
  26.5 0.0 copy-start.3
  26.5 0.0 copy-start.4
  26.5 0.0 collective-permute-start.3
  26.5 0.0 copy-done
  26.5 0.0 copy-done.1
  26.5 0.6 %copy-done.2 = f32[32]{0:T(128)S(1)} copy-done((f32[32]{0:T(128)S(1)}, f32[32]{0:T(128)}, u32[]{:S(2)}) %copy-start.2) | copy-done | bytes 152
  27.2 0.0 copy-done.3
  27.2 0.0 copy-done.4
  27.2 2.8 %own_cells.1 = (f32[12,64,128]{2,1,0:T(8,128)S(1)}, f32[14,14,8,128]{3,2,1,0:T(8,128)S(1)}, f32[12,14,8,128]{3,2,1,0:T(8,128)S(1)}, f32[108,1,128]{2,1,0:T(1,128)S(1)}) custom-call(f32[6,32]{1,0:T(8,128)S(1)} %bitcast.14, f32[32]{0:T(128)S(1)} %copy-done.2, s32[9]{0:T(128)S(1)} %copy-done.3, s32[1,2]{1,0:T(1,128)S(1)} %bitcast.15, f32[14,64,128]{2,1,0:T(8,128)S(1)} %bitcast.9), custom_call_target="tpu_custom_call" | custom-call | tf_op jit(solution)/shard_map/own_cells/pallas_call | solution.py:424
  30.0 1.1 %all-to-all-done = f32[256,1,128]{2,1,0:T(1,128)S(1)} async-done(((f32[256,1,128]{2,1,0:T(1,128)}), f32[256,1,128]{2,1,0:T(1,128)S(1)}, u32[]{:S(2)}, u32[]{:S(2)}) %all-to-all-start) | async-done | bytes 131104 | tf_op jit(solution)/shard_map/all_to_all | solution.py:476
  31.1 3.2 %columns.1 = (f32[14,64,128]{2,1,0:T(8,128)S(1)}, f32[4,8,128]{2,1,0:T(8,128)S(1)}) custom-call(f32[256,128]{1,0:T(8,128)S(1)} %bitcast.12, f32[14,14,8,128]{3,2,1,0:T(8,128)S(1)} %get-tuple-element.17.tall_ref, f32[12,14,8,128]{3,2,1,0:T(8,128)S(1)} %get-tuple-element.18.tall_coef), custom_call_target="tpu_custom_call" | custom-call | tf_op jit(solution)/shard_map/columns/pallas_call | solution.py:434
  34.3 0.0 collective-permute-done.low
  34.3 0.0 collective-permute-done.1.high
  34.3 3.0 %x_rates.1.sum_ref = f32[14,64,128]{2,1,0:T(8,128)S(1)} custom-call(f32[4,8,128]{2,1,0:T(8,128)S(1)} %get-tuple-element.19.speed_ref, f32[14,64,128]{2,1,0:T(8,128)S(1)} %bitcast.10, f32[12,64,128]{2,1,0:T(8,128)S(1)} %get-tuple-element.20.coef_ref, f32[14,64,128]{2,1,0:T(8,128)S(1)} %get-tuple-element.21.z_ref, f32[108,1,128]{2,1,0:T(1,128)S(1)} %get-tuple-element.22.const, ...), custom_call_target="tpu_custom_call" | custom-call | tf_op jit(solution)/shard_map/x_rates/pallas_call | solution.py:443
  37.3 0.0 collective-permute-done.2.low
  37.3 0.0 collective-permute-done.3.high
  37.4 4.1 %y_rates.1 = f32[14,64,128]{2,1,0:T(8,128)} custom-call(f32[4,8,128]{2,1,0:T(8,128)S(1)} %get-tuple-element.19.speed_ref, f32[14,64,128]{2,1,0:T(8,128)S(1)} %bitcast.11, f32[12,64,128]{2,1,0:T(8,128)S(1)} %get-tuple-element.20.coef_ref, f32[14,64,128]{2,1,0:T(8,128)S(1)} %x_rates.1.sum_ref, f32[108,1,128]{2,1,0:T(1,128)S(1)} %get-tuple-element.22.const, ...), custom_call_target="tpu_custom_call" | custom-call | tf_op jit(solution)/shard_map/y_rates/pallas_call | solution.py:452
Async XLA Ops:
  0.0 26.5 %copy-start = (f32[14,8,8,128]{3,2,1,0:T(8,128)S(1)}, f32[14,8,8,128]{3,2,1,0:T(8,128)}, u32[]{:S(2)}) copy-start(f32[14,8,8,128]{3,2,1,0:T(8,128)} %param.5) | copy-start | bytes 1376260
  2.3 28.8 %all-to-all-start = ((f32[256,1,128]{2,1,0:T(1,128)}), f32[256,1,128]{2,1,0:T(1,128)S(1)}, u32[]{:S(2)}, u32[]{:S(2)}) async-start(f32[256,1,128]{2,1,0:T(1,128)} %bitcast.3), calls=%async_computation | async-start | bytes 262144 | tf_op jit(solution)/shard_map/all_to_all | solution.py:476
  18.0 8.6 %copy-start.1 = (f32[32,6]{0,1:T(8,128)S(1)}, f32[32,6]{0,1:T(8,128)}, u32[]{:S(2)}) copy-start(f32[32,6]{0,1:T(8,128)} %param.6) | copy-start | bytes 2308
  18.0 16.3 %collective-permute-start = (f32[14,24,128]{2,1,0:T(8,128)}, f32[14,24,128]{2,1,0:T(8,128)S(1)}, u32[]{:S(2)}, u32[]{:S(2)}) collective-permute-start(f32[14,24,128]{2,1,0:T(8,128)} %get-tuple-element.23), channel_id=1, source_target_pairs={{0,16},{16,32},{32,48},{48,64},{64,80},{80,96},{96,112},{112,128},... | collective-permute-start | bytes 516104 | tf_op jit(solution)/shard_map/ppermute | solution.py:467
  19.4 14.9 %collective-permute-start.1 = (f32[14,24,128]{2,1,0:T(8,128)}, f32[14,24,128]{2,1,0:T(8,128)S(1)}, u32[]{:S(2)}, u32[]{:S(2)}) collective-permute-start(f32[14,24,128]{2,1,0:T(8,128)} %get-tuple-element.24), channel_id=1, source_target_pairs={{16,0},{32,16},{48,32},{64,48},{80,64},{96,80},{112,96},{128,112},... | collective-permute-start | bytes 516104 | tf_op jit(solution)/shard_map/ppermute | solution.py:468
  23.4 13.9 %collective-permute-start.2 = (f32[14,24,128]{2,1,0:T(8,128)}, f32[14,24,128]{2,1,0:T(8,128)S(1)}, u32[]{:S(2)}, u32[]{:S(2)}) collective-permute-start(f32[14,24,128]{2,1,0:T(8,128)} %get-tuple-element.25), channel_id=1, source_target_pairs={{0,1},{1,2},{2,3},{3,4},{4,5},{5,6},{6,7},{7,8},{8,9},{9,10},{10,1... | collective-permute-start | bytes 516104 | tf_op jit(solution)/shard_map/ppermute | solution.py:467
  26.5 0.7 %copy-start.2 = (f32[32]{0:T(128)S(1)}, f32[32]{0:T(128)}, u32[]{:S(2)}) copy-start(f32[32]{0:T(128)} %gas_h.3) | copy-start | bytes 388
  26.5 0.7 %copy-start.3 = (s32[9]{0:T(128)S(1)}, s32[9]{0:T(128)}, u32[]{:S(2)}) copy-start(s32[9]{0:T(128)} %index_h.3) | copy-start | bytes 112
  26.5 0.7 %copy-start.4 = (s32[1,1,2]{2,1,0:T(1,128)S(1)}, s32[1,1,2]{2,1,0:T(1,128)}, u32[]{:S(2)}) copy-start(s32[1,1,2]{2,1,0:T(1,128)} %param.9) | copy-start | bytes 28
  26.5 10.8 %collective-permute-start.3 = (f32[14,24,128]{2,1,0:T(8,128)S(1)}, f32[14,24,128]{2,1,0:T(8,128)S(1)}, u32[]{:S(2)}, u32[]{:S(2)}) collective-permute-start(f32[14,24,128]{2,1,0:T(8,128)S(1)} %get-tuple-element.26), channel_id=1, source_target_pairs={{1,0},{2,1},{3,2},{4,3},{5,4},{6,5},{7,6},{8,7},{9,8},{10,9},{11,1... | collective-permute-start | bytes 516104 | tf_op jit(solution)/shard_map/ppermute | solution.py:468

commit v7 on v6

--- a/solution.py
+++ b/solution.py
@@ -286,7 +286,7 @@
             pm[i, 15 + k] = down[k]
         return 0
 
-    lax.fori_loop(0, 14, cell, 0, unroll=2)
+    lax.fori_loop(0, 14, cell, 0, unroll=7)
 
     def jump(i, _):
         for k in range(30):
@@ -332,7 +332,7 @@
              [coef_ref[k, at, :] for k in range(12)])
         return 0
 
-    lax.fori_loop(0, 8, own, 0, unroll=2)
+    lax.fori_loop(0, 8, own, 0, unroll=8)
     for high in range(2):
         def halo(i, _, high=high):
             at = pl.ds(pl.multiple_of(i * 8, 8), 8)
@@ -382,7 +382,7 @@
 
     line_flux((1, 0, 2), True, speed_ref[1], u_ref, coef_ref, const, (low, high), pm, mean, jumps,
               flux, done)
-    copies = fetch([(out_ref.at[k], out_h.at[k]) for k in range(NVAR)], out_sem)
+    copies = fetch([(out_ref.at[pl.ds(k, 7)], out_h.at[pl.ds(k, 7)]) for k in (0, 7)], out_sem)
     for copy in copies:
         copy.wait()
 
@@ -453,7 +453,7 @@
         y_kernel, name="y_rates", in_specs=[VMEM] * 7, out_specs=HBM,
         out_shape=struct(NVAR, 64, LANES),
         scratch_shapes=[vmem(14, 30, *PLANES), vmem(14, 24, *PLANES), vmem(13, 30, *PLANES),
-                        vmem(9, NVAR, *PLANES), vmem(NVAR, 64, LANES), dma(NVAR)],
+                        vmem(9, NVAR, *PLANES), vmem(NVAR, 64, LANES), dma(2)],
         compiler_params=params())(speed, u, coef, total, const, low, high)
 
 

time: 41.6 us -> 41.3 us (level)
  no operation moved by 1% of the time
where the time goes in v7:
time: 41.3 us; the launch traced here: 41.2 us
  starting transfers between devices  24.2 us (59%)
  Pallas kernels  15.1 us (37%)
  waiting for transfers between devices  1.09 us (3%)
  local copies, waits for them, and re-layouts  0.67 us (2%)
    all_to_all x1, starting transfers between devices, shards(): wide = lax.all_to_all(wide, AXES, 0, 0, tiled=True)  15.7 us
    ppermute x2, starting transfers between devices, neighbours(): low = lax.ppermute(end, axis, up)  4.51 us
    ppermute x2, starting transfers between devices, neighbours(): high = lax.ppermute(start, axis, [(b, a) for a, b in up])  4.01 us
    pallas_call x1, Pallas kernels, y_rates(): pl.pallas_call(y_kernel, name='y_rates', in_specs=[VMEM] * 7, out_specs=H...  3.92 us
    pallas_call x1, Pallas kernels, columns(): pl.pallas_call(column_kernel, name='columns', in_specs=[VMEM] * 3, out_sp...  3.11 us
    pallas_call x1, Pallas kernels, x_rates(): pl.pallas_call(x_kernel, name='x_rates', in_specs=[VMEM] * 7, out_specs=V...  2.96 us
    pallas_call x1, Pallas kernels, own_cells(): pl.pallas_call(own_kernel, name='own_cells', in_specs=[HBM] * 4 + [VMEM],...  2.84 us
    pallas_call x1, Pallas kernels, cells(): pl.pallas_call(cell_kernel, name='cells', in_specs=[HBM] * 4, out_specs=[...  2.3 us
  transfers between devices with their start and end apart: 5, of which 1 were waited for; matrix products, arithmetic and copies ran while one was open for 0% of the time, Pallas kernels for 22%

profile of v7, /device:TPU:1, one launch (start us, length us, event | category | flops | bytes accessed | tf_op | source)
XLA Modules:
  0.0 41.2 jit_solution(13782560137036814425)
XLA Ops:
  0.0 0.0 copy-start
  0.0 2.3 %cells.1 = (f32[256,128]{1,0:T(8,128)}, f32[14,24,128]{2,1,0:T(8,128)}, f32[14,24,128]{2,1,0:T(8,128)}, f32[14,24,128]{2,1,0:T(8,128)S(1)}, f32[14,24,128]{2,1,0:T(8,128)}) custom-call(f32[6,32]{1,0:T(8,128)} %bitcast.13, f32[32]{0:T(128)} %gas_h.3, s32[9]{0:T(128)} %index_h.3, f32[14,64,128]{2,1,0:T(8,128)} %bitcast.8), custom_call_target="tpu_custom_call" | custom-call | tf_op jit(solution)/shard_map/cells/pallas_call | solution.py:415
  2.3 15.7 %all-to-all-start = ((f32[256,1,128]{2,1,0:T(1,128)}), f32[256,1,128]{2,1,0:T(1,128)S(1)}, u32[]{:S(2)}, u32[]{:S(2)}) async-start(f32[256,1,128]{2,1,0:T(1,128)} %bitcast.3), calls=%async_computation | async-start | bytes 262144 | tf_op jit(solution)/shard_map/all_to_all | solution.py:476
  18.0 0.0 copy-start.1
  18.0 1.4 %collective-permute-start = (f32[14,24,128]{2,1,0:T(8,128)}, f32[14,24,128]{2,1,0:T(8,128)S(1)}, u32[]{:S(2)}, u32[]{:S(2)}) collective-permute-start(f32[14,24,128]{2,1,0:T(8,128)} %get-tuple-element.23), channel_id=1, source_target_pairs={{0,16},{16,32},{32,48},{48,64},{64,80},{80,96},{96,112},{112,128},... | collective-permute-start | bytes 516104 | tf_op jit(solution)/shard_map/ppermute | solution.py:467
  19.4 4.0 %collective-permute-start.1 = (f32[14,24,128]{2,1,0:T(8,128)}, f32[14,24,128]{2,1,0:T(8,128)S(1)}, u32[]{:S(2)}, u32[]{:S(2)}) collective-permute-start(f32[14,24,128]{2,1,0:T(8,128)} %get-tuple-element.24), channel_id=1, source_target_pairs={{16,0},{32,16},{48,32},{64,48},{80,64},{96,80},{112,96},{128,112},... | collective-permute-start | bytes 516104 | tf_op jit(solution)/shard_map/ppermute | solution.py:468
  23.4 3.1 %collective-permute-start.2 = (f32[14,24,128]{2,1,0:T(8,128)}, f32[14,24,128]{2,1,0:T(8,128)S(1)}, u32[]{:S(2)}, u32[]{:S(2)}) collective-permute-start(f32[14,24,128]{2,1,0:T(8,128)} %get-tuple-element.25), channel_id=1, source_target_pairs={{0,1},{1,2},{2,3},{3,4},{4,5},{5,6},{6,7},{7,8},{8,9},{9,10},{10,1... | collective-permute-start | bytes 516104 | tf_op jit(solution)/shard_map/ppermute | solution.py:467
  26.5 0.0 copy-start.2
  26.5 0.0 copy-start.3
  26.5 0.0 copy-start.4
  26.5 0.0 collective-permute-start.3
  26.5 0.0 copy-done
  26.5 0.0 copy-done.1
  26.5 0.6 %copy-done.2 = f32[32]{0:T(128)S(1)} copy-done((f32[32]{0:T(128)S(1)}, f32[32]{0:T(128)}, u32[]{:S(2)}) %copy-start.2) | copy-done | bytes 152
  27.2 0.0 copy-done.3
  27.2 0.0 copy-done.4
  27.2 2.8 %own_cells.1 = (f32[12,64,128]{2,1,0:T(8,128)S(1)}, f32[14,14,8,128]{3,2,1,0:T(8,128)S(1)}, f32[12,14,8,128]{3,2,1,0:T(8,128)S(1)}, f32[108,1,128]{2,1,0:T(1,128)S(1)}) custom-call(f32[6,32]{1,0:T(8,128)S(1)} %bitcast.14, f32[32]{0:T(128)S(1)} %copy-done.2, s32[9]{0:T(128)S(1)} %copy-done.3, s32[1,2]{1,0:T(1,128)S(1)} %bitcast.15, f32[14,64,128]{2,1,0:T(8,128)S(1)} %bitcast.9), custom_call_target="tpu_custom_call" | custom-call | tf_op jit(solution)/shard_map/own_cells/pallas_call | solution.py:424
  30.0 1.1 %all-to-all-done = f32[256,1,128]{2,1,0:T(1,128)S(1)} async-done(((f32[256,1,128]{2,1,0:T(1,128)}), f32[256,1,128]{2,1,0:T(1,128)S(1)}, u32[]{:S(2)}, u32[]{:S(2)}) %all-to-all-start) | async-done | bytes 131104 | tf_op jit(solution)/shard_map/all_to_all | solution.py:476
  31.1 3.1 %columns.1 = (f32[14,64,128]{2,1,0:T(8,128)S(1)}, f32[4,8,128]{2,1,0:T(8,128)S(1)}) custom-call(f32[256,128]{1,0:T(8,128)S(1)} %bitcast.12, f32[14,14,8,128]{3,2,1,0:T(8,128)S(1)} %get-tuple-element.17.tall_ref, f32[12,14,8,128]{3,2,1,0:T(8,128)S(1)} %get-tuple-element.18.tall_coef), custom_call_target="tpu_custom_call" | custom-call | tf_op jit(solution)/shard_map/columns/pallas_call | solution.py:434
  34.2 0.0 collective-permute-done.low
  34.2 0.0 collective-permute-done.1.high
  34.2 3.0 %x_rates.1.sum_ref = f32[14,64,128]{2,1,0:T(8,128)S(1)} custom-call(f32[4,8,128]{2,1,0:T(8,128)S(1)} %get-tuple-element.19.speed_ref, f32[14,64,128]{2,1,0:T(8,128)S(1)} %bitcast.10, f32[12,64,128]{2,1,0:T(8,128)S(1)} %get-tuple-element.20.coef_ref, f32[14,64,128]{2,1,0:T(8,128)S(1)} %get-tuple-element.21.z_ref, f32[108,1,128]{2,1,0:T(1,128)S(1)} %get-tuple-element.22.const, ...), custom_call_target="tpu_custom_call" | custom-call | tf_op jit(solution)/shard_map/x_rates/pallas_call | solution.py:443
  37.2 0.0 collective-permute-done.2.low
  37.2 0.0 collective-permute-done.3.high
  37.2 3.9 %y_rates.1 = f32[14,64,128]{2,1,0:T(8,128)} custom-call(f32[4,8,128]{2,1,0:T(8,128)S(1)} %get-tuple-element.19.speed_ref, f32[14,64,128]{2,1,0:T(8,128)S(1)} %bitcast.11, f32[12,64,128]{2,1,0:T(8,128)S(1)} %get-tuple-element.20.coef_ref, f32[14,64,128]{2,1,0:T(8,128)S(1)} %x_rates.1.sum_ref, f32[108,1,128]{2,1,0:T(1,128)S(1)} %get-tuple-element.22.const, ...), custom_call_target="tpu_custom_call" | custom-call | tf_op jit(solution)/shard_map/y_rates/pallas_call | solution.py:452
Async XLA Ops:
  0.0 26.5 %copy-start = (f32[14,8,8,128]{3,2,1,0:T(8,128)S(1)}, f32[14,8,8,128]{3,2,1,0:T(8,128)}, u32[]{:S(2)}) copy-start(f32[14,8,8,128]{3,2,1,0:T(8,128)} %param.5) | copy-start | bytes 1376260
  2.3 28.8 %all-to-all-start = ((f32[256,1,128]{2,1,0:T(1,128)}), f32[256,1,128]{2,1,0:T(1,128)S(1)}, u32[]{:S(2)}, u32[]{:S(2)}) async-start(f32[256,1,128]{2,1,0:T(1,128)} %bitcast.3), calls=%async_computation | async-start | bytes 262144 | tf_op jit(solution)/shard_map/all_to_all | solution.py:476
  18.0 8.6 %copy-start.1 = (f32[32,6]{0,1:T(8,128)S(1)}, f32[32,6]{0,1:T(8,128)}, u32[]{:S(2)}) copy-start(f32[32,6]{0,1:T(8,128)} %param.6) | copy-start | bytes 2308
  18.0 16.2 %collective-permute-start = (f32[14,24,128]{2,1,0:T(8,128)}, f32[14,24,128]{2,1,0:T(8,128)S(1)}, u32[]{:S(2)}, u32[]{:S(2)}) collective-permute-start(f32[14,24,128]{2,1,0:T(8,128)} %get-tuple-element.23), channel_id=1, source_target_pairs={{0,16},{16,32},{32,48},{48,64},{64,80},{80,96},{96,112},{112,128},... | collective-permute-start | bytes 516104 | tf_op jit(solution)/shard_map/ppermute | solution.py:467
  19.4 14.8 %collective-permute-start.1 = (f32[14,24,128]{2,1,0:T(8,128)}, f32[14,24,128]{2,1,0:T(8,128)S(1)}, u32[]{:S(2)}, u32[]{:S(2)}) collective-permute-start(f32[14,24,128]{2,1,0:T(8,128)} %get-tuple-element.24), channel_id=1, source_target_pairs={{16,0},{32,16},{48,32},{64,48},{80,64},{96,80},{112,96},{128,112},... | collective-permute-start | bytes 516104 | tf_op jit(solution)/shard_map/ppermute | solution.py:468
  23.4 13.8 %collective-permute-start.2 = (f32[14,24,128]{2,1,0:T(8,128)}, f32[14,24,128]{2,1,0:T(8,128)S(1)}, u32[]{:S(2)}, u32[]{:S(2)}) collective-permute-start(f32[14,24,128]{2,1,0:T(8,128)} %get-tuple-element.25), channel_id=1, source_target_pairs={{0,1},{1,2},{2,3},{3,4},{4,5},{5,6},{6,7},{7,8},{8,9},{9,10},{10,1... | collective-permute-start | bytes 516104 | tf_op jit(solution)/shard_map/ppermute | solution.py:467
  26.5 0.7 %copy-start.2 = (f32[32]{0:T(128)S(1)}, f32[32]{0:T(128)}, u32[]{:S(2)}) copy-start(f32[32]{0:T(128)} %gas_h.3) | copy-start | bytes 388
  26.5 0.7 %copy-start.3 = (s32[9]{0:T(128)S(1)}, s32[9]{0:T(128)}, u32[]{:S(2)}) copy-start(s32[9]{0:T(128)} %index_h.3) | copy-start | bytes 112
  26.5 0.7 %copy-start.4 = (s32[1,1,2]{2,1,0:T(1,128)S(1)}, s32[1,1,2]{2,1,0:T(1,128)}, u32[]{:S(2)}) copy-start(s32[1,1,2]{2,1,0:T(1,128)} %param.9) | copy-start | bytes 28
  26.5 10.7 %collective-permute-start.3 = (f32[14,24,128]{2,1,0:T(8,128)S(1)}, f32[14,24,128]{2,1,0:T(8,128)S(1)}, u32[]{:S(2)}, u32[]{:S(2)}) collective-permute-start(f32[14,24,128]{2,1,0:T(8,128)S(1)} %get-tuple-element.26), channel_id=1, source_target_pairs={{1,0},{2,1},{3,2},{4,3},{5,4},{6,5},{7,6},{8,7},{9,8},{10,9},{11,1... | collective-permute-start | bytes 516104 | tf_op jit(solution)/shard_map/ppermute | solution.py:468
